TPU v7x, 128 devices: a whole 4x4x4 slice. The times are simulated.
128 devices in a mesh: site: 128 (over y, z, x, core).
Axes of the slice: x: 4, y: 4, z: 4, core: 2. Of those that a mesh axis runs over, the one named last changes fastest.
Arguments:
- sites: float32 [128, 2, 12, 128, 128], P('site'), may hold values from -0.5 to 0.5
- sector_sizes: int32 [128, 12], P('site'), may hold values from 64 to 128, as said below
- charge_steps: int32 [128], P('site'), may hold values from 0 to 1
- kept_counts: int32 [128, 12], P('site'), may hold values from 64 to 128, as said below
- gates: float32 [128, 6], P('site'), may hold values from 0.4 to 1.2
- sketches: float32 [128, 12, 256, 128], P('site'), may hold values from -0.375 to 0.375
Outputs:
- new_sites: float32 [128, 2, 12, 128, 128], P('site')
- totals: float32 [2], replicated
Inputs may be any that keep to these rules, and one draw needn't show every extreme that they name: `sector_sizes`: every sector holds at least 64 states; each bond has one sector of exactly 128 states. kept_counts[i, c] is at least 64 and at most sector_sizes[(i + 1) mod 128, c]; on each bond the sector of 128 states keeps all of them.
All inputs are finite; a program needn't handle non-finite values.
Results may differ from a plain program's by a relative error of at most 0.0003.
Values sent between devices are 32-bit elements; how exact they have to be, the bound alone decides.
No kernel may reach another device: no remote copies, remote signals or barrier semaphores. Data moves between devices by JAX's collectives and lax.ppermute only.
A program may use at most 64 MiB of HBM per device.

v0:
```python
import jax
import jax.numpy as jnp
from jax import lax
from jax.sharding import PartitionSpec as P

STEPS = 4


def from_behind(value, axis, steps):
    count = lax.axis_size(axis)
    pairs = [(source, (source + steps) % count) for source in range(count)]
    return lax.ppermute(value, axis, pairs)


def shifted(value, axis, by):
    count = lax.axis_size(axis)
    pairs = [(i, i + by) for i in range(count) if 0 <= i + by < count]
    return lax.ppermute(value, axis, pairs)


def together(arrays, axis):
    vector, at, done = (jnp.concatenate([a.reshape(-1) for a in arrays]), 0, [])
    so_far = lax.psum(vector, axis)
    for a in arrays:
        done.append(so_far[at : at + a.size].reshape(a.shape))
        at += a.size
    return tuple(done)


def sector_index(count, shift, extra):
    return (jnp.arange(count, dtype=jnp.int32) + extra - shift) % count


def theta_blocks(left, right, shift, gate):
    count = left.shape[1]
    lower_mid = sector_index(count, shift, 0)
    upper_mid = sector_index(count, shift, 1)

    def product(first, second):
        return jnp.einsum("lam,lmb->lab", first, second, precision=lax.Precision.HIGHEST)

    zero_zero = product(left[0], right[0][lower_mid])
    zero_one = product(left[0], right[1][lower_mid])
    one_zero = product(left[1], right[0][upper_mid])
    one_one = product(left[1], right[1][upper_mid])
    mixed_up = gate[2] * zero_one + gate[3] * one_zero
    mixed_down = gate[4] * zero_one + gate[5] * one_zero
    return (gate[0] * zero_zero, mixed_up, mixed_down, gate[1] * one_one)


def split_sectors(blocks, middle, shift, sketch, kept):
    count = blocks[0].shape[0]
    width = blocks[0].shape[-1]
    top = (middle + shift) % count
    bottom = (middle + shift - 1) % count
    upper = jnp.concatenate([blocks[0][top], blocks[1][top]], axis=2)
    lower = jnp.concatenate([blocks[2][bottom], blocks[3][bottom]], axis=2)
    matrix = jnp.concatenate([upper, lower], axis=1)
    used = (jnp.arange(width, dtype=jnp.int32)[None, :] < kept[:, None]).astype(jnp.float32)
    sample = jnp.einsum(
        "kij,kjs->kis", matrix, sketch * used[:, None, :], precision=lax.Precision.HIGHEST
    )
    gram = jnp.einsum("kis,kit->kst", sample, sample, precision=lax.Precision.HIGHEST)
    diag_sum = jnp.sum(sample * sample, axis=(1, 2))
    ridge = 0.001 * diag_sum / kept.astype(jnp.float32) + 1e-06
    identity = jnp.eye(width, dtype=jnp.float32)[None]
    gram = gram + identity * ridge[:, None, None] + identity * (1.0 - used)[:, None, :]
    factor = jnp.linalg.cholesky(gram)
    solved = jax.scipy.linalg.solve_triangular(factor, jnp.swapaxes(sample, 1, 2), lower=True)
    basis = jnp.swapaxes(solved, 1, 2)
    reduced = jnp.einsum("kis,kij->ksj", basis, matrix, precision=lax.Precision.HIGHEST)
    return (basis, reduced, jnp.sum(matrix * matrix), jnp.sum(reduced * reduced))


def rebuild_left(basis, shift):
    count = basis.shape[0]
    width = basis.shape[2]
    return jnp.stack(
        [basis[sector_index(count, shift, 0), :width], basis[sector_index(count, shift, 1), width:]]
    )


def rebuild_right(reduced, weight):
    width = reduced.shape[1]
    return jnp.stack([reduced[..., :width], reduced[..., width:]]) / jnp.sqrt(weight)


def mask_tensor(tensor, sizes, next_sizes, step):
    count = tensor.shape[1]
    width = tensor.shape[-1]
    states = jnp.arange(width, dtype=jnp.int32)
    rows = states[None, :] < sizes[:, None]
    masks = []
    for phys in range(2):
        target = sector_index(count, step, phys)
        cols = states[None, :] < next_sizes[target][:, None]
        masks.append(rows[:, :, None] & cols[:, None, :])
    return tensor * jnp.stack(masks).astype(jnp.float32)


def body(sites, sector_sizes, charge_steps, kept_counts, gates, sketches):
    tensor = sites[0]
    step = charge_steps[0]
    kept = kept_counts[0]
    gate = gates[0]
    sketch = sketches[0]
    position = lax.axis_index("site")
    chain = lax.axis_size("site")
    next_sizes = from_behind(sector_sizes, "site", -1)[0]
    tensor = mask_tensor(tensor, sector_sizes[0], next_sizes, step)
    count = tensor.shape[1]
    prev_gates, prev_sketches = shifted((gates, sketches), "site", 1)
    prev_steps, prev_kept = shifted((charge_steps, kept_counts), "site", 1)

    def one_sweep(tensor, lost_sum, log_sum, parity):
        is_left = (position % 2 == parity) & (position + 1 < chain)
        is_right = ((position - 1) % 2 == parity) & (position >= 1)
        from_right = shifted(tensor, "site", -1)
        from_left = shifted(tensor, "site", 1)
        left_in = jnp.where(is_left, tensor, from_left)
        right_in = jnp.where(is_left, from_right, tensor)
        shift_in = jnp.where(is_left, step, prev_steps[0])
        gate_in = jnp.where(is_left, gate, prev_gates[0])
        sketch_in = jnp.where(is_left, sketch, prev_sketches[0])
        kept_in = jnp.where(is_left, kept, prev_kept[0])
        blocks = theta_blocks(left_in, right_in, shift_in, gate_in)
        half = count // 2
        middle = jnp.arange(half, dtype=jnp.int32) + jnp.where(is_left, 0, half)
        basis_half, reduced_half, total_half, weight_half = split_sectors(
            blocks, middle, shift_in, sketch_in[middle], kept_in[middle]
        )
        partial_value = jnp.stack([total_half, weight_half])
        basis_other, sums_right = shifted((basis_half, partial_value), "site", -1)
        reduced_other, sums_left = shifted((reduced_half, partial_value), "site", 1)
        basis = jnp.concatenate([basis_half, basis_other], axis=0)
        reduced = jnp.concatenate([reduced_other, reduced_half], axis=0)
        total = total_half + sums_right[0]
        weight_left = weight_half + sums_right[1]
        weight_right = weight_half + sums_left[1]
        new_left = rebuild_left(basis, shift_in)
        new_right = rebuild_right(reduced, weight_right)
        lost = 1.0 - weight_left / total
        log_norm = jnp.log(total)
        tensor = jnp.where(is_left, new_left, jnp.where(is_right, new_right, tensor))
        lost_now = jnp.where(is_left, lost, 0.0)
        log_now = jnp.where(is_left, log_norm, 0.0)
        lost_sum = lost_sum + lost_now
        log_sum = log_sum + log_now
        return (tensor, lost_sum, log_sum)

    def one_step(index, carry):
        tensor, lost_sum, log_sum = carry
        tensor, lost_sum, log_sum = one_sweep(tensor, lost_sum, log_sum, 0)
        tensor, lost_sum, log_sum = one_sweep(tensor, lost_sum, log_sum, 1)
        return (tensor, lost_sum, log_sum)

    start = (tensor, jnp.zeros((), jnp.float32), jnp.zeros((), jnp.float32))
    tensor, lost_sum, log_sum = lax.fori_loop(0, STEPS, one_step, start)
    lost_sum, log_sum = together((lost_sum, log_sum), "site")
    return (tensor[None], jnp.stack([lost_sum, log_sum]))


def solution(mesh):
    placed = (
        P("site", None, None, None, None),
        P("site", None),
        P("site"),
        P("site", None),
        P("site", None),
        P("site", None, None, None),
    )
    return jax.shard_map(
        body,
        mesh=mesh,
        in_specs=placed,
        out_specs=(P("site", None, None, None, None), P()),
        check_vma=False,
    )
```

profile of v0, /device:TPU:0, one launch (start us, length us, event | category | flops | bytes accessed | tf_op | source)
XLA Modules:
  0.0 2061.3 jit_solution(13319599465956033576)
XLA Ops:
  8.8 4.2 collective-permute-start.12
  30.4 1874.7 %while.19 = (s32[]{:T(128)}, f32[2,12,128,128]{3,2,1,0:T(8,128)S(1)}, f32[]{:T(128)}, f32[]{:T(128)}, pred[]{:T(512)}, /*index=5*/f32[1,6]{1,0:T(1,128)S(1)}, f3...) while((s32[]{:T(128)}, ...), condition=%wide.region_9.12_spmd, body=%wide.region_0.11_spmd.sunk | while | flops 6066817024 | bytes 249431600 | solution.py:158
  30.4 8.3 collective-permute-start
  56.0 4.7 multiply_add_fusion.6
  77.1 70.7 %custom-call.108 = f32[6,128,128]{2,1,0:T(8,128)S(1)} custom-call(f32[6,128,128]{2,1,0:T(8,128)S(1)} %fusion.138), custom_call_target="Cholesky" | custom-call | tf_op jit(solution)/shard_map/while/body/eval_jaxpr/jit(cholesky)/cholesky | solution.py:68
  148.9 59.0 %custom-call.109 = f32[6,1,128,128]{2,3,1,0:T(8,128)S(1)} custom-call(f32[6,1,128,128]{3,2,1,0:T(8,128)S(1)} %select_bitcast_fusion.6), custom_call_target="InvertDiagBlocksLowerTriangular" | custom-call | tf_op jit(solution)/shard_map/while/body/eval_jaxpr/jit(_solve_triangular)/vmap()/triangular_solve | solution.py:69
  212.6 20.3 collective-permute-start.3
  256.0 6.3 collective-permute-start.5
  284.1 5.9 multiply_add_fusion.7
  302.1 70.5 %custom-call.110 = f32[6,128,128]{2,1,0:T(8,128)S(1)} custom-call(f32[6,128,128]{2,1,0:T(8,128)S(1)} %fusion.146), custom_call_target="Cholesky" | custom-call | tf_op jit(solution)/shard_map/while/body/eval_jaxpr/jit(cholesky)/cholesky | solution.py:68
  373.7 59.0 %custom-call.111 = f32[6,1,128,128]{2,3,1,0:T(8,128)S(1)} custom-call(f32[6,1,128,128]{3,2,1,0:T(8,128)S(1)} %select_bitcast_fusion.7), custom_call_target="InvertDiagBlocksLowerTriangular" | custom-call | tf_op jit(solution)/shard_map/while/body/eval_jaxpr/jit(_solve_triangular)/vmap()/triangular_solve | solution.py:69
  437.5 20.4 collective-permute-start.8
  468.1 5.2 collective-permute-start.9
  493.0 3.7 collective-permute-start
  513.4 4.7 multiply_add_fusion.6
  534.4 70.8 %custom-call.108 = f32[6,128,128]{2,1,0:T(8,128)S(1)} custom-call(f32[6,128,128]{2,1,0:T(8,128)S(1)} %fusion.138), custom_call_target="Cholesky" | custom-call | tf_op jit(solution)/shard_map/while/body/eval_jaxpr/jit(cholesky)/cholesky | solution.py:68
  606.3 59.0 %custom-call.109 = f32[6,1,128,128]{2,3,1,0:T(8,128)S(1)} custom-call(f32[6,1,128,128]{3,2,1,0:T(8,128)S(1)} %select_bitcast_fusion.6), custom_call_target="InvertDiagBlocksLowerTriangular" | custom-call | tf_op jit(solution)/shard_map/while/body/eval_jaxpr/jit(_solve_triangular)/vmap()/triangular_solve | solution.py:69
  670.0 20.3 collective-permute-start.3
  713.2 9.7 collective-permute-start.5
  744.6 5.9 multiply_add_fusion.7
  762.6 70.6 %custom-call.110 = f32[6,128,128]{2,1,0:T(8,128)S(1)} custom-call(f32[6,128,128]{2,1,0:T(8,128)S(1)} %fusion.146), custom_call_target="Cholesky" | custom-call | tf_op jit(solution)/shard_map/while/body/eval_jaxpr/jit(cholesky)/cholesky | solution.py:68
  834.3 59.0 %custom-call.111 = f32[6,1,128,128]{2,3,1,0:T(8,128)S(1)} custom-call(f32[6,1,128,128]{3,2,1,0:T(8,128)S(1)} %select_bitcast_fusion.7), custom_call_target="InvertDiagBlocksLowerTriangular" | custom-call | tf_op jit(solution)/shard_map/while/body/eval_jaxpr/jit(_solve_triangular)/vmap()/triangular_solve | solution.py:69
  898.0 24.7 %collective-permute-start.8 = (f32[6,128,256]{2,1,0:T(8,128)}, f32[6,128,256]{2,1,0:T(8,128)}, u32[]{:S(2)}, u32[]{:S(2)}) collective-permute-start(f32[6,128,256]{2,1,0:T(8,128)} %get-tuple-element.925), channel_id=1, source_target_pairs={{0,1},{1,2},{2,3},{3,4},{4,5},{5,6},{6,7},{7,8},{8,9},{9,10},{10,1... | collective-permute-start | bytes 2359304 | tf_op jit(solution)/shard_map/while/body/eval_jaxpr/ppermute | solution.py:18
  932.9 7.5 collective-permute-start.9
  960.3 3.7 collective-permute-start
  969.9 4.8 collective-permute-done.1
  984.8 4.7 multiply_add_fusion.6
  1005.9 70.6 %custom-call.108 = f32[6,128,128]{2,1,0:T(8,128)S(1)} custom-call(f32[6,128,128]{2,1,0:T(8,128)S(1)} %fusion.138), custom_call_target="Cholesky" | custom-call | tf_op jit(solution)/shard_map/while/body/eval_jaxpr/jit(cholesky)/cholesky | solution.py:68
  1077.5 59.0 %custom-call.109 = f32[6,1,128,128]{2,3,1,0:T(8,128)S(1)} custom-call(f32[6,1,128,128]{3,2,1,0:T(8,128)S(1)} %select_bitcast_fusion.6), custom_call_target="InvertDiagBlocksLowerTriangular" | custom-call | tf_op jit(solution)/shard_map/while/body/eval_jaxpr/jit(_solve_triangular)/vmap()/triangular_solve | solution.py:69
  1141.2 20.3 collective-permute-start.3
  1184.5 10.1 collective-permute-start.5
  1216.2 5.9 multiply_add_fusion.7
  1234.3 70.5 %custom-call.110 = f32[6,128,128]{2,1,0:T(8,128)S(1)} custom-call(f32[6,128,128]{2,1,0:T(8,128)S(1)} %fusion.146), custom_call_target="Cholesky" | custom-call | tf_op jit(solution)/shard_map/while/body/eval_jaxpr/jit(cholesky)/cholesky | solution.py:68
  1305.9 59.0 %custom-call.111 = f32[6,1,128,128]{2,3,1,0:T(8,128)S(1)} custom-call(f32[6,1,128,128]{3,2,1,0:T(8,128)S(1)} %select_bitcast_fusion.7), custom_call_target="InvertDiagBlocksLowerTriangular" | custom-call | tf_op jit(solution)/shard_map/while/body/eval_jaxpr/jit(_solve_triangular)/vmap()/triangular_solve | solution.py:69
  1369.6 24.7 %collective-permute-start.8 = (f32[6,128,256]{2,1,0:T(8,128)}, f32[6,128,256]{2,1,0:T(8,128)}, u32[]{:S(2)}, u32[]{:S(2)}) collective-permute-start(f32[6,128,256]{2,1,0:T(8,128)} %get-tuple-element.925), channel_id=1, source_target_pairs={{0,1},{1,2},{2,3},{3,4},{4,5},{5,6},{6,7},{7,8},{8,9},{9,10},{10,1... | collective-permute-start | bytes 2359304 | tf_op jit(solution)/shard_map/while/body/eval_jaxpr/ppermute | solution.py:18
  1404.5 7.5 collective-permute-start.9
  1441.3 4.8 collective-permute-done.1
  1456.2 4.7 multiply_add_fusion.6
  1477.2 70.8 %custom-call.108 = f32[6,128,128]{2,1,0:T(8,128)S(1)} custom-call(f32[6,128,128]{2,1,0:T(8,128)S(1)} %fusion.138), custom_call_target="Cholesky" | custom-call | tf_op jit(solution)/shard_map/while/body/eval_jaxpr/jit(cholesky)/cholesky | solution.py:68
  1549.2 59.0 %custom-call.109 = f32[6,1,128,128]{2,3,1,0:T(8,128)S(1)} custom-call(f32[6,1,128,128]{3,2,1,0:T(8,128)S(1)} %select_bitcast_fusion.6), custom_call_target="InvertDiagBlocksLowerTriangular" | custom-call | tf_op jit(solution)/shard_map/while/body/eval_jaxpr/jit(_solve_triangular)/vmap()/triangular_solve | solution.py:69
  1612.8 20.3 collective-permute-start.3
  1656.0 10.1 collective-permute-start.5
  1687.8 5.9 multiply_add_fusion.7
  1705.8 70.6 %custom-call.110 = f32[6,128,128]{2,1,0:T(8,128)S(1)} custom-call(f32[6,128,128]{2,1,0:T(8,128)S(1)} %fusion.146), custom_call_target="Cholesky" | custom-call | tf_op jit(solution)/shard_map/while/body/eval_jaxpr/jit(cholesky)/cholesky | solution.py:68
  1777.5 59.0 %custom-call.111 = f32[6,1,128,128]{2,3,1,0:T(8,128)S(1)} custom-call(f32[6,1,128,128]{3,2,1,0:T(8,128)S(1)} %select_bitcast_fusion.7), custom_call_target="InvertDiagBlocksLowerTriangular" | custom-call | tf_op jit(solution)/shard_map/while/body/eval_jaxpr/jit(_solve_triangular)/vmap()/triangular_solve | solution.py:69
  1841.2 24.7 %collective-permute-start.8 = (f32[6,128,256]{2,1,0:T(8,128)}, f32[6,128,256]{2,1,0:T(8,128)}, u32[]{:S(2)}, u32[]{:S(2)}) collective-permute-start(f32[6,128,256]{2,1,0:T(8,128)} %get-tuple-element.925), channel_id=1, source_target_pairs={{0,1},{1,2},{2,3},{3,4},{4,5},{5,6},{6,7},{7,8},{8,9},{9,10},{10,1... | collective-permute-start | bytes 2359304 | tf_op jit(solution)/shard_map/while/body/eval_jaxpr/ppermute | solution.py:18
  1876.2 7.5 collective-permute-start.9
  1905.2 155.9 %psum.7 = f32[2]{0:T(128)} all-reduce(f32[2]{0:T(128)S(1)} %pad_maximum_fusion.6), channel_id=1, replica_groups=mesh['site'=128] {'site'}, use_global_device_ids=true, to_apply=%region_10.13 | all-reduce | flops 2 | bytes 16 | tf_op jit(solution)/shard_map/psum | solution.py:23
  (775 shorter events, 517.1 us)
Async XLA Ops:
  0.6 21.4 %collective-permute-start.16 = (f32[1,12,256,128]{3,2,1,0:T(8,128)}, f32[1,12,256,128]{3,2,1,0:T(8,128)}, u32[]{:S(2)}, u32[]{:S(2)}) collective-permute-start(f32[1,12,256,128]{3,2,1,0:T(8,128)} %param.16), channel_id=1, source_target_pairs={{0,1},{1,2},{2,3},{3,4},{4,5},{5,6},{6,7},{7,8},{8,9},{9,10},{10,1... | collective-permute-start | bytes 4718600 | tf_op jit(solution)/shard_map/ppermute | solution.py:18
  3.2 13.7 collective-permute-start.15
  6.3 9.5 collective-permute-start.14
  8.8 11.2 collective-permute-start.12
  14.5 15.9 collective-permute-start.13
  30.4 14.1 collective-permute-start
  38.7 7.3 collective-permute-start.1
  208.7 31.8 %collective-permute-start.2 = (f32[6,256,128]{1,2,0:T(8,128)S(1)}, f32[6,256,128]{1,2,0:T(8,128)S(1)}, u32[]{:S(2)}, u32[]{:S(2)}) collective-permute-start(f32[6,256,128]{1,2,0:T(8,128)S(1)} %bitcast.315), channel_id=1, source_target_pairs={{1,0},{2,1},{3,2},{4,3},{5,4},{6,5},{7,6},{8,7},{9,8},{10,9},{11,1... | collective-permute-start | bytes 2359304 | tf_op jit(solution)/shard_map/while/body/eval_jaxpr/ppermute | solution.py:18
  212.6 40.8 %collective-permute-start.3 = (f32[6,128,256]{2,1,0:T(8,128)}, f32[6,128,256]{2,1,0:T(8,128)}, u32[]{:S(2)}, u32[]{:S(2)}) collective-permute-start(f32[6,128,256]{2,1,0:T(8,128)} %get-tuple-element.901), channel_id=1, source_target_pairs={{0,1},{1,2},{2,3},{3,4},{4,5},{5,6},{6,7},{7,8},{8,9},{9,10},{10,1... | collective-permute-start | bytes 2359304 | tf_op jit(solution)/shard_map/while/body/eval_jaxpr/ppermute | solution.py:18
  235.1 3.6 collective-permute-start.4
  256.0 12.0 collective-permute-start.5
  262.3 7.2 collective-permute-start.6
  433.6 45.0 %collective-permute-start.7 = (f32[6,256,128]{1,2,0:T(8,128)S(1)}, f32[6,256,128]{1,2,0:T(8,128)S(1)}, u32[]{:S(2)}, u32[]{:S(2)}) collective-permute-start(f32[6,256,128]{1,2,0:T(8,128)S(1)} %bitcast.313), channel_id=1, source_target_pairs={{1,0},{2,1},{3,2},{4,3},{5,4},{6,5},{7,6},{8,7},{9,8},{10,9},{11,1... | collective-permute-start | bytes 2359304 | tf_op jit(solution)/shard_map/while/body/eval_jaxpr/ppermute | solution.py:18
  437.5 50.5 %collective-permute-start.8 = (f32[6,128,256]{2,1,0:T(8,128)}, f32[6,128,256]{2,1,0:T(8,128)}, u32[]{:S(2)}, u32[]{:S(2)}) collective-permute-start(f32[6,128,256]{2,1,0:T(8,128)} %get-tuple-element.925), channel_id=1, source_target_pairs={{0,1},{1,2},{2,3},{3,4},{4,5},{5,6},{6,7},{7,8},{8,9},{9,10},{10,1... | collective-permute-start | bytes 2359304 | tf_op jit(solution)/shard_map/while/body/eval_jaxpr/ppermute | solution.py:18
  466.8 6.5 collective-permute-start.11
  468.1 8.6 collective-permute-start.9
  493.0 9.6 collective-permute-start
  496.8 6.5 collective-permute-start.1
  666.2 31.8 %collective-permute-start.2 = (f32[6,256,128]{1,2,0:T(8,128)S(1)}, f32[6,256,128]{1,2,0:T(8,128)S(1)}, u32[]{:S(2)}, u32[]{:S(2)}) collective-permute-start(f32[6,256,128]{1,2,0:T(8,128)S(1)} %bitcast.315), channel_id=1, source_target_pairs={{1,0},{2,1},{3,2},{4,3},{5,4},{6,5},{7,6},{8,7},{9,8},{10,9},{11,1... | collective-permute-start | bytes 2359304 | tf_op jit(solution)/shard_map/while/body/eval_jaxpr/ppermute | solution.py:18
  670.0 40.6 %collective-permute-start.3 = (f32[6,128,256]{2,1,0:T(8,128)}, f32[6,128,256]{2,1,0:T(8,128)}, u32[]{:S(2)}, u32[]{:S(2)}) collective-permute-start(f32[6,128,256]{2,1,0:T(8,128)} %get-tuple-element.901), channel_id=1, source_target_pairs={{0,1},{1,2},{2,3},{3,4},{4,5},{5,6},{6,7},{7,8},{8,9},{9,10},{10,1... | collective-permute-start | bytes 2359304 | tf_op jit(solution)/shard_map/while/body/eval_jaxpr/ppermute | solution.py:18
  692.6 3.6 collective-permute-start.4
  713.2 15.0 collective-permute-start.5
  722.9 7.0 collective-permute-start.6
  894.1 51.6 %collective-permute-start.7 = (f32[6,256,128]{1,2,0:T(8,128)S(1)}, f32[6,256,128]{1,2,0:T(8,128)S(1)}, u32[]{:S(2)}, u32[]{:S(2)}) collective-permute-start(f32[6,256,128]{1,2,0:T(8,128)S(1)} %bitcast.313), channel_id=1, source_target_pairs={{1,0},{2,1},{3,2},{4,3},{5,4},{6,5},{7,6},{8,7},{9,8},{10,9},{11,1... | collective-permute-start | bytes 2359304 | tf_op jit(solution)/shard_map/while/body/eval_jaxpr/ppermute | solution.py:18
  898.0 57.4 %collective-permute-start.8 = (f32[6,128,256]{2,1,0:T(8,128)}, f32[6,128,256]{2,1,0:T(8,128)}, u32[]{:S(2)}, u32[]{:S(2)}) collective-permute-start(f32[6,128,256]{2,1,0:T(8,128)} %get-tuple-element.925), channel_id=1, source_target_pairs={{0,1},{1,2},{2,3},{3,4},{4,5},{5,6},{6,7},{7,8},{8,9},{9,10},{10,1... | collective-permute-start | bytes 2359304 | tf_op jit(solution)/shard_map/while/body/eval_jaxpr/ppermute | solution.py:18
  931.6 8.8 collective-permute-start.11
  932.9 10.9 collective-permute-start.9
  960.3 9.6 collective-permute-start
  964.1 10.7 collective-permute-start.1
  1137.3 31.8 %collective-permute-start.2 = (f32[6,256,128]{1,2,0:T(8,128)S(1)}, f32[6,256,128]{1,2,0:T(8,128)S(1)}, u32[]{:S(2)}, u32[]{:S(2)}) collective-permute-start(f32[6,256,128]{1,2,0:T(8,128)S(1)} %bitcast.315), channel_id=1, source_target_pairs={{1,0},{2,1},{3,2},{4,3},{5,4},{6,5},{7,6},{8,7},{9,8},{10,9},{11,1... | collective-permute-start | bytes 2359304 | tf_op jit(solution)/shard_map/while/body/eval_jaxpr/ppermute | solution.py:18
  1141.2 40.7 %collective-permute-start.3 = (f32[6,128,256]{2,1,0:T(8,128)}, f32[6,128,256]{2,1,0:T(8,128)}, u32[]{:S(2)}, u32[]{:S(2)}) collective-permute-start(f32[6,128,256]{2,1,0:T(8,128)} %get-tuple-element.901), channel_id=1, source_target_pairs={{0,1},{1,2},{2,3},{3,4},{4,5},{5,6},{6,7},{7,8},{8,9},{9,10},{10,1... | collective-permute-start | bytes 2359304 | tf_op jit(solution)/shard_map/while/body/eval_jaxpr/ppermute | solution.py:18
  1163.8 3.6 collective-permute-start.4
  1184.5 15.7 collective-permute-start.5
  1194.6 7.0 collective-permute-start.6
  1365.7 51.6 %collective-permute-start.7 = (f32[6,256,128]{1,2,0:T(8,128)S(1)}, f32[6,256,128]{1,2,0:T(8,128)S(1)}, u32[]{:S(2)}, u32[]{:S(2)}) collective-permute-start(f32[6,256,128]{1,2,0:T(8,128)S(1)} %bitcast.313), channel_id=1, source_target_pairs={{1,0},{2,1},{3,2},{4,3},{5,4},{6,5},{7,6},{8,7},{9,8},{10,9},{11,1... | collective-permute-start | bytes 2359304 | tf_op jit(solution)/shard_map/while/body/eval_jaxpr/ppermute | solution.py:18
  1369.6 57.1 %collective-permute-start.8 = (f32[6,128,256]{2,1,0:T(8,128)}, f32[6,128,256]{2,1,0:T(8,128)}, u32[]{:S(2)}, u32[]{:S(2)}) collective-permute-start(f32[6,128,256]{2,1,0:T(8,128)} %get-tuple-element.925), channel_id=1, source_target_pairs={{0,1},{1,2},{2,3},{3,4},{4,5},{5,6},{6,7},{7,8},{8,9},{9,10},{10,1... | collective-permute-start | bytes 2359304 | tf_op jit(solution)/shard_map/while/body/eval_jaxpr/ppermute | solution.py:18
  1403.2 8.8 collective-permute-start.11
  1404.5 10.9 collective-permute-start.9
  1431.7 9.6 collective-permute-start
  1435.5 10.7 collective-permute-start.1
  1609.0 31.8 %collective-permute-start.2 = (f32[6,256,128]{1,2,0:T(8,128)S(1)}, f32[6,256,128]{1,2,0:T(8,128)S(1)}, u32[]{:S(2)}, u32[]{:S(2)}) collective-permute-start(f32[6,256,128]{1,2,0:T(8,128)S(1)} %bitcast.315), channel_id=1, source_target_pairs={{1,0},{2,1},{3,2},{4,3},{5,4},{6,5},{7,6},{8,7},{9,8},{10,9},{11,1... | collective-permute-start | bytes 2359304 | tf_op jit(solution)/shard_map/while/body/eval_jaxpr/ppermute | solution.py:18
  1612.8 40.6 %collective-permute-start.3 = (f32[6,128,256]{2,1,0:T(8,128)}, f32[6,128,256]{2,1,0:T(8,128)}, u32[]{:S(2)}, u32[]{:S(2)}) collective-permute-start(f32[6,128,256]{2,1,0:T(8,128)} %get-tuple-element.901), channel_id=1, source_target_pairs={{0,1},{1,2},{2,3},{3,4},{4,5},{5,6},{6,7},{7,8},{8,9},{9,10},{10,1... | collective-permute-start | bytes 2359304 | tf_op jit(solution)/shard_map/while/body/eval_jaxpr/ppermute | solution.py:18
  1656.0 15.4 collective-permute-start.5
  1666.2 7.0 collective-permute-start.6
  1837.4 51.6 %collective-permute-start.7 = (f32[6,256,128]{1,2,0:T(8,128)S(1)}, f32[6,256,128]{1,2,0:T(8,128)S(1)}, u32[]{:S(2)}, u32[]{:S(2)}) collective-permute-start(f32[6,256,128]{1,2,0:T(8,128)S(1)} %bitcast.313), channel_id=1, source_target_pairs={{1,0},{2,1},{3,2},{4,3},{5,4},{6,5},{7,6},{8,7},{9,8},{10,9},{11,1... | collective-permute-start | bytes 2359304 | tf_op jit(solution)/shard_map/while/body/eval_jaxpr/ppermute | solution.py:18
  1841.2 57.3 %collective-permute-start.8 = (f32[6,128,256]{2,1,0:T(8,128)}, f32[6,128,256]{2,1,0:T(8,128)}, u32[]{:S(2)}, u32[]{:S(2)}) collective-permute-start(f32[6,128,256]{2,1,0:T(8,128)} %get-tuple-element.925), channel_id=1, source_target_pairs={{0,1},{1,2},{2,3},{3,4},{4,5},{5,6},{6,7},{7,8},{8,9},{9,10},{10,1... | collective-permute-start | bytes 2359304 | tf_op jit(solution)/shard_map/while/body/eval_jaxpr/ppermute | solution.py:18
  1874.9 8.8 collective-permute-start.11
  1876.2 10.9 collective-permute-start.9
  (153 other events, 2014.2 us)
where the time goes:
time: 2070 us; the launch traced here: 2060 us
  other arithmetic  1140 us (55%)
  starting transfers between devices  317 us (15%)
  local copies, waits for them, and re-layouts  218 us (11%)
  matrix products  157 us (8%)
  blocking collectives  156 us (8%)
  loops' own time  37.1 us (2%)
  waiting for transfers between devices  29.4 us (1%)
    another operation x28, other arithmetic, split_sectors(): factor = jnp.linalg.cholesky(gram)  575 us
    another operation x20, other arithmetic, split_sectors(): jax.scipy.linalg.solve_triangular(factor, jnp.swapaxes(sample, 1, 2), low...  473 us
    ppermute x52, starting transfers between devices, shifted(): return lax.ppermute(value, axis, pairs)  312 us
    psum x1, blocking collectives, together(): so_far = lax.psum(vector, axis)  156 us
    dot_general x32, matrix products, product(): jnp.einsum('lam,lmb->lab', first, second, precision=lax.Precision.HIGHEST)  94.1 us
  transfers between devices with their start and end apart: 53, of which 16 were waited for; matrix products, arithmetic and copies ran while one was open for 9% of the time, Pallas kernels for 0%

commit v1 on v0

v1 whole, which is shorter than its diff:
```python
import functools

import jax
import jax.numpy as jnp
from jax import lax
from jax.experimental import pallas as pl
from jax.experimental.pallas import tpu as pltpu
from jax.sharding import PartitionSpec as P

STEPS = 4
N = 128
NSEC = 12
HALF = 6
BLOCK = 2 * N
BULK = HALF * BLOCK
META = 32
F32 = jnp.float32
BF16 = jnp.bfloat16


def parts(x):
    one = x.astype(BF16)
    rest = x - one.astype(F32)
    two = rest.astype(BF16)
    three = (rest - two.astype(F32)).astype(BF16)
    return one, two, three


def dot(a, b, dims):
    return lax.dot_general(a, b, (dims, ((), ())), preferred_element_type=F32)


def product(a, b, dims):
    a1, a2, a3 = a
    b1, b2, b3 = b
    ca, cb = dims[0][0], dims[1][0]
    if a1.shape[ca] <= 128:
        low = dot(jnp.concatenate([a1, a3], ca), jnp.concatenate([b3, b1], cb), dims)
        pair = jnp.concatenate([a2, a1], ca)
        low = low + dot(pair, jnp.concatenate([b2, b2], cb), dims)
        return low + dot(pair, jnp.concatenate([b1, b1], cb), dims)
    out = dot(a1, b3, dims)
    out = out + dot(a3, b1, dims)
    out = out + dot(a2, b2, dims)
    out = out + dot(a1, b2, dims)
    out = out + dot(a2, b1, dims)
    return out + dot(a1, b1, dims)


NN = ((1,), (0,))
NT = ((1,), (1,))
TN = ((0,), (0,))


def row_of(x, m):
    return jnp.broadcast_to(x[m : m + 1, :], x.shape)


def eliminate(rows, start, lane, sub):
    columns = []
    for m in range(8):
        hit = lane == start + m
        columns.append(
            [
                jnp.broadcast_to(
                    jnp.sum(jnp.where(hit, r, 0.0), axis=1, keepdims=True), (8, N)
                )
                for r in rows
            ]
        )
    inside = (lane >= start) & (lane < start + 8)
    out = [jnp.where(inside, jnp.where(lane == start + sub, 1.0, 0.0), rows[0])]
    out += [jnp.where(inside, 0.0, r) for r in rows[1:]]
    scale = jnp.ones((8, N), F32)
    for m in range(8):
        inverse = lax.rsqrt(row_of(columns[m][0], m))
        lower = [c * inverse for c in columns[m]]
        lower[0] = jnp.where(sub > m, lower[0], 0.0)
        for j in range(m + 1, 8):
            factor = row_of(lower[0], j)
            for r in range(len(rows)):
                columns[j][r] = columns[j][r] - lower[r] * factor
        pivot = row_of(out[0], m) * inverse
        for r in range(len(rows)):
            out[r] = out[r] - lower[r] * pivot
        scale = jnp.where(sub == m, inverse, scale)
    out[0] = out[0] * scale
    return out


def invert_factors(gram):
    lane = lax.broadcasted_iota(jnp.int32, (8, N), 1)
    sub = lax.broadcasted_iota(jnp.int32, (8, N), 0)
    wide = lax.broadcasted_iota(jnp.int32, (N, N), 1)
    pair = lax.broadcasted_iota(jnp.int32, (16, N), 1)

    def body(index, carry):
        start = pl.multiple_of(index * 16, 16)
        inside = (wide >= start) & (wide < start + 16)
        for k in range(HALF):
            first = gram[k, pl.ds(start, 8), :]
            second = gram[k, pl.ds(start + 8, 8), :]
            first, second = eliminate([first, second], start, lane, sub)
            first = jnp.where((lane >= start + 8) & (lane < start + 16), 0.0, first)
            (second,) = eliminate([second], start + 8, lane, sub)
            both = jnp.concatenate([first, second], axis=0)
            z1, z2, z3 = parts(both)
            u1, u2, u3 = parts(jnp.where(pair >= start + 16, both, 0.0))
            change = dot(
                jnp.concatenate([u1, u1, u2, u2, u1, u3], 0),
                jnp.concatenate([z1, z2, z1, z2, z3, z1], 0),
                TN,
            )
            gram[k, :, :] = jnp.where(inside, 0.0, gram[k, :, :]) - change
            gram[k, pl.ds(start, 16), :] = both
        return carry

    lax.fori_loop(0, N // 16, body, 0)


def move(pairs, sem):
    copies = [
        pltpu.make_async_copy(source, target, sem.at[i])
        for i, (source, target) in enumerate(pairs)
    ]
    for c in copies:
        c.start()
    for c in copies:
        c.wait()


def sweep_kernel(
    parity,
    first_ref,
    scal,
    acc_in,
    keep,
    recv,
    chip,
    cross,
    sketch,
    acc_out,
    keep_out,
    send_out,
    chip_out,
    cross_out,
    left,
    left_sums,
    left_tail,
    right,
    matrix,
    up,
    down,
    sample,
    gram,
    red,
    bas,
    sem,
):
    core = scal[13]
    left_step = scal[14].astype(jnp.int32)
    right_step = scal[15].astype(jnp.int32)
    phantom = scal[12] > 0.5
    is_zero = core < 0.5
    first = first_ref[0] == 1
    left_kept = jnp.logical_or(first, is_zero if parity == 1 else jnp.logical_not(is_zero))
    left_chip = jnp.logical_or(first, is_zero)

    def load(left_from, right_from):
        move(
            [
                (
                    left_from.at[pl.ds(0, BULK)],
                    left.at[pl.ds(pl.multiple_of((1 - left_step) * BLOCK, BLOCK), BULK)],
                ),
                (left_from.at[pl.ds(BULK, 8)], left_sums),
                (
                    right_from.at[pl.ds(0, BULK)],
                    right.at[pl.ds(pl.multiple_of(right_step * BLOCK, BLOCK), BULK)],
                ),
            ],
            sem,
        )

    def load_edges(left_from, right_from):
        move(
            [
                (
                    left_from.at[pl.ds(0, BLOCK)],
                    left.at[pl.ds(pl.multiple_of(left_step * BULK, BLOCK), BLOCK)],
                ),
                (left_from.at[pl.ds(BLOCK, 8)], left_tail),
                (
                    right_from.at[pl.ds(0, BLOCK)],
                    right.at[pl.ds(pl.multiple_of((1 - right_step) * BULK, BLOCK), BLOCK)],
                ),
            ],
            sem,
        )

    pl.when(left_kept)(lambda: load(keep, recv))
    pl.when(jnp.logical_not(left_kept))(lambda: load(recv, keep))
    pl.when(left_chip)(lambda: load_edges(chip, cross))
    pl.when(jnp.logical_not(left_chip))(lambda: load_edges(cross, chip))

    sums = left_sums[...] + left_tail[...]
    weight_in = sums[0:1, :]
    total_in = sums[1:2, :]
    alpha = 1.0 / jnp.sqrt(weight_in)
    sub = lax.broadcasted_iota(jnp.int32, (8, N), 0)
    lost = 1.0 - weight_in / total_in
    acc_out[...] = acc_in[...] + jnp.where(
        sub == 0, lost, jnp.where(sub == 1, jnp.log(total_in), 0.0)
    )

    def finish(weight, total):
        tail = jnp.where(sub == 0, weight, jnp.where(sub == 1, total, 0.0))
        red[pl.ds(BULK, 8), :] = tail
        bas[pl.ds(BULK, 8), :] = tail

    @pl.when(phantom)
    def _():
        for k in range(HALF):
            at = k * BLOCK
            red[pl.ds(at, N), :] = right[pl.ds(at, N), :]
            red[pl.ds(at + N, N), :] = right[pl.ds(at + BLOCK + N, N), :]
            bas[pl.ds(at, N), :] = left[pl.ds(at + BLOCK, N), :] * alpha
            bas[pl.ds(at + N, N), :] = left[pl.ds(at + N, N), :] * alpha
        one = jnp.full((1, N), 1.0 - core, F32)
        finish(one, one)

    @pl.when(jnp.logical_not(phantom))
    def _():
        g = [scal[i] * alpha for i in range(6)]

        def thetas(k, carry):
            at = pl.multiple_of(k * BLOCK, BLOCK)
            a = jnp.concatenate(
                [left[pl.ds(at + BLOCK, N), :], left[pl.ds(at + N, N), :]], axis=0
            )
            b = jnp.concatenate(
                [right[pl.ds(at, N), :], right[pl.ds(at + BLOCK + N, N), :]], axis=1
            )
            theta = product(parts(a), parts(b), NN)
            matrix[k, 0:N, 0:N] = theta[0:N, 0:N] * g[0]
            matrix[k, N:BLOCK, N:BLOCK] = theta[N:BLOCK, N:BLOCK] * g[1]
            up[k + 1] = theta[0:N, N:BLOCK]
            down[k] = theta[N:BLOCK, 0:N]
            return carry

        lax.fori_loop(0, HALF, thetas, 0)
        up[0] = product(
            parts(left[pl.ds(0, N), :]), parts(right[pl.ds(N, N), :]), NN
        )
        down[HALF] = product(
            parts(left[pl.ds(BULK + N, N), :]), parts(right[pl.ds(BULK, N), :]), NN
        )

        row = lax.broadcasted_iota(jnp.int32, (N, N), 0)
        col = lax.broadcasted_iota(jnp.int32, (N, N), 1)

        def samples(k, total):
            matrix[k, 0:N, N:BLOCK] = up[k + 1] * g[2] + down[k + 1] * g[3]
            matrix[k, N:BLOCK, 0:N] = up[k] * g[4] + down[k] * g[5]
            m = matrix[k]
            squares = jnp.sum(m * m, axis=0, keepdims=True)
            s = product(parts(m), parts(sketch[k]), NN)
            sample[k] = s
            sp = parts(s)
            gr = product(sp, sp, TN)
            diag = jnp.sum(jnp.sum(s * s, axis=0, keepdims=True), axis=1, keepdims=True)
            kept = scal[6 + k]
            ridge = 0.001 * diag / kept + 1e-06
            extra = ridge + jnp.where(col.astype(F32) < kept, 0.0, 1.0)
            gram[k] = gr + jnp.where(row == col, extra, 0.0)
            return total + squares[:, 0:N] + squares[:, N:BLOCK]

        total = lax.fori_loop(0, HALF, samples, jnp.zeros((1, N), F32))
        invert_factors(gram)

        def split(k, weight):
            at = pl.multiple_of(k * BLOCK, BLOCK)
            x = jnp.where(col <= row, gram[k], 0.0)
            basis = product(parts(sample[k]), parts(x), NT)
            bas[pl.ds(at, BLOCK), :] = basis
            reduced = product(parts(basis), parts(matrix[k]), TN)
            red[pl.ds(at, N), :] = reduced[:, 0:N]
            red[pl.ds(at + N, N), :] = reduced[:, N:BLOCK]
            squares = jnp.sum(reduced * reduced, axis=0, keepdims=True)
            return weight + squares[:, 0:N] + squares[:, N:BLOCK]

        weight = lax.fori_loop(0, HALF, split, jnp.zeros((1, N), F32))
        finish(
            jnp.broadcast_to(jnp.sum(weight, axis=1, keepdims=True), (1, N)),
            jnp.broadcast_to(jnp.sum(total, axis=1, keepdims=True), (1, N)),
        )

    last = (HALF - 1) * BLOCK
    red_edge_at = pl.multiple_of((1 - right_step) * last, BLOCK)
    bas_edge_at = pl.multiple_of(left_step * last, BLOCK)

    def store(kept, sent):
        move([(kept, keep_out), (sent, send_out)], sem)

    def store_edges(red_edge, bas_edge):
        move(
            [
                (red.at[pl.ds(red_edge_at, BLOCK)], red_edge.at[pl.ds(0, BLOCK)]),
                (red.at[pl.ds(BULK, 8)], red_edge.at[pl.ds(BLOCK, 8)]),
                (bas.at[pl.ds(bas_edge_at, BLOCK)], bas_edge.at[pl.ds(0, BLOCK)]),
                (bas.at[pl.ds(BULK, 8)], bas_edge.at[pl.ds(BLOCK, 8)]),
            ],
            sem,
        )

    keeps_red = jnp.logical_not(is_zero) if parity == 1 else is_zero
    pl.when(keeps_red)(lambda: store(red, bas))
    pl.when(jnp.logical_not(keeps_red))(lambda: store(bas, red))
    pl.when(is_zero)(lambda: store_edges(cross_out, chip_out))
    pl.when(jnp.logical_not(is_zero))(lambda: store_edges(chip_out, cross_out))


VM = pl.BlockSpec(memory_space=pltpu.VMEM)
SM = pl.BlockSpec(memory_space=pltpu.SMEM)
HB = pl.BlockSpec(memory_space=pl.ANY)


def shape(*dims):
    return jax.ShapeDtypeStruct(dims, F32)


def sweep(parity, first, scal, acc, keep, recv, chip, cross, sketch):
    return pl.pallas_call(
        functools.partial(sweep_kernel, parity),
        out_shape=(
            shape(8, N),
            shape(BULK + 8, N),
            shape(BULK + 8, N),
            shape(BLOCK + 8, N),
            shape(BLOCK + 8, N),
        ),
        in_specs=[SM, SM, VM, HB, HB, HB, HB, VM],
        out_specs=(VM, HB, HB, HB, HB),
        scratch_shapes=[
            pltpu.VMEM((BLOCK + BULK, N), F32),
            pltpu.VMEM((8, N), F32),
            pltpu.VMEM((8, N), F32),
            pltpu.VMEM((BULK + BLOCK, N), F32),
            pltpu.VMEM((HALF, BLOCK, BLOCK), F32),
            pltpu.VMEM((HALF + 1, N, N), F32),
            pltpu.VMEM((HALF + 1, N, N), F32),
            pltpu.VMEM((HALF, BLOCK, N), F32),
            pltpu.VMEM((HALF, N, N), F32),
            pltpu.VMEM((BULK + 8, N), F32),
            pltpu.VMEM((BULK + 8, N), F32),
            pltpu.SemaphoreType.DMA((4,)),
        ],
        compiler_params=pltpu.CompilerParams(vmem_limit_bytes=56 * 1024 * 1024),
        cost_estimate=pl.CostEstimate(
            flops=4 * 10**8, bytes_accessed=4 * 10**6, transcendentals=0
        ),
        name="sweep",
    )(first, scal, acc, keep, recv, chip, cross, sketch)


HERE, THERE, AFTER, BEFORE = 0, 1, 2, 3


def wrap(index):
    return lax.rem(index + NSEC, NSEC)


def bond_scalars(scal, meta, bond, beyond, half, phantom, core):
    for i in range(6):
        scal[i] = meta[bond, i]
    for k in range(HALF):
        scal[6 + k] = meta[bond, 7 + half + k]
    scal[12] = jnp.where(phantom, 1.0, 0.0)
    scal[13] = jnp.where(core == 0, 0.0, 1.0)
    scal[14] = meta[bond, 6]
    scal[15] = meta[beyond, 6]


def mask_sketch(sketch, scal):
    col = lax.broadcasted_iota(jnp.int32, (BLOCK, N), 1).astype(F32)
    for k in range(HALF):
        sketch[k] = jnp.where(col < scal[6 + k], sketch[k], 0.0)


def start_kernel(
    pos, meta, site, other, mine, theirs, scal, odd_scal, left, right, chip, cross, sketch, sem
):
    position = pos[0]
    chain = pos[1]
    core = lax.rem(position, 2)
    half = core * HALF
    bond_scalars(scal, meta, HERE, THERE, half, False, core)
    phantom = jnp.where(core == 0, position == chain - 2, position == 1)
    odd = jnp.where(core == 0, THERE, BEFORE)
    beyond = jnp.where(core == 0, AFTER, HERE)
    bond_scalars(odd_scal, meta, odd, beyond, half, phantom, core)
    step = meta[HERE, 6].astype(jnp.int32)
    next_step = meta[THERE, 6].astype(jnp.int32)
    edge_left = wrap(half + jnp.where(step == 1, HALF, -1))
    edge_right = half + jnp.where(next_step == 1, -1, HALF)
    row = lax.broadcasted_iota(jnp.int32, (N, N), 0).astype(F32)
    col = lax.broadcasted_iota(jnp.int32, (N, N), 1).astype(F32)

    blocks = []
    for p in range(2):
        for k in range(HALF):
            at = k * BLOCK + p * N
            blocks.append((left, at, 0, p, half + k))
            blocks.append((right, at, 1, p, wrap(half + k - p + next_step)))
        blocks.append((chip, p * N, 0, p, edge_left))
        blocks.append((cross, p * N, 1, p, wrap(edge_right - p + next_step)))

    def load(pair, sketch_from):
        move(
            [(sketch_from.at[pl.ds(half, HALF)], sketch)]
            + [
                (pair[which].at[p, sector], ref.at[pl.ds(at, N)])
                for ref, at, which, p, sector in blocks
            ],
            sem,
        )

    pl.when(core == 0)(lambda: load((site, other), mine))
    pl.when(core == 1)(lambda: load((other, site), theirs))
    mask_sketch(sketch, scal)
    for ref, at, which, p, sector in blocks:
        target = wrap(sector + p - (next_step if which else step))
        rows = meta[THERE if which else HERE, 19 + sector]
        cols = meta[AFTER if which else THERE, 19 + target]
        ref[pl.ds(at, N), :] = jnp.where(
            (row < rows) & (col < cols), ref[pl.ds(at, N), :], 0.0
        )
    left[pl.ds(BULK, 8), :] = jnp.ones((8, N), F32)
    right[pl.ds(BULK, 8), :] = jnp.ones((8, N), F32)
    chip[pl.ds(BLOCK, 8), :] = jnp.zeros((8, N), F32)
    cross[pl.ds(BLOCK, 8), :] = jnp.zeros((8, N), F32)


def start(position, meta, site, other, mine, theirs):
    return pl.pallas_call(
        start_kernel,
        out_shape=(
            shape(16),
            shape(16),
            shape(BULK + 8, N),
            shape(BULK + 8, N),
            shape(BLOCK + 8, N),
            shape(BLOCK + 8, N),
            shape(HALF, BLOCK, N),
        ),
        in_specs=[SM, SM, HB, HB, HB, HB],
        out_specs=(SM, SM, VM, VM, VM, VM, VM),
        scratch_shapes=[pltpu.SemaphoreType.DMA((4 * HALF + 5,))],
        compiler_params=pltpu.CompilerParams(vmem_limit_bytes=24 * 1024 * 1024),
        name="start",
    )(position, meta, site, other, mine, theirs)


def odd_sketch_kernel(pos, odd_scal, theirs, behind, sketch, sem):
    core = lax.rem(pos[0], 2)

    def load(source):
        move([(source.at[pl.ds(core * HALF, HALF)], sketch)], sem)

    pl.when(core == 0)(lambda: load(theirs))
    pl.when(core == 1)(lambda: load(behind))
    mask_sketch(sketch, odd_scal)


def odd_sketch(position, odd_scal, theirs, behind):
    return pl.pallas_call(
        odd_sketch_kernel,
        out_shape=shape(HALF, BLOCK, N),
        in_specs=[SM, SM, HB, HB],
        out_specs=VM,
        scratch_shapes=[pltpu.SemaphoreType.DMA((1,))],
        compiler_params=pltpu.CompilerParams(vmem_limit_bytes=16 * 1024 * 1024),
        name="odd_sketch",
    )(position, odd_scal, theirs, behind)


def finish_kernel(pos, meta, acc, recv, swap, out, acc_out, sem):
    position = pos[0]
    core = lax.rem(position, 2)
    step = jnp.where(core == 0, 0.0, meta[THERE, 6]).astype(jnp.int32)
    sums = recv[pl.ds(BULK, 8), :] + swap[pl.ds(BULK, 8), :]
    weight = sums[0:1, :]
    total = sums[1:2, :]
    sub = lax.broadcasted_iota(jnp.int32, (8, N), 0)
    new = jnp.where(
        sub == 0, 1.0 - weight / total, jnp.where(sub == 1, jnp.log(total), 0.0)
    )
    acc_out[...] = jnp.where(core == 0, acc[...] + new, 0.0)

    @pl.when(core == 0)
    def _():
        alpha = 1.0 / jnp.sqrt(weight)
        recv[pl.ds(0, BULK), :] = recv[pl.ds(0, BULK), :] * alpha
        swap[pl.ds(0, BULK), :] = swap[pl.ds(0, BULK), :] * alpha
        pairs = []
        for k in range(HALF):
            for p in range(2):
                rows = pl.ds(k * BLOCK + p * N, N)
                pairs.append((recv.at[rows], out.at[p, k]))
                pairs.append((swap.at[rows], out.at[p, k + HALF]))
        move(pairs, sem)

    @pl.when(core == 1)
    def _():
        pairs = []
        for k in range(HALF):
            for p in range(2):
                rows = pl.ds(k * BLOCK + p * N, N)
                pairs.append((swap.at[rows], out.at[p, wrap(k - p + step)]))
                pairs.append((recv.at[rows], out.at[p, wrap(k + HALF - p + step)]))
        move(pairs, sem)


def finish(position, meta, acc, recv, swap):
    return pl.pallas_call(
        finish_kernel,
        out_shape=(shape(2, NSEC, N, N), shape(8, N)),
        in_specs=[SM, SM, VM, VM, VM],
        out_specs=(HB, VM),
        scratch_shapes=[pltpu.SemaphoreType.DMA((4 * HALF,))],
        compiler_params=pltpu.CompilerParams(vmem_limit_bytes=16 * 1024 * 1024),
        name="finish",
    )(position, meta, acc, recv, swap)


def everywhere(value, chain):
    stride = 1
    while stride < chain:
        size = 4 if (chain // stride) % 4 == 0 and stride > 1 else 2
        terms = [value]
        for turn in range(1, size):
            moves = [(i, i ^ (turn * stride)) for i in range(chain)]
            terms.append(lax.ppermute(value, "site", moves))
        while len(terms) > 1:
            terms = [a + b for a, b in zip(terms[0::2], terms[1::2])]
        value = terms[0]
        stride *= size
    return value


def body(sites, sector_sizes, charge_steps, kept_counts, gates, sketches):
    chain = lax.axis_size("site")
    here = lax.axis_index("site").astype(jnp.int32)
    position = jnp.stack([here, jnp.int32(chain)])
    core = here % 2
    chips = chain // 2

    def device(chip, core):
        return 2 * (chip % chips) + core

    swap = [(i, i ^ 1) for i in range(chain)]
    over = [(device(j, 0), device(j + 1, 1)) for j in range(chips)]
    over += [(device(j + 1, 1), device(j, 0)) for j in range(chips)]
    apart = [(device(j, 0), device(j - 1, 0)) for j in range(chips)]
    apart += [(device(j, 1), device(j + 1, 1)) for j in range(chips)]
    back = [(target, source) for source, target in apart]
    ahead = [(device(j, 1), device(j + 1, 1)) for j in range(chips)]

    row = jnp.concatenate(
        [
            gates[0],
            charge_steps.astype(F32),
            kept_counts[0].astype(F32),
            sector_sizes[0].astype(F32),
            jnp.zeros((1,), F32),
        ]
    )
    partner = lax.ppermute(row, "site", swap)
    along = lax.ppermute(row, "site", apart)
    across = lax.ppermute(along, "site", swap)
    after = jnp.where(core == 0, along, across)
    before = jnp.where(core == 0, across, along)
    meta = jnp.stack(
        [
            jnp.where(core == 0, row, partner),
            jnp.where(core == 0, partner, row),
            after,
            before,
        ]
    )
    site = sites[0]
    sketch = sketches[0]
    other = lax.ppermute(site, "site", swap)
    theirs = lax.ppermute(sketch, "site", swap)
    later, meta = lax.optimization_barrier((sketch, meta))
    behind = lax.ppermute(later, "site", ahead)
    scal, odd_scal, left, right, chip, cross, even = start(
        position, meta, site, other, sketch, theirs
    )
    odd = odd_sketch(position, odd_scal, theirs, behind)

    def spread(out, moves):
        acc, keep, send, chip, cross = out
        recv = lax.ppermute(send, "site", moves)
        cross = lax.ppermute(cross, "site", over)
        chip = lax.ppermute(chip, "site", swap)
        return acc, keep, recv, chip, cross

    def step(index, carry):
        first = jnp.where(index == 0, 1, 0).astype(jnp.int32)[None]
        none = jnp.zeros((1,), jnp.int32)
        carry = spread(sweep(0, first, scal, *carry, even), apart)
        return spread(sweep(1, none, scal_odd, *carry, odd), back)

    scal_odd = odd_scal
    carry = (jnp.zeros((8, N), F32), left, right, chip, cross)
    acc, keep, recv, chip, cross = lax.fori_loop(0, STEPS, step, carry)
    swapped = lax.ppermute(keep, "site", swap)
    out, acc = finish(position, meta, acc, recv, swapped)
    totals = everywhere(acc, chain)[0:2, 0]
    return (out[None], totals)


def solution(mesh):
    placed = (
        P("site", None, None, None, None),
        P("site", None),
        P("site"),
        P("site", None),
        P("site", None),
        P("site", None, None, None),
    )
    return jax.shard_map(
        body,
        mesh=mesh,
        in_specs=placed,
        out_specs=(P("site", None, None, None, None), P()),
        check_vma=False,
    )
```

time: 2070 us -> 541 us (0.26)
  other arithmetic: 1140 us -> 0.79 us
  Pallas kernels: 0 us -> 334 us
  starting transfers between devices: 317 us -> 85.3 us
  local copies, waits for them, and re-layouts: 218 us -> 11.3 us
  matrix products: 157 us -> 0 us
  blocking collectives: 156 us -> 0 us
  waiting for transfers between devices: 29.4 us -> 107 us
  loops' own time: 37.1 us -> 0.18 us
    another operation x64 -> x4, other arithmetic: 1070 us -> 0.1 us  [the longest x1 0.08 us: body(): position = jnp.stack([here, jnp.int32(chain)])]
    pallas_call x0 -> x11, Pallas kernels: none -> 334 us  [the longest x8 326 us: sweep(): pl.pallas_call(functools.partial(sweep_kernel, parity), out_shape=(shape(...]
    ppermute x53 -> x41, starting transfers between devices: 317 us -> 85.3 us  [the longest x8 34.5 us: spread(): chip = lax.ppermute(chip, 'site', swap)]
    gather x102 -> x0, local copies, waits for them, and re-layouts: 172 us -> none  [the longest x16 35.3 us: split_sectors(): upper = jnp.concatenate([blocks[0][top], blocks[1][top]], axis=2)]
    psum x1 -> x0, blocking collectives: 156 us -> none  [together(): so_far = lax.psum(vector, axis)]
    dot_general x56 -> x0, matrix products: 150 us -> none  [the longest x32 94.1 us: product(): jnp.einsum('lam,lmb->lab', first, second, precision=lax.Precision.HIGHEST)]
    ppermute x53 -> x41, waiting for transfers between devices: 29.4 us -> 107 us  [the longest x8 44 us: spread(): cross = lax.ppermute(cross, 'site', over)]
    another operation x1, loops' own time: 37.1 us -> 0.18 us  [body(): acc, keep, recv, chip, cross = lax.fori_loop(0, STEPS, step, carry)]
  transfers between devices with their start and end apart: 53 -> 41, of which waited for: 16 -> 32; matrix products, arithmetic and copies ran while one was open for 9% -> 0% of each run, Pallas kernels for 0% -> 1%
where the time goes in v1:
time: 541 us; the launch traced here: 540 us
  Pallas kernels  334 us (62%)
  waiting for transfers between devices  107 us (20%)
  starting transfers between devices  85.3 us (16%)
  local copies, waits for them, and re-layouts  11.3 us (2%)
    pallas_call x8, Pallas kernels, sweep(): pl.pallas_call(functools.partial(sweep_kernel, parity), out_shape=(shape(...  326 us
    ppermute x8, waiting for transfers between devices, spread(): cross = lax.ppermute(cross, 'site', over)  44 us
    ppermute x8, waiting for transfers between devices, spread(): recv = lax.ppermute(send, 'site', moves)  36.9 us
    ppermute x8, starting transfers between devices, spread(): chip = lax.ppermute(chip, 'site', swap)  34.5 us
    ppermute x8, starting transfers between devices, spread(): recv = lax.ppermute(send, 'site', moves)  24.1 us
    ppermute x10, starting transfers between devices, everywhere(): terms.append(lax.ppermute(value, 'site', moves))  14.5 us
  transfers between devices with their start and end apart: 41, of which 32 were waited for; matrix products, arithmetic and copies ran while one was open for 0% of the time, Pallas kernels for 1%

profile of v1, /device:TPU:0, one launch (start us, length us, event | category | flops | bytes accessed | tf_op | source)
XLA Modules:
  0.0 540.1 jit_solution(6996140510689735494)
XLA Ops:
  2.7 8.8 %collective-permute-start.7 = (f32[32]{0:T(128)S(1)}, f32[32]{0:T(128)S(1)}, u32[]{:S(2)}, u32[]{:S(2)}) collective-permute-start(f32[32]{0:T(128)S(1)} %concatenate.3), channel_id=1, source_target_pairs={{0,126},{2,0},{4,2},{6,4},{8,6},{10,8},{12,10},{14,12},{16,14},{18... | collective-permute-start | bytes 392 | tf_op jit(solution)/shard_map/ppermute | solution.py:579
  12.8 4.7 collective-permute-done.8
  18.4 1.4 copy-done
  19.8 1.4 copy-done.1
  21.2 4.7 start.1
  25.9 1.6 odd_sketch.1
  27.5 483.3 %while.21 = (s32[]{:T(128)}, f32[8,128]{1,0:T(8,128)S(1)}, f32[1544,128]{1,0:T(8,128)}, f32[1544,128]{1,0:T(8,128)}, f32[264,128]{1,0:T(8,128)S(1)}, /*index=5*/...) while((s32[]{:T(128)}, f32[8,128]{1,0:T(8,128)S(1)}, ...), condition=%wide.region_1.2_spmd, body=%wide.region_0.1_spmd.sunk | while | flops 800000000 | bytes 27038736 | solution.py:617
  27.5 40.9 %sweep.10 = (f32[8,128]{1,0:T(8,128)}, f32[1544,128]{1,0:T(8,128)}, f32[1544,128]{1,0:T(8,128)}, f32[264,128]{1,0:T(8,128)}, f32[264,128]{1,0:T(8,128)}) custom-call(s32[1]{0:T(128)} %bitcast.19.first_ref, f32[16]{0:T(128)S(1)} %get-tuple-element.328.scal, f32[8,128]{1,0:T(8,128)S(1)} %get-tuple-element.310.acc_in, f32[1544,128]{1,0:T(8,128)} %get-tuple-element.311.keep, ...), custom_call_target="tpu_custom_call" | custom-call | flops 400000000 | bytes 4000000 | tf_op jit(solution)/shard_map/while/body/eval_jaxpr/sweep/pallas_call | solution.py:333
  68.5 4.2 collective-permute-start
  72.7 14.5 %collective-permute-start.1 = (f32[264,128]{1,0:T(8,128)}, f32[264,128]{1,0:T(8,128)S(1)}, u32[]{:S(2)}, u32[]{:S(2)}) collective-permute-start(f32[264,128]{1,0:T(8,128)} %get-tuple-element.289), channel_id=1, source_target_pairs={{0,1},{1,0},{2,3},{3,2},{4,5},{5,4},{6,7},{7,6},{8,9},{9,8},{10,11... | collective-permute-start | bytes 405512 | tf_op jit(solution)/shard_map/while/body/eval_jaxpr/ppermute | solution.py:606
  87.2 1.2 collective-permute-done.1.chip
  88.4 3.4 collective-permute-done.2.cross
  92.8 40.5 %sweep.11 = (f32[8,128]{1,0:T(8,128)S(1)}, f32[1544,128]{1,0:T(8,128)}, f32[1544,128]{1,0:T(8,128)}, f32[264,128]{1,0:T(8,128)}, f32[264,128]{1,0:T(8,128)}) custom-call(s32[1]{0:T(128)} %get-tuple-element.333.first_ref, f32[16]{0:T(128)S(1)} %get-tuple-element.330.scal, f32[8,128]{1,0:T(8,128)} %get-tuple-element.286.acc_in, ...), custom_call_target="tpu_custom_call" | custom-call | flops 400000000 | bytes 4000000 | tf_op jit(solution)/shard_map/while/body/eval_jaxpr/sweep/pallas_call | solution.py:333
  133.3 12.8 %collective-permute-start.4 = (f32[264,128]{1,0:T(8,128)}, f32[264,128]{1,0:T(8,128)S(1)}, u32[]{:S(2)}, u32[]{:S(2)}) collective-permute-start(f32[264,128]{1,0:T(8,128)} %get-tuple-element.294), channel_id=1, source_target_pairs={{0,1},{1,0},{2,3},{3,2},{4,5},{5,4},{6,7},{7,6},{8,9},{9,8},{10,11... | collective-permute-start | bytes 405512 | tf_op jit(solution)/shard_map/while/body/eval_jaxpr/ppermute | solution.py:606
  146.2 1.2 collective-permute-done.4
  147.4 5.0 collective-permute-done.5
  153.3 40.9 %sweep.10 = (f32[8,128]{1,0:T(8,128)}, f32[1544,128]{1,0:T(8,128)}, f32[1544,128]{1,0:T(8,128)}, f32[264,128]{1,0:T(8,128)}, f32[264,128]{1,0:T(8,128)}) custom-call(s32[1]{0:T(128)} %bitcast.19.first_ref, f32[16]{0:T(128)S(1)} %get-tuple-element.328.scal, f32[8,128]{1,0:T(8,128)S(1)} %get-tuple-element.310.acc_in, f32[1544,128]{1,0:T(8,128)} %get-tuple-element.311.keep, ...), custom_call_target="tpu_custom_call" | custom-call | flops 400000000 | bytes 4000000 | tf_op jit(solution)/shard_map/while/body/eval_jaxpr/sweep/pallas_call | solution.py:333
  194.2 12.3 %collective-permute-start = (f32[1544,128]{1,0:T(8,128)}, f32[1544,128]{1,0:T(8,128)S(1)}, u32[]{:S(2)}, u32[]{:S(2)}) collective-permute-start(f32[1544,128]{1,0:T(8,128)} %get-tuple-element.288), channel_id=1, source_target_pairs={{0,126},{2,0},{4,2},{6,4},{8,6},{10,8},{12,10},{14,12},{16,14},{18... | collective-permute-start | bytes 2371592 | tf_op jit(solution)/shard_map/while/body/eval_jaxpr/ppermute | solution.py:604
  206.5 1.6 collective-permute-done.1.chip
  208.1 3.1 collective-permute-done.2.cross
  211.2 6.5 %collective-permute-done.recv = f32[1544,128]{1,0:T(8,128)S(1)} collective-permute-done((f32[1544,128]{1,0:T(8,128)}, f32[1544,128]{1,0:T(8,128)S(1)}, u32[]{:S(2)}, u32[]{:S(2)}) %collective-permute-start) | collective-permute-done | bytes 790560 | tf_op jit(solution)/shard_map/while/body/eval_jaxpr/ppermute | solution.py:604
  218.6 40.5 %sweep.11 = (f32[8,128]{1,0:T(8,128)S(1)}, f32[1544,128]{1,0:T(8,128)}, f32[1544,128]{1,0:T(8,128)}, f32[264,128]{1,0:T(8,128)}, f32[264,128]{1,0:T(8,128)}) custom-call(s32[1]{0:T(128)} %get-tuple-element.333.first_ref, f32[16]{0:T(128)S(1)} %get-tuple-element.330.scal, f32[8,128]{1,0:T(8,128)} %get-tuple-element.286.acc_in, ...), custom_call_target="tpu_custom_call" | custom-call | flops 400000000 | bytes 4000000 | tf_op jit(solution)/shard_map/while/body/eval_jaxpr/sweep/pallas_call | solution.py:333
  259.3 1.5 collective-permute-done.4
  260.8 9.7 %collective-permute-done.5 = f32[264,128]{1,0:T(8,128)S(1)} collective-permute-done((f32[264,128]{1,0:T(8,128)}, f32[264,128]{1,0:T(8,128)S(1)}, u32[]{:S(2)}, u32[]{:S(2)}) %collective-permute-start.5) | collective-permute-done | bytes 135200 | tf_op jit(solution)/shard_map/while/body/eval_jaxpr/ppermute | solution.py:605
  270.4 6.4 %collective-permute-done.3 = f32[1544,128]{1,0:T(8,128)S(1)} collective-permute-done((f32[1544,128]{1,0:T(8,128)}, f32[1544,128]{1,0:T(8,128)S(1)}, u32[]{:S(2)}, u32[]{:S(2)}) %collective-permute-start.3) | collective-permute-done | bytes 790560 | tf_op jit(solution)/shard_map/while/body/eval_jaxpr/ppermute | solution.py:604
  277.7 40.9 %sweep.10 = (f32[8,128]{1,0:T(8,128)}, f32[1544,128]{1,0:T(8,128)}, f32[1544,128]{1,0:T(8,128)}, f32[264,128]{1,0:T(8,128)}, f32[264,128]{1,0:T(8,128)}) custom-call(s32[1]{0:T(128)} %bitcast.19.first_ref, f32[16]{0:T(128)S(1)} %get-tuple-element.328.scal, f32[8,128]{1,0:T(8,128)S(1)} %get-tuple-element.310.acc_in, f32[1544,128]{1,0:T(8,128)} %get-tuple-element.311.keep, ...), custom_call_target="tpu_custom_call" | custom-call | flops 400000000 | bytes 4000000 | tf_op jit(solution)/shard_map/while/body/eval_jaxpr/sweep/pallas_call | solution.py:333
  321.4 4.8 collective-permute-done.2.cross
  326.2 6.2 %collective-permute-done.recv = f32[1544,128]{1,0:T(8,128)S(1)} collective-permute-done((f32[1544,128]{1,0:T(8,128)}, f32[1544,128]{1,0:T(8,128)S(1)}, u32[]{:S(2)}, u32[]{:S(2)}) %collective-permute-start) | collective-permute-done | bytes 790560 | tf_op jit(solution)/shard_map/while/body/eval_jaxpr/ppermute | solution.py:604
  333.3 40.5 %sweep.11 = (f32[8,128]{1,0:T(8,128)S(1)}, f32[1544,128]{1,0:T(8,128)}, f32[1544,128]{1,0:T(8,128)}, f32[264,128]{1,0:T(8,128)}, f32[264,128]{1,0:T(8,128)}) custom-call(s32[1]{0:T(128)} %get-tuple-element.333.first_ref, f32[16]{0:T(128)S(1)} %get-tuple-element.330.scal, f32[8,128]{1,0:T(8,128)} %get-tuple-element.286.acc_in, ...), custom_call_target="tpu_custom_call" | custom-call | flops 400000000 | bytes 4000000 | tf_op jit(solution)/shard_map/while/body/eval_jaxpr/sweep/pallas_call | solution.py:333
  373.8 5.2 collective-permute-start.4
  380.3 5.0 collective-permute-done.5
  385.2 6.3 %collective-permute-done.3 = f32[1544,128]{1,0:T(8,128)S(1)} collective-permute-done((f32[1544,128]{1,0:T(8,128)}, f32[1544,128]{1,0:T(8,128)S(1)}, u32[]{:S(2)}, u32[]{:S(2)}) %collective-permute-start.3) | collective-permute-done | bytes 790560 | tf_op jit(solution)/shard_map/while/body/eval_jaxpr/ppermute | solution.py:604
  392.4 40.9 %sweep.10 = (f32[8,128]{1,0:T(8,128)}, f32[1544,128]{1,0:T(8,128)}, f32[1544,128]{1,0:T(8,128)}, f32[264,128]{1,0:T(8,128)}, f32[264,128]{1,0:T(8,128)}) custom-call(s32[1]{0:T(128)} %bitcast.19.first_ref, f32[16]{0:T(128)S(1)} %get-tuple-element.328.scal, f32[8,128]{1,0:T(8,128)S(1)} %get-tuple-element.310.acc_in, f32[1544,128]{1,0:T(8,128)} %get-tuple-element.311.keep, ...), custom_call_target="tpu_custom_call" | custom-call | flops 400000000 | bytes 4000000 | tf_op jit(solution)/shard_map/while/body/eval_jaxpr/sweep/pallas_call | solution.py:333
  433.3 6.1 %collective-permute-start = (f32[1544,128]{1,0:T(8,128)}, f32[1544,128]{1,0:T(8,128)S(1)}, u32[]{:S(2)}, u32[]{:S(2)}) collective-permute-start(f32[1544,128]{1,0:T(8,128)} %get-tuple-element.288), channel_id=1, source_target_pairs={{0,126},{2,0},{4,2},{6,4},{8,6},{10,8},{12,10},{14,12},{16,14},{18... | collective-permute-start | bytes 2371592 | tf_op jit(solution)/shard_map/while/body/eval_jaxpr/ppermute | solution.py:604
  439.4 1.6 collective-permute-done.1.chip
  441.0 4.5 collective-permute-done.2.cross
  445.5 5.2 collective-permute-done.recv
  451.6 40.5 %sweep.11 = (f32[8,128]{1,0:T(8,128)S(1)}, f32[1544,128]{1,0:T(8,128)}, f32[1544,128]{1,0:T(8,128)}, f32[264,128]{1,0:T(8,128)}, f32[264,128]{1,0:T(8,128)}) custom-call(s32[1]{0:T(128)} %get-tuple-element.333.first_ref, f32[16]{0:T(128)S(1)} %get-tuple-element.330.scal, f32[8,128]{1,0:T(8,128)} %get-tuple-element.286.acc_in, ...), custom_call_target="tpu_custom_call" | custom-call | flops 400000000 | bytes 4000000 | tf_op jit(solution)/shard_map/while/body/eval_jaxpr/sweep/pallas_call | solution.py:333
  492.2 1.6 collective-permute-start.4
  495.0 8.5 %collective-permute-done.5 = f32[264,128]{1,0:T(8,128)S(1)} collective-permute-done((f32[264,128]{1,0:T(8,128)}, f32[264,128]{1,0:T(8,128)S(1)}, u32[]{:S(2)}, u32[]{:S(2)}) %collective-permute-start.5) | collective-permute-done | bytes 135200 | tf_op jit(solution)/shard_map/while/body/eval_jaxpr/ppermute | solution.py:605
  503.5 6.4 %collective-permute-done.3 = f32[1544,128]{1,0:T(8,128)S(1)} collective-permute-done((f32[1544,128]{1,0:T(8,128)}, f32[1544,128]{1,0:T(8,128)S(1)}, u32[]{:S(2)}, u32[]{:S(2)}) %collective-permute-start.3) | collective-permute-done | bytes 790560 | tf_op jit(solution)/shard_map/while/body/eval_jaxpr/ppermute | solution.py:604
  510.7 1.3 collective-permute-start.12
  512.0 2.1 collective-permute-done.12.swap
  514.1 2.6 finish.1
  518.0 4.7 collective-permute-start.16
  524.4 4.6 collective-permute-start.19
  530.6 4.1 collective-permute-start.21
  536.2 3.2 collective-permute-done.22
  (102 shorter events, 23.1 us)
Async XLA Ops:
  2.7 10.1 %collective-permute-start.6 = (f32[32]{0:T(128)S(1)}, f32[32]{0:T(128)S(1)}, u32[]{:S(2)}, u32[]{:S(2)}) collective-permute-start(f32[32]{0:T(128)S(1)} %concatenate.3), channel_id=1, source_target_pairs={{0,1},{1,0},{2,3},{3,2},{4,5},{5,4},{6,7},{7,6},{8,9},{9,8},{10,11... | collective-permute-start | bytes 392 | tf_op jit(solution)/shard_map/ppermute | solution.py:578
  2.7 10.1 %collective-permute-start.7 = (f32[32]{0:T(128)S(1)}, f32[32]{0:T(128)S(1)}, u32[]{:S(2)}, u32[]{:S(2)}) collective-permute-start(f32[32]{0:T(128)S(1)} %concatenate.3), channel_id=1, source_target_pairs={{0,126},{2,0},{4,2},{6,4},{8,6},{10,8},{12,10},{14,12},{16,14},{18... | collective-permute-start | bytes 392 | tf_op jit(solution)/shard_map/ppermute | solution.py:579
  11.5 6.9 %collective-permute-start.10 = (f32[12,256,128]{2,1,0:T(8,128)}, f32[12,256,128]{2,1,0:T(8,128)S(1)}, u32[]{:S(2)}, u32[]{:S(2)}) collective-permute-start(f32[12,256,128]{2,1,0:T(8,128)} %bitcast.22), channel_id=1, source_target_pairs={{0,1},{1,0},{2,3},{3,2},{4,5},{5,4},{6,7},{7,6},{8,9},{9,8},{10,11... | collective-permute-start | bytes 4718600 | tf_op jit(solution)/shard_map/ppermute | solution.py:594
  11.5 6.9 %collective-permute-start.9 = (f32[2,12,128,128]{3,2,1,0:T(8,128)}, f32[2,12,128,128]{3,2,1,0:T(8,128)}, u32[]{:S(2)}, u32[]{:S(2)}) collective-permute-start(f32[2,12,128,128]{3,2,1,0:T(8,128)} %bitcast.20), channel_id=1, source_target_pairs={{0,1},{1,0},{2,3},{3,2},{4,5},{5,4},{6,7},{7,6},{8,9},{9,8},{10,11... | collective-permute-start | bytes 4718600 | tf_op jit(solution)/shard_map/ppermute | solution.py:593
  12.8 4.7 collective-permute-start.8
  17.5 8.4 %collective-permute-start.11 = (f32[12,256,128]{2,1,0:T(8,128)}, f32[12,256,128]{2,1,0:T(8,128)S(1)}, u32[]{:S(2)}, u32[]{:S(2)}) collective-permute-start(f32[12,256,128]{2,1,0:T(8,128)} %bitcast.23), channel_id=1, source_target_pairs={{1,3},{3,5},{5,7},{7,9},{9,11},{11,13},{13,15},{15,17},{17,19},{19... | collective-permute-start | bytes 4718600 | tf_op jit(solution)/shard_map/ppermute | solution.py:596
  27.5 65.3 %copy-start.3 = (f32[6,256,128]{2,1,0:T(8,128)S(1)}, f32[6,256,128]{2,1,0:T(8,128)}, u32[]{:S(2)}) copy-start(f32[6,256,128]{2,1,0:T(8,128)} %get-tuple-element.331.sketch) | copy-start | bytes 2359300 | tf_op jit(solution)/shard_map/while
  68.5 23.4 %collective-permute-start = (f32[1544,128]{1,0:T(8,128)}, f32[1544,128]{1,0:T(8,128)S(1)}, u32[]{:S(2)}, u32[]{:S(2)}) collective-permute-start(f32[1544,128]{1,0:T(8,128)} %get-tuple-element.288), channel_id=1, source_target_pairs={{0,126},{2,0},{4,2},{6,4},{8,6},{10,8},{12,10},{14,12},{16,14},{18... | collective-permute-start | bytes 2371592 | tf_op jit(solution)/shard_map/while/body/eval_jaxpr/ppermute | solution.py:604
  72.7 15.7 %collective-permute-start.1 = (f32[264,128]{1,0:T(8,128)}, f32[264,128]{1,0:T(8,128)S(1)}, u32[]{:S(2)}, u32[]{:S(2)}) collective-permute-start(f32[264,128]{1,0:T(8,128)} %get-tuple-element.289), channel_id=1, source_target_pairs={{0,1},{1,0},{2,3},{3,2},{4,5},{5,4},{6,7},{7,6},{8,9},{9,8},{10,11... | collective-permute-start | bytes 405512 | tf_op jit(solution)/shard_map/while/body/eval_jaxpr/ppermute | solution.py:606
  87.2 4.6 collective-permute-start.2
  133.3 19.1 %collective-permute-start.3 = (f32[1544,128]{1,0:T(8,128)}, f32[1544,128]{1,0:T(8,128)S(1)}, u32[]{:S(2)}, u32[]{:S(2)}) collective-permute-start(f32[1544,128]{1,0:T(8,128)} %get-tuple-element.293), channel_id=1, source_target_pairs={{126,0},{0,2},{2,4},{4,6},{6,8},{8,10},{10,12},{12,14},{14,16},{16... | collective-permute-start | bytes 2371592 | tf_op jit(solution)/shard_map/while/body/eval_jaxpr/ppermute | solution.py:604
  133.3 14.0 %collective-permute-start.4 = (f32[264,128]{1,0:T(8,128)}, f32[264,128]{1,0:T(8,128)S(1)}, u32[]{:S(2)}, u32[]{:S(2)}) collective-permute-start(f32[264,128]{1,0:T(8,128)} %get-tuple-element.294), channel_id=1, source_target_pairs={{0,1},{1,0},{2,3},{3,2},{4,5},{5,4},{6,7},{7,6},{8,9},{9,8},{10,11... | collective-permute-start | bytes 405512 | tf_op jit(solution)/shard_map/while/body/eval_jaxpr/ppermute | solution.py:606
  146.2 6.2 %collective-permute-start.5 = (f32[264,128]{1,0:T(8,128)}, f32[264,128]{1,0:T(8,128)S(1)}, u32[]{:S(2)}, u32[]{:S(2)}) collective-permute-start(f32[264,128]{1,0:T(8,128)} %get-tuple-element.295), channel_id=1, source_target_pairs={{0,3},{2,5},{4,7},{6,9},{8,11},{10,13},{12,15},{14,17},{16,19},{18... | collective-permute-start | bytes 405512 | tf_op jit(solution)/shard_map/while/body/eval_jaxpr/ppermute | solution.py:605
  153.2 65.3 %copy-start.3 = (f32[6,256,128]{2,1,0:T(8,128)S(1)}, f32[6,256,128]{2,1,0:T(8,128)}, u32[]{:S(2)}) copy-start(f32[6,256,128]{2,1,0:T(8,128)} %get-tuple-element.331.sketch) | copy-start | bytes 2359300 | tf_op jit(solution)/shard_map/while
  194.2 23.5 %collective-permute-start = (f32[1544,128]{1,0:T(8,128)}, f32[1544,128]{1,0:T(8,128)S(1)}, u32[]{:S(2)}, u32[]{:S(2)}) collective-permute-start(f32[1544,128]{1,0:T(8,128)} %get-tuple-element.288), channel_id=1, source_target_pairs={{0,126},{2,0},{4,2},{6,4},{8,6},{10,8},{12,10},{14,12},{16,14},{18... | collective-permute-start | bytes 2371592 | tf_op jit(solution)/shard_map/while/body/eval_jaxpr/ppermute | solution.py:604
  206.5 1.6 collective-permute-start.1
  206.5 4.6 collective-permute-start.2
  208.1 9.6 %copy-start.5 = (f32[264,128]{1,0:T(8,128)}, f32[264,128]{1,0:T(8,128)S(1)}, u32[]{:S(2)}) copy-start(f32[264,128]{1,0:T(8,128)S(1)} %collective-permute-done.1.chip) | copy-start | bytes 405508 | tf_op jit(solution)/shard_map/while
  259.0 17.7 %collective-permute-start.3 = (f32[1544,128]{1,0:T(8,128)}, f32[1544,128]{1,0:T(8,128)S(1)}, u32[]{:S(2)}, u32[]{:S(2)}) collective-permute-start(f32[1544,128]{1,0:T(8,128)} %get-tuple-element.293), channel_id=1, source_target_pairs={{126,0},{0,2},{2,4},{4,6},{6,8},{8,10},{10,12},{12,14},{14,16},{16... | collective-permute-start | bytes 2371592 | tf_op jit(solution)/shard_map/while/body/eval_jaxpr/ppermute | solution.py:604
  259.1 1.6 collective-permute-start.4
  259.2 11.2 %collective-permute-start.5 = (f32[264,128]{1,0:T(8,128)}, f32[264,128]{1,0:T(8,128)S(1)}, u32[]{:S(2)}, u32[]{:S(2)}) collective-permute-start(f32[264,128]{1,0:T(8,128)} %get-tuple-element.295), channel_id=1, source_target_pairs={{0,3},{2,5},{4,7},{6,9},{8,11},{10,13},{12,15},{14,17},{16,19},{18... | collective-permute-start | bytes 405512 | tf_op jit(solution)/shard_map/while/body/eval_jaxpr/ppermute | solution.py:605
  277.7 55.6 %copy-start.3 = (f32[6,256,128]{2,1,0:T(8,128)S(1)}, f32[6,256,128]{2,1,0:T(8,128)}, u32[]{:S(2)}) copy-start(f32[6,256,128]{2,1,0:T(8,128)} %get-tuple-element.331.sketch) | copy-start | bytes 2359300 | tf_op jit(solution)/shard_map/while
  318.6 13.8 %collective-permute-start = (f32[1544,128]{1,0:T(8,128)}, f32[1544,128]{1,0:T(8,128)S(1)}, u32[]{:S(2)}, u32[]{:S(2)}) collective-permute-start(f32[1544,128]{1,0:T(8,128)} %get-tuple-element.288), channel_id=1, source_target_pairs={{0,126},{2,0},{4,2},{6,4},{8,6},{10,8},{12,10},{14,12},{16,14},{18... | collective-permute-start | bytes 2371592 | tf_op jit(solution)/shard_map/while/body/eval_jaxpr/ppermute | solution.py:604
  319.8 1.6 collective-permute-start.1
  320.1 6.1 %collective-permute-start.2 = (f32[264,128]{1,0:T(8,128)}, f32[264,128]{1,0:T(8,128)S(1)}, u32[]{:S(2)}, u32[]{:S(2)}) collective-permute-start(f32[264,128]{1,0:T(8,128)} %get-tuple-element.290), channel_id=1, source_target_pairs={{0,3},{2,5},{4,7},{6,9},{8,11},{10,13},{12,15},{14,17},{16,19},{18... | collective-permute-start | bytes 405512 | tf_op jit(solution)/shard_map/while/body/eval_jaxpr/ppermute | solution.py:605
  321.4 11.0 %copy-start.5 = (f32[264,128]{1,0:T(8,128)}, f32[264,128]{1,0:T(8,128)S(1)}, u32[]{:S(2)}) copy-start(f32[264,128]{1,0:T(8,128)S(1)} %collective-permute-done.1.chip) | copy-start | bytes 405508 | tf_op jit(solution)/shard_map/while
  373.8 17.7 %collective-permute-start.3 = (f32[1544,128]{1,0:T(8,128)}, f32[1544,128]{1,0:T(8,128)S(1)}, u32[]{:S(2)}, u32[]{:S(2)}) collective-permute-start(f32[1544,128]{1,0:T(8,128)} %get-tuple-element.293), channel_id=1, source_target_pairs={{126,0},{0,2},{2,4},{4,6},{6,8},{8,10},{10,12},{12,14},{14,16},{16... | collective-permute-start | bytes 2371592 | tf_op jit(solution)/shard_map/while/body/eval_jaxpr/ppermute | solution.py:604
  373.8 6.4 %collective-permute-start.4 = (f32[264,128]{1,0:T(8,128)}, f32[264,128]{1,0:T(8,128)S(1)}, u32[]{:S(2)}, u32[]{:S(2)}) collective-permute-start(f32[264,128]{1,0:T(8,128)} %get-tuple-element.294), channel_id=1, source_target_pairs={{0,1},{1,0},{2,3},{3,2},{4,5},{5,4},{6,7},{7,6},{8,9},{9,8},{10,11... | collective-permute-start | bytes 405512 | tf_op jit(solution)/shard_map/while/body/eval_jaxpr/ppermute | solution.py:606
  379.1 6.2 %collective-permute-start.5 = (f32[264,128]{1,0:T(8,128)}, f32[264,128]{1,0:T(8,128)S(1)}, u32[]{:S(2)}, u32[]{:S(2)}) collective-permute-start(f32[264,128]{1,0:T(8,128)} %get-tuple-element.295), channel_id=1, source_target_pairs={{0,3},{2,5},{4,7},{6,9},{8,11},{10,13},{12,15},{14,17},{16,19},{18... | collective-permute-start | bytes 405512 | tf_op jit(solution)/shard_map/while/body/eval_jaxpr/ppermute | solution.py:605
  392.4 59.2 %copy-start.3 = (f32[6,256,128]{2,1,0:T(8,128)S(1)}, f32[6,256,128]{2,1,0:T(8,128)}, u32[]{:S(2)}) copy-start(f32[6,256,128]{2,1,0:T(8,128)} %get-tuple-element.331.sketch) | copy-start | bytes 2359300 | tf_op jit(solution)/shard_map/while
  433.3 17.4 %collective-permute-start = (f32[1544,128]{1,0:T(8,128)}, f32[1544,128]{1,0:T(8,128)S(1)}, u32[]{:S(2)}, u32[]{:S(2)}) collective-permute-start(f32[1544,128]{1,0:T(8,128)} %get-tuple-element.288), channel_id=1, source_target_pairs={{0,126},{2,0},{4,2},{6,4},{8,6},{10,8},{12,10},{14,12},{16,14},{18... | collective-permute-start | bytes 2371592 | tf_op jit(solution)/shard_map/while/body/eval_jaxpr/ppermute | solution.py:604
  439.4 1.6 collective-permute-start.1
  439.4 6.1 %collective-permute-start.2 = (f32[264,128]{1,0:T(8,128)}, f32[264,128]{1,0:T(8,128)S(1)}, u32[]{:S(2)}, u32[]{:S(2)}) collective-permute-start(f32[264,128]{1,0:T(8,128)} %get-tuple-element.290), channel_id=1, source_target_pairs={{0,3},{2,5},{4,7},{6,9},{8,11},{10,13},{12,15},{14,17},{16,19},{18... | collective-permute-start | bytes 405512 | tf_op jit(solution)/shard_map/while/body/eval_jaxpr/ppermute | solution.py:605
  441.0 9.8 %copy-start.5 = (f32[264,128]{1,0:T(8,128)}, f32[264,128]{1,0:T(8,128)S(1)}, u32[]{:S(2)}) copy-start(f32[264,128]{1,0:T(8,128)S(1)} %collective-permute-done.1.chip) | copy-start | bytes 405508 | tf_op jit(solution)/shard_map/while
  492.1 17.7 %collective-permute-start.3 = (f32[1544,128]{1,0:T(8,128)}, f32[1544,128]{1,0:T(8,128)S(1)}, u32[]{:S(2)}, u32[]{:S(2)}) collective-permute-start(f32[1544,128]{1,0:T(8,128)} %get-tuple-element.293), channel_id=1, source_target_pairs={{126,0},{0,2},{2,4},{4,6},{6,8},{8,10},{10,12},{12,14},{14,16},{16... | collective-permute-start | bytes 2371592 | tf_op jit(solution)/shard_map/while/body/eval_jaxpr/ppermute | solution.py:604
  492.2 2.8 collective-permute-start.4
  493.8 9.7 %collective-permute-start.5 = (f32[264,128]{1,0:T(8,128)}, f32[264,128]{1,0:T(8,128)S(1)}, u32[]{:S(2)}, u32[]{:S(2)}) collective-permute-start(f32[264,128]{1,0:T(8,128)} %get-tuple-element.295), channel_id=1, source_target_pairs={{0,3},{2,5},{4,7},{6,9},{8,11},{10,13},{12,15},{14,17},{16,19},{18... | collective-permute-start | bytes 405512 | tf_op jit(solution)/shard_map/while/body/eval_jaxpr/ppermute | solution.py:605
  510.7 3.4 collective-permute-start.12
  516.7 1.2 collective-permute-start.13
  518.0 4.7 collective-permute-start.14
  518.0 5.1 collective-permute-start.15
  518.0 6.3 %collective-permute-start.16 = (f32[8,128]{1,0:T(8,128)S(1)}, f32[8,128]{1,0:T(8,128)S(1)}, u32[]{:S(2)}, u32[]{:S(2)}) collective-permute-start(f32[8,128]{1,0:T(8,128)S(1)} %add.51), channel_id=1, source_target_pairs={{0,6},{1,7},{2,4},{3,5},{4,2},{5,3},{6,0},{7,1},{8,14},{9,15},{10,... | collective-permute-start | bytes 12296 | tf_op jit(solution)/shard_map/ppermute | solution.py:543
  524.3 4.7 collective-permute-start.17
  524.3 5.2 collective-permute-start.18
  524.4 6.2 %collective-permute-start.19 = (f32[8,128]{1,0:T(8,128)S(1)}, f32[8,128]{1,0:T(8,128)S(1)}, u32[]{:S(2)}, u32[]{:S(2)}) collective-permute-start(f32[8,128]{1,0:T(8,128)S(1)} %add_add_fusion.2), channel_id=1, source_target_pairs={{0,24},{1,25},{2,26},{3,27},{4,28},{5,29},{6,30},{7,31},{8,16},{9,... | collective-permute-start | bytes 12296 | tf_op jit(solution)/shard_map/ppermute | solution.py:543
  530.6 4.7 collective-permute-start.20
  530.6 5.7 %collective-permute-start.21 = (f32[8,128]{1,0:T(8,128)S(1)}, f32[8,128]{1,0:T(8,128)S(1)}, u32[]{:S(2)}, u32[]{:S(2)}) collective-permute-start(f32[8,128]{1,0:T(8,128)S(1)} %add_add_fusion.1), channel_id=1, source_target_pairs={{0,64},{1,65},{2,66},{3,67},{4,68},{5,69},{6,70},{7,71},{8,72},{9,... | collective-permute-start | bytes 12296 | tf_op jit(solution)/shard_map/ppermute | solution.py:543
  534.6 4.8 collective-permute-start.22
  (15 other events, 32.0 us)

commit v2 on v1

--- a/solution.py
+++ b/solution.py
@@ -56,36 +56,44 @@
     return jnp.broadcast_to(x[m : m + 1, :], x.shape)
 
 
-def eliminate(rows, start, lane, sub):
-    columns = []
-    for m in range(8):
-        hit = lane == start + m
-        columns.append(
+def eliminate(groups, start, lane, sub):
+    columns = [
+        [
             [
                 jnp.broadcast_to(
-                    jnp.sum(jnp.where(hit, r, 0.0), axis=1, keepdims=True), (8, N)
+                    jnp.sum(jnp.where(lane == start + m, r, 0.0), axis=1, keepdims=True),
+                    (8, N),
                 )
                 for r in rows
             ]
-        )
+            for m in range(8)
+        ]
+        for rows in groups
+    ]
     inside = (lane >= start) & (lane < start + 8)
-    out = [jnp.where(inside, jnp.where(lane == start + sub, 1.0, 0.0), rows[0])]
-    out += [jnp.where(inside, 0.0, r) for r in rows[1:]]
-    scale = jnp.ones((8, N), F32)
+    unit = jnp.where(lane == start + sub, 1.0, 0.0)
+    outs = [
+        [jnp.where(inside, unit, rows[0])] + [jnp.where(inside, 0.0, r) for r in rows[1:]]
+        for rows in groups
+    ]
+    scales = [jnp.ones((8, N), F32) for _ in groups]
     for m in range(8):
-        inverse = lax.rsqrt(row_of(columns[m][0], m))
-        lower = [c * inverse for c in columns[m]]
-        lower[0] = jnp.where(sub > m, lower[0], 0.0)
-        for j in range(m + 1, 8):
-            factor = row_of(lower[0], j)
-            for r in range(len(rows)):
-                columns[j][r] = columns[j][r] - lower[r] * factor
-        pivot = row_of(out[0], m) * inverse
-        for r in range(len(rows)):
-            out[r] = out[r] - lower[r] * pivot
-        scale = jnp.where(sub == m, inverse, scale)
-    out[0] = out[0] * scale
-    return out
+        for g, out in enumerate(outs):
+            column = columns[g]
+            inverse = lax.rsqrt(row_of(column[m][0], m))
+            lower = [c * inverse for c in column[m]]
+            lower[0] = jnp.where(sub > m, lower[0], 0.0)
+            for j in range(m + 1, 8):
+                factor = row_of(lower[0], j)
+                for r in range(len(out)):
+                    column[j][r] = column[j][r] - lower[r] * factor
+            pivot = row_of(out[0], m) * inverse
+            for r in range(len(out)):
+                out[r] = out[r] - lower[r] * pivot
+            scales[g] = jnp.where(sub == m, inverse, scales[g])
+    for out, scale in zip(outs, scales):
+        out[0] = out[0] * scale
+    return outs
 
 
 def invert_factors(gram):
@@ -97,22 +105,32 @@
     def body(index, carry):
         start = pl.multiple_of(index * 16, 16)
         inside = (wide >= start) & (wide < start + 16)
+        whole = [gram[k] for k in range(HALF)]
+        rows = [
+            [gram[k, pl.ds(start, 8), :], gram[k, pl.ds(start + 8, 8), :]]
+            for k in range(HALF)
+        ]
+        rows = eliminate(rows, start, lane, sub)
+        seconds = eliminate([[r[1]] for r in rows], start + 8, lane, sub)
+        beyond = (lane >= start + 8) & (lane < start + 16)
+        boths, changes = [], []
         for k in range(HALF):
-            first = gram[k, pl.ds(start, 8), :]
-            second = gram[k, pl.ds(start + 8, 8), :]
-            first, second = eliminate([first, second], start, lane, sub)
-            first = jnp.where((lane >= start + 8) & (lane < start + 16), 0.0, first)
-            (second,) = eliminate([second], start + 8, lane, sub)
-            both = jnp.concatenate([first, second], axis=0)
+            first = jnp.where(beyond, 0.0, rows[k][0])
+            both = jnp.concatenate([first, seconds[k][0]], axis=0)
             z1, z2, z3 = parts(both)
             u1, u2, u3 = parts(jnp.where(pair >= start + 16, both, 0.0))
-            change = dot(
-                jnp.concatenate([u1, u1, u2, u2, u1, u3], 0),
-                jnp.concatenate([z1, z2, z1, z2, z3, z1], 0),
-                TN,
+            changes.append(
+                dot(
+                    jnp.concatenate([u1, u1, u2, u2, u1, u3], 0),
+                    jnp.concatenate([z1, z2, z1, z2, z3, z1], 0),
+                    TN,
+                )
             )
-            gram[k, :, :] = jnp.where(inside, 0.0, gram[k, :, :]) - change
-            gram[k, pl.ds(start, 16), :] = both
+            boths.append(both)
+        for k in range(HALF):
+            gram[k] = jnp.where(inside, 0.0, whole[k]) - changes[k]
+        for k in range(HALF):
+            gram[k, pl.ds(start, 16), :] = boths[k]
         return carry
 
     lax.fori_loop(0, N // 16, body, 0)
@@ -145,8 +163,6 @@
     chip_out,
     cross_out,
     left,
-    left_sums,
-    left_tail,
     right,
     matrix,
     up,
@@ -155,7 +171,6 @@
     gram,
     red,
     bas,
-    sem,
 ):
     core = scal[13]
     left_step = scal[14].astype(jnp.int32)
@@ -166,44 +181,26 @@
     left_kept = jnp.logical_or(first, is_zero if parity == 1 else jnp.logical_not(is_zero))
     left_chip = jnp.logical_or(first, is_zero)
 
+    def place(target, at, source, rows):
+        target[pl.ds(pl.multiple_of(at, BLOCK), rows), :] = source[pl.ds(0, rows), :]
+
     def load(left_from, right_from):
-        move(
-            [
-                (
-                    left_from.at[pl.ds(0, BULK)],
-                    left.at[pl.ds(pl.multiple_of((1 - left_step) * BLOCK, BLOCK), BULK)],
-                ),
-                (left_from.at[pl.ds(BULK, 8)], left_sums),
-                (
-                    right_from.at[pl.ds(0, BULK)],
-                    right.at[pl.ds(pl.multiple_of(right_step * BLOCK, BLOCK), BULK)],
-                ),
-            ],
-            sem,
-        )
+        place(left, (1 - left_step) * BLOCK, left_from, BULK)
+        place(right, right_step * BLOCK, right_from, BULK)
 
     def load_edges(left_from, right_from):
-        move(
-            [
-                (
-                    left_from.at[pl.ds(0, BLOCK)],
-                    left.at[pl.ds(pl.multiple_of(left_step * BULK, BLOCK), BLOCK)],
-                ),
-                (left_from.at[pl.ds(BLOCK, 8)], left_tail),
-                (
-                    right_from.at[pl.ds(0, BLOCK)],
-                    right.at[pl.ds(pl.multiple_of((1 - right_step) * BULK, BLOCK), BLOCK)],
-                ),
-            ],
-            sem,
-        )
+        place(left, left_step * BULK, left_from, BLOCK)
+        place(right, (1 - right_step) * BULK, right_from, BLOCK)
 
     pl.when(left_kept)(lambda: load(keep, recv))
     pl.when(jnp.logical_not(left_kept))(lambda: load(recv, keep))
     pl.when(left_chip)(lambda: load_edges(chip, cross))
     pl.when(jnp.logical_not(left_chip))(lambda: load_edges(cross, chip))
 
-    sums = left_sums[...] + left_tail[...]
+    tail = pl.ds(BULK, 8)
+    edge_tail = pl.ds(BLOCK, 8)
+    sums = jnp.where(left_kept, keep[tail, :], recv[tail, :])
+    sums = sums + jnp.where(left_chip, chip[edge_tail, :], cross[edge_tail, :])
     weight_in = sums[0:1, :]
     total_in = sums[1:2, :]
     alpha = 1.0 / jnp.sqrt(weight_in)
@@ -214,12 +211,11 @@
     )
 
     def finish(weight, total):
-        tail = jnp.where(sub == 0, weight, jnp.where(sub == 1, total, 0.0))
-        red[pl.ds(BULK, 8), :] = tail
-        bas[pl.ds(BULK, 8), :] = tail
-
-    @pl.when(phantom)
-    def _():
+        both = jnp.where(sub == 0, weight, jnp.where(sub == 1, total, 0.0))
+        red[tail, :] = both
+        bas[tail, :] = both
+
+    def relabel():
         for k in range(HALF):
             at = k * BLOCK
             red[pl.ds(at, N), :] = right[pl.ds(at, N), :]
@@ -228,6 +224,9 @@
             bas[pl.ds(at + N, N), :] = left[pl.ds(at + N, N), :] * alpha
         one = jnp.full((1, N), 1.0 - core, F32)
         finish(one, one)
+
+    if parity == 1:
+        pl.when(phantom)(relabel)
 
     @pl.when(jnp.logical_not(phantom))
     def _():
@@ -248,7 +247,7 @@
             down[k] = theta[N:BLOCK, 0:N]
             return carry
 
-        lax.fori_loop(0, HALF, thetas, 0)
+        lax.fori_loop(0, HALF, thetas, 0, unroll=6)
         up[0] = product(
             parts(left[pl.ds(0, N), :]), parts(right[pl.ds(N, N), :]), NN
         )
@@ -275,7 +274,7 @@
             gram[k] = gr + jnp.where(row == col, extra, 0.0)
             return total + squares[:, 0:N] + squares[:, N:BLOCK]
 
-        total = lax.fori_loop(0, HALF, samples, jnp.zeros((1, N), F32))
+        total = lax.fori_loop(0, HALF, samples, jnp.zeros((1, N), F32), unroll=6)
         invert_factors(gram)
 
         def split(k, weight):
@@ -289,7 +288,7 @@
             squares = jnp.sum(reduced * reduced, axis=0, keepdims=True)
             return weight + squares[:, 0:N] + squares[:, N:BLOCK]
 
-        weight = lax.fori_loop(0, HALF, split, jnp.zeros((1, N), F32))
+        weight = lax.fori_loop(0, HALF, split, jnp.zeros((1, N), F32), unroll=6)
         finish(
             jnp.broadcast_to(jnp.sum(weight, axis=1, keepdims=True), (1, N)),
             jnp.broadcast_to(jnp.sum(total, axis=1, keepdims=True), (1, N)),
@@ -300,18 +299,14 @@
     bas_edge_at = pl.multiple_of(left_step * last, BLOCK)
 
     def store(kept, sent):
-        move([(kept, keep_out), (sent, send_out)], sem)
+        keep_out[...] = kept[...]
+        send_out[...] = sent[...]
 
     def store_edges(red_edge, bas_edge):
-        move(
-            [
-                (red.at[pl.ds(red_edge_at, BLOCK)], red_edge.at[pl.ds(0, BLOCK)]),
-                (red.at[pl.ds(BULK, 8)], red_edge.at[pl.ds(BLOCK, 8)]),
-                (bas.at[pl.ds(bas_edge_at, BLOCK)], bas_edge.at[pl.ds(0, BLOCK)]),
-                (bas.at[pl.ds(BULK, 8)], bas_edge.at[pl.ds(BLOCK, 8)]),
-            ],
-            sem,
-        )
+        red_edge[pl.ds(0, BLOCK), :] = red[pl.ds(red_edge_at, BLOCK), :]
+        red_edge[edge_tail, :] = red[tail, :]
+        bas_edge[pl.ds(0, BLOCK), :] = bas[pl.ds(bas_edge_at, BLOCK), :]
+        bas_edge[edge_tail, :] = bas[tail, :]
 
     keeps_red = jnp.logical_not(is_zero) if parity == 1 else is_zero
     pl.when(keeps_red)(lambda: store(red, bas))
@@ -339,12 +334,10 @@
             shape(BLOCK + 8, N),
             shape(BLOCK + 8, N),
         ),
-        in_specs=[SM, SM, VM, HB, HB, HB, HB, VM],
-        out_specs=(VM, HB, HB, HB, HB),
+        in_specs=[SM, SM, VM, VM, VM, VM, VM, VM],
+        out_specs=(VM, VM, VM, VM, VM),
         scratch_shapes=[
             pltpu.VMEM((BLOCK + BULK, N), F32),
-            pltpu.VMEM((8, N), F32),
-            pltpu.VMEM((8, N), F32),
             pltpu.VMEM((BULK + BLOCK, N), F32),
             pltpu.VMEM((HALF, BLOCK, BLOCK), F32),
             pltpu.VMEM((HALF + 1, N, N), F32),
@@ -353,9 +346,8 @@
             pltpu.VMEM((HALF, N, N), F32),
             pltpu.VMEM((BULK + 8, N), F32),
             pltpu.VMEM((BULK + 8, N), F32),
-            pltpu.SemaphoreType.DMA((4,)),
         ],
-        compiler_params=pltpu.CompilerParams(vmem_limit_bytes=56 * 1024 * 1024),
+        compiler_params=pltpu.CompilerParams(vmem_limit_bytes=32 * 1024 * 1024),
         cost_estimate=pl.CostEstimate(
             flops=4 * 10**8, bytes_accessed=4 * 10**6, transcendentals=0
         ),
@@ -465,9 +457,9 @@
     core = lax.rem(pos[0], 2)
 
     def load(source):
-        move([(source.at[pl.ds(core * HALF, HALF)], sketch)], sem)
-
-    pl.when(core == 0)(lambda: load(theirs))
+        move([(source, sketch)], sem)
+
+    pl.when(core == 0)(lambda: load(theirs.at[pl.ds(0, HALF)]))
     pl.when(core == 1)(lambda: load(behind))
     mask_sketch(sketch, odd_scal)
 
@@ -484,18 +476,12 @@
     )(position, odd_scal, theirs, behind)
 
 
-def finish_kernel(pos, meta, acc, recv, swap, out, acc_out, sem):
+def finish_kernel(pos, meta, recv, swap, out, sem):
     position = pos[0]
     core = lax.rem(position, 2)
     step = jnp.where(core == 0, 0.0, meta[THERE, 6]).astype(jnp.int32)
     sums = recv[pl.ds(BULK, 8), :] + swap[pl.ds(BULK, 8), :]
     weight = sums[0:1, :]
-    total = sums[1:2, :]
-    sub = lax.broadcasted_iota(jnp.int32, (8, N), 0)
-    new = jnp.where(
-        sub == 0, 1.0 - weight / total, jnp.where(sub == 1, jnp.log(total), 0.0)
-    )
-    acc_out[...] = jnp.where(core == 0, acc[...] + new, 0.0)
 
     @pl.when(core == 0)
     def _():
@@ -521,16 +507,16 @@
         move(pairs, sem)
 
 
-def finish(position, meta, acc, recv, swap):
+def finish(position, meta, recv, swap):
     return pl.pallas_call(
         finish_kernel,
-        out_shape=(shape(2, NSEC, N, N), shape(8, N)),
-        in_specs=[SM, SM, VM, VM, VM],
-        out_specs=(HB, VM),
+        out_shape=shape(2, NSEC, N, N),
+        in_specs=[SM, SM, VM, VM],
+        out_specs=HB,
         scratch_shapes=[pltpu.SemaphoreType.DMA((4 * HALF,))],
         compiler_params=pltpu.CompilerParams(vmem_limit_bytes=16 * 1024 * 1024),
         name="finish",
-    )(position, meta, acc, recv, swap)
+    )(position, meta, recv, swap)
 
 
 def everywhere(value, chain):
@@ -564,6 +550,8 @@
     apart = [(device(j, 0), device(j - 1, 0)) for j in range(chips)]
     apart += [(device(j, 1), device(j + 1, 1)) for j in range(chips)]
     back = [(target, source) for source, target in apart]
+    slant = [(device(j + 1, 0), device(j, 1)) for j in range(chips)]
+    slant += [(device(j, 1), device(j + 1, 0)) for j in range(chips)]
     ahead = [(device(j, 1), device(j + 1, 1)) for j in range(chips)]
 
     row = jnp.concatenate(
@@ -577,22 +565,20 @@
     )
     partner = lax.ppermute(row, "site", swap)
     along = lax.ppermute(row, "site", apart)
-    across = lax.ppermute(along, "site", swap)
-    after = jnp.where(core == 0, along, across)
-    before = jnp.where(core == 0, across, along)
+    across = lax.ppermute(row, "site", slant)
     meta = jnp.stack(
         [
             jnp.where(core == 0, row, partner),
             jnp.where(core == 0, partner, row),
-            after,
-            before,
+            jnp.where(core == 0, along, across),
+            jnp.where(core == 0, across, along),
         ]
     )
     site = sites[0]
     sketch = sketches[0]
     other = lax.ppermute(site, "site", swap)
     theirs = lax.ppermute(sketch, "site", swap)
-    later, meta = lax.optimization_barrier((sketch, meta))
+    later, meta = lax.optimization_barrier((sketch[HALF:], meta))
     behind = lax.ppermute(later, "site", ahead)
     scal, odd_scal, left, right, chip, cross, even = start(
         position, meta, site, other, sketch, theirs
@@ -606,18 +592,29 @@
         chip = lax.ppermute(chip, "site", swap)
         return acc, keep, recv, chip, cross
 
-    def step(index, carry):
-        first = jnp.where(index == 0, 1, 0).astype(jnp.int32)[None]
-        none = jnp.zeros((1,), jnp.int32)
-        carry = spread(sweep(0, first, scal, *carry, even), apart)
-        return spread(sweep(1, none, scal_odd, *carry, odd), back)
-
-    scal_odd = odd_scal
+    none = jnp.zeros((1,), jnp.int32)
+
+    def even_sweep(first, carry):
+        return spread(sweep(0, first, scal, *carry, even), apart)
+
+    def odd_sweep(carry):
+        return spread(sweep(1, none, odd_scal, *carry, odd), back)
+
     carry = (jnp.zeros((8, N), F32), left, right, chip, cross)
-    acc, keep, recv, chip, cross = lax.fori_loop(0, STEPS, step, carry)
+    carry = even_sweep(none + 1, carry)
+    carry = lax.fori_loop(
+        0, STEPS - 1, lambda _, carry: even_sweep(none, odd_sweep(carry)), carry
+    )
+    acc, keep, send, chip, cross = sweep(1, none, odd_scal, *carry, odd)
+    tail = keep[BULK:]
+    met = tail + lax.ppermute(tail, "site", over)
+    weight, total = met[0:1], met[1:2]
+    last = jnp.concatenate([1.0 - weight / total, jnp.log(total), met[2:]], axis=0)
+    acc = jnp.where(core == 0, acc + last, 0.0)
+    totals = everywhere(acc, chain)[0:2, 0]
+    recv = lax.ppermute(send, "site", back)
     swapped = lax.ppermute(keep, "site", swap)
-    out, acc = finish(position, meta, acc, recv, swapped)
-    totals = everywhere(acc, chain)[0:2, 0]
+    out = finish(position, meta, recv, swapped)
     return (out[None], totals)
 
 

time: 541 us -> 288 us (0.53)
  Pallas kernels: 334 us -> 114 us
  starting transfers between devices: 85.3 us -> 60.5 us
  local copies, waits for them, and re-layouts: 11.3 us -> 4.86 us
    pallas_call x8, Pallas kernels: 326 us -> 107 us  [sweep(): pl.pallas_call(functools.partial(sweep_kernel, parity), out_shape=(shape(...]
    ppermute x8 -> x7, starting transfers between devices: 34.5 us -> 14.5 us  [spread(): chip = lax.ppermute(chip, 'site', swap)]
    ppermute x8 -> x7, waiting for transfers between devices: 44 us -> 34.8 us  [spread(): cross = lax.ppermute(cross, 'site', over)]
    ppermute x8 -> x7, starting transfers between devices: 24.1 us -> 16.8 us  [spread(): recv = lax.ppermute(send, 'site', moves)]
    while x40 -> x6, local copies, waits for them, and re-layouts: 7.17 us -> 0.01 us
    ppermute x1 -> x3, waiting for transfers between devices: 4.69 us -> 10.5 us  [the longest x1 7.47 us: body(): across = lax.ppermute(row, 'site', slant)]
    ppermute x8 -> x7, waiting for transfers between devices: 36.9 us -> 40.5 us  [spread(): recv = lax.ppermute(send, 'site', moves)]
  transfers between devices with their start and end apart: 41 -> 40, of which waited for: 32 -> 28; matrix products, arithmetic and copies ran while one was open for 0% -> 1% of each run, Pallas kernels for 1% -> 0%
where the time goes in v2:
time: 288 us
  Pallas kernels  114 us (40%)
  waiting for transfers between devices  105 us (36%)
  starting transfers between devices  60.5 us (21%)
  local copies, waits for them, and re-layouts  4.86 us (2%)
    pallas_call x8, Pallas kernels, sweep(): pl.pallas_call(functools.partial(sweep_kernel, parity), out_shape=(shape(...  107 us
    ppermute x7, waiting for transfers between devices, spread(): recv = lax.ppermute(send, 'site', moves)  40.5 us
    ppermute x7, waiting for transfers between devices, spread(): cross = lax.ppermute(cross, 'site', over)  34.8 us
    ppermute x7, starting transfers between devices, spread(): recv = lax.ppermute(send, 'site', moves)  16.8 us
    ppermute x10, starting transfers between devices, everywhere(): terms.append(lax.ppermute(value, 'site', moves))  15.2 us
    ppermute x7, starting transfers between devices, spread(): chip = lax.ppermute(chip, 'site', swap)  14.5 us
    ppermute x10, waiting for transfers between devices, everywhere(): terms.append(lax.ppermute(value, 'site', moves))  13.6 us
    ppermute x1, starting transfers between devices, body(): along = lax.ppermute(row, 'site', apart)  8.8 us
  transfers between devices with their start and end apart: 40, of which 28 were waited for; matrix products, arithmetic and copies ran while one was open for 1% of the time, Pallas kernels for 0%

profile of v2, /device:TPU:0, one launch (start us, length us, event | category | flops | bytes accessed | tf_op | source)
XLA Modules:
  0.0 287.6 jit_solution(12620838696008208821)
XLA Ops:
  3.3 8.8 %collective-permute-start.7 = (f32[32]{0:T(128)S(1)}, f32[32]{0:T(128)S(1)}, u32[]{:S(2)}, u32[]{:S(2)}) collective-permute-start(f32[32]{0:T(128)S(1)} %concatenate.6), channel_id=1, source_target_pairs={{0,126},{2,0},{4,2},{6,4},{8,6},{10,8},{12,10},{14,12},{16,14},{18... | collective-permute-start | bytes 392 | tf_op jit(solution)/shard_map/ppermute | solution.py:567
  12.2 2.1 slice_bitcast_fusion
  15.2 7.5 %collective-permute-done.8 = f32[32]{0:T(128)S(1)} collective-permute-done((f32[32]{0:T(128)S(1)}, f32[32]{0:T(128)S(1)}, u32[]{:S(2)}, u32[]{:S(2)}) %collective-permute-start.8) | collective-permute-done | bytes 160 | tf_op jit(solution)/shard_map/ppermute | solution.py:568
  22.7 1.4 copy-done.1
  24.1 4.1 %start.1 = (f32[16]{0:T(128)S(1)}, f32[16]{0:T(128)S(1)}, f32[1544,128]{1,0:T(8,128)S(1)}, f32[1544,128]{1,0:T(8,128)S(1)}, f32[264,128]{1,0:T(8,128)S(1)}, /*in...) custom-call(s32[2]{0:T(128)S(1)} %pad_add_fusion.pos, f32[4,32]{1,0:T(4,128)S(1)} %pad_maximum_fusion.meta, ...), custom_call_target="tpu_custom_call" | custom-call | tf_op jit(solution)/shard_map/start/pallas_call | solution.py:437
  28.3 13.4 %sweep.4 = (f32[8,128]{1,0:T(8,128)S(1)}, f32[1544,128]{1,0:T(8,128)}, f32[1544,128]{1,0:T(8,128)S(1)}, f32[264,128]{1,0:T(8,128)S(1)}, f32[264,128]{1,0:T(8,128)S(1)}) custom-call(s32[1]{0:T(128)} %constant.34.clone.1.first_ref, f32[16]{0:T(128)S(1)} %get-tuple-element.224.scal, f32[8,128]{1,0:T(8,128)S(1)} %broadcast_in_dim.8.acc_in, ...), custom_call_target="tpu_custom_call" | custom-call | flops 400000000 | bytes 4000000 | tf_op jit(solution)/shard_map/sweep/pallas_call | solution.py:328
  42.4 2.1 collective-permute-start.13
  45.3 3.4 %collective-permute-done.13 = f32[264,128]{1,0:T(8,128)S(1)} collective-permute-done((f32[264,128]{1,0:T(8,128)S(1)}, f32[264,128]{1,0:T(8,128)S(1)}, u32[]{:S(2)}, u32[]{:S(2)}) %collective-permute-start.13) | collective-permute-done | bytes 135200 | tf_op jit(solution)/shard_map/ppermute | solution.py:591
  48.7 6.5 %collective-permute-done.11 = f32[1544,128]{1,0:T(8,128)} collective-permute-done((f32[1544,128]{1,0:T(8,128)S(1)}, f32[1544,128]{1,0:T(8,128)}, u32[]{:S(2)}, u32[]{:S(2)}) %collective-permute-start.11) | collective-permute-done | bytes 790560 | tf_op jit(solution)/shard_map/ppermute | solution.py:590
  55.2 183.7 %while.18 = (s32[]{:T(128)}, f32[8,128]{1,0:T(8,128)S(1)}, f32[1544,128]{1,0:T(8,128)}, f32[1544,128]{1,0:T(8,128)}, f32[264,128]{1,0:T(8,128)S(1)}, /*index=5*/...) while((s32[]{:T(128)}, f32[8,128]{1,0:T(8,128)S(1)}, ...), condition=%wide.region_1.2_spmd, body=%wide.region_0.1_spmd.sunk | while | flops 800000000 | bytes 19633024 | solution.py:605
  55.2 13.4 %sweep.6 = (f32[8,128]{1,0:T(8,128)S(1)}, f32[1544,128]{1,0:T(8,128)S(1)}, f32[1544,128]{1,0:T(8,128)S(1)}, f32[264,128]{1,0:T(8,128)S(1)}, f32[264,128]{1,0:T(8,128)S(1)}) custom-call(s32[1]{0:T(128)} %get-tuple-element.251.first_ref, f32[16]{0:T(128)S(1)} %get-tuple-element.246.scal, f32[8,128]{1,0:T(8,128)S(1)} %get-tuple-element.229.acc_in, ...), custom_call_target="tpu_custom_call" | custom-call | flops 400000000 | bytes 4000000 | tf_op jit(solution)/shard_map/while/body/eval_jaxpr/sweep/pallas_call | solution.py:328
  68.7 9.0 %collective-permute-start.1 = (f32[264,128]{1,0:T(8,128)S(1)}, f32[264,128]{1,0:T(8,128)S(1)}, u32[]{:S(2)}, u32[]{:S(2)}) collective-permute-start(f32[264,128]{1,0:T(8,128)S(1)} %get-tuple-element.209), channel_id=1, source_target_pairs={{0,1},{1,0},{2,3},{3,2},{4,5},{5,4},{6,7},{7,6},{8,9},{9,8},{10,11... | collective-permute-start | bytes 405512 | tf_op jit(solution)/shard_map/while/body/eval_jaxpr/ppermute | solution.py:592
  78.7 4.1 %collective-permute-done.2.cross = f32[264,128]{1,0:T(8,128)S(1)} collective-permute-done((f32[264,128]{1,0:T(8,128)S(1)}, f32[264,128]{1,0:T(8,128)S(1)}, u32[]{:S(2)}, u32[]{:S(2)}) %collective-permute-start.2) | collective-permute-done | bytes 135200 | tf_op jit(solution)/shard_map/while/body/eval_jaxpr/ppermute | solution.py:591
  82.8 3.4 %collective-permute-done.recv = f32[1544,128]{1,0:T(8,128)S(1)} collective-permute-done((f32[1544,128]{1,0:T(8,128)S(1)}, f32[1544,128]{1,0:T(8,128)S(1)}, u32[]{:S(2)}, u32[]{:S(2)}) %collective-permute-start) | collective-permute-done | bytes 790560 | tf_op jit(solution)/shard_map/while/body/eval_jaxpr/ppermute | solution.py:590
  86.1 13.3 %sweep.7 = (f32[8,128]{1,0:T(8,128)S(1)}, f32[1544,128]{1,0:T(8,128)}, f32[1544,128]{1,0:T(8,128)S(1)}, f32[264,128]{1,0:T(8,128)S(1)}, f32[264,128]{1,0:T(8,128)S(1)}) custom-call(s32[1]{0:T(128)} %get-tuple-element.251.first_ref, f32[16]{0:T(128)S(1)} %get-tuple-element.248.scal, f32[8,128]{1,0:T(8,128)S(1)} %get-tuple-element.206.acc_in, ...), custom_call_target="tpu_custom_call" | custom-call | flops 400000000 | bytes 4000000 | tf_op jit(solution)/shard_map/while/body/eval_jaxpr/sweep/pallas_call | solution.py:328
  99.5 9.8 %collective-permute-start.3 = (f32[1544,128]{1,0:T(8,128)S(1)}, f32[1544,128]{1,0:T(8,128)}, u32[]{:S(2)}, u32[]{:S(2)}) collective-permute-start(f32[1544,128]{1,0:T(8,128)S(1)} %get-tuple-element.213), channel_id=1, source_target_pairs={{0,126},{2,0},{4,2},{6,4},{8,6},{10,8},{12,10},{14,12},{16,14},{18... | collective-permute-start | bytes 2371592 | tf_op jit(solution)/shard_map/while/body/eval_jaxpr/ppermute | solution.py:590
  109.2 1.3 collective-permute-done.4
  110.6 3.1 %collective-permute-done.5 = f32[264,128]{1,0:T(8,128)S(1)} collective-permute-done((f32[264,128]{1,0:T(8,128)S(1)}, f32[264,128]{1,0:T(8,128)S(1)}, u32[]{:S(2)}, u32[]{:S(2)}) %collective-permute-start.5) | collective-permute-done | bytes 135200 | tf_op jit(solution)/shard_map/while/body/eval_jaxpr/ppermute | solution.py:591
  113.7 6.4 %collective-permute-done.3 = f32[1544,128]{1,0:T(8,128)} collective-permute-done((f32[1544,128]{1,0:T(8,128)S(1)}, f32[1544,128]{1,0:T(8,128)}, u32[]{:S(2)}, u32[]{:S(2)}) %collective-permute-start.3) | collective-permute-done | bytes 790560 | tf_op jit(solution)/shard_map/while/body/eval_jaxpr/ppermute | solution.py:590
  120.1 13.4 %sweep.6 = (f32[8,128]{1,0:T(8,128)S(1)}, f32[1544,128]{1,0:T(8,128)S(1)}, f32[1544,128]{1,0:T(8,128)S(1)}, f32[264,128]{1,0:T(8,128)S(1)}, f32[264,128]{1,0:T(8,128)S(1)}) custom-call(s32[1]{0:T(128)} %get-tuple-element.251.first_ref, f32[16]{0:T(128)S(1)} %get-tuple-element.246.scal, f32[8,128]{1,0:T(8,128)S(1)} %get-tuple-element.229.acc_in, ...), custom_call_target="tpu_custom_call" | custom-call | flops 400000000 | bytes 4000000 | tf_op jit(solution)/shard_map/while/body/eval_jaxpr/sweep/pallas_call | solution.py:328
  133.7 1.2 collective-permute-done.1.chip
  134.9 9.6 %collective-permute-done.2.cross = f32[264,128]{1,0:T(8,128)S(1)} collective-permute-done((f32[264,128]{1,0:T(8,128)S(1)}, f32[264,128]{1,0:T(8,128)S(1)}, u32[]{:S(2)}, u32[]{:S(2)}) %collective-permute-start.2) | collective-permute-done | bytes 135200 | tf_op jit(solution)/shard_map/while/body/eval_jaxpr/ppermute | solution.py:591
  144.5 6.5 %collective-permute-done.recv = f32[1544,128]{1,0:T(8,128)S(1)} collective-permute-done((f32[1544,128]{1,0:T(8,128)S(1)}, f32[1544,128]{1,0:T(8,128)S(1)}, u32[]{:S(2)}, u32[]{:S(2)}) %collective-permute-start) | collective-permute-done | bytes 790560 | tf_op jit(solution)/shard_map/while/body/eval_jaxpr/ppermute | solution.py:590
  151.0 13.3 %sweep.7 = (f32[8,128]{1,0:T(8,128)S(1)}, f32[1544,128]{1,0:T(8,128)}, f32[1544,128]{1,0:T(8,128)S(1)}, f32[264,128]{1,0:T(8,128)S(1)}, f32[264,128]{1,0:T(8,128)S(1)}) custom-call(s32[1]{0:T(128)} %get-tuple-element.251.first_ref, f32[16]{0:T(128)S(1)} %get-tuple-element.248.scal, f32[8,128]{1,0:T(8,128)S(1)} %get-tuple-element.206.acc_in, ...), custom_call_target="tpu_custom_call" | custom-call | flops 400000000 | bytes 4000000 | tf_op jit(solution)/shard_map/while/body/eval_jaxpr/sweep/pallas_call | solution.py:328
  166.6 4.9 %collective-permute-done.5 = f32[264,128]{1,0:T(8,128)S(1)} collective-permute-done((f32[264,128]{1,0:T(8,128)S(1)}, f32[264,128]{1,0:T(8,128)S(1)}, u32[]{:S(2)}, u32[]{:S(2)}) %collective-permute-start.5) | collective-permute-done | bytes 135200 | tf_op jit(solution)/shard_map/while/body/eval_jaxpr/ppermute | solution.py:591
  171.5 6.4 %collective-permute-done.3 = f32[1544,128]{1,0:T(8,128)} collective-permute-done((f32[1544,128]{1,0:T(8,128)S(1)}, f32[1544,128]{1,0:T(8,128)}, u32[]{:S(2)}, u32[]{:S(2)}) %collective-permute-start.3) | collective-permute-done | bytes 790560 | tf_op jit(solution)/shard_map/while/body/eval_jaxpr/ppermute | solution.py:590
  177.9 13.4 %sweep.6 = (f32[8,128]{1,0:T(8,128)S(1)}, f32[1544,128]{1,0:T(8,128)S(1)}, f32[1544,128]{1,0:T(8,128)S(1)}, f32[264,128]{1,0:T(8,128)S(1)}, f32[264,128]{1,0:T(8,128)S(1)}) custom-call(s32[1]{0:T(128)} %get-tuple-element.251.first_ref, f32[16]{0:T(128)S(1)} %get-tuple-element.246.scal, f32[8,128]{1,0:T(8,128)S(1)} %get-tuple-element.229.acc_in, ...), custom_call_target="tpu_custom_call" | custom-call | flops 400000000 | bytes 4000000 | tf_op jit(solution)/shard_map/while/body/eval_jaxpr/sweep/pallas_call | solution.py:328
  191.3 5.0 %collective-permute-start.1 = (f32[264,128]{1,0:T(8,128)S(1)}, f32[264,128]{1,0:T(8,128)S(1)}, u32[]{:S(2)}, u32[]{:S(2)}) collective-permute-start(f32[264,128]{1,0:T(8,128)S(1)} %get-tuple-element.209), channel_id=1, source_target_pairs={{0,1},{1,0},{2,3},{3,2},{4,5},{5,4},{6,7},{7,6},{8,9},{9,8},{10,11... | collective-permute-start | bytes 405512 | tf_op jit(solution)/shard_map/while/body/eval_jaxpr/ppermute | solution.py:592
  197.3 5.2 %collective-permute-done.2.cross = f32[264,128]{1,0:T(8,128)S(1)} collective-permute-done((f32[264,128]{1,0:T(8,128)S(1)}, f32[264,128]{1,0:T(8,128)S(1)}, u32[]{:S(2)}, u32[]{:S(2)}) %collective-permute-start.2) | collective-permute-done | bytes 135200 | tf_op jit(solution)/shard_map/while/body/eval_jaxpr/ppermute | solution.py:591
  202.5 6.2 %collective-permute-done.recv = f32[1544,128]{1,0:T(8,128)S(1)} collective-permute-done((f32[1544,128]{1,0:T(8,128)S(1)}, f32[1544,128]{1,0:T(8,128)S(1)}, u32[]{:S(2)}, u32[]{:S(2)}) %collective-permute-start) | collective-permute-done | bytes 790560 | tf_op jit(solution)/shard_map/while/body/eval_jaxpr/ppermute | solution.py:590
  208.8 13.3 %sweep.7 = (f32[8,128]{1,0:T(8,128)S(1)}, f32[1544,128]{1,0:T(8,128)}, f32[1544,128]{1,0:T(8,128)S(1)}, f32[264,128]{1,0:T(8,128)S(1)}, f32[264,128]{1,0:T(8,128)S(1)}) custom-call(s32[1]{0:T(128)} %get-tuple-element.251.first_ref, f32[16]{0:T(128)S(1)} %get-tuple-element.248.scal, f32[8,128]{1,0:T(8,128)S(1)} %get-tuple-element.206.acc_in, ...), custom_call_target="tpu_custom_call" | custom-call | flops 400000000 | bytes 4000000 | tf_op jit(solution)/shard_map/while/body/eval_jaxpr/sweep/pallas_call | solution.py:328
  222.1 5.8 %collective-permute-start.3 = (f32[1544,128]{1,0:T(8,128)S(1)}, f32[1544,128]{1,0:T(8,128)}, u32[]{:S(2)}, u32[]{:S(2)}) collective-permute-start(f32[1544,128]{1,0:T(8,128)S(1)} %get-tuple-element.213), channel_id=1, source_target_pairs={{0,126},{2,0},{4,2},{6,4},{8,6},{10,8},{12,10},{14,12},{16,14},{18... | collective-permute-start | bytes 2371592 | tf_op jit(solution)/shard_map/while/body/eval_jaxpr/ppermute | solution.py:590
  227.9 1.3 collective-permute-done.4
  229.2 4.5 %collective-permute-done.5 = f32[264,128]{1,0:T(8,128)S(1)} collective-permute-done((f32[264,128]{1,0:T(8,128)S(1)}, f32[264,128]{1,0:T(8,128)S(1)}, u32[]{:S(2)}, u32[]{:S(2)}) %collective-permute-start.5) | collective-permute-done | bytes 135200 | tf_op jit(solution)/shard_map/while/body/eval_jaxpr/ppermute | solution.py:591
  233.8 5.1 %collective-permute-done.3 = f32[1544,128]{1,0:T(8,128)} collective-permute-done((f32[1544,128]{1,0:T(8,128)S(1)}, f32[1544,128]{1,0:T(8,128)}, u32[]{:S(2)}, u32[]{:S(2)}) %collective-permute-start.3) | collective-permute-done | bytes 790560 | tf_op jit(solution)/shard_map/while/body/eval_jaxpr/ppermute | solution.py:590
  238.9 14.0 %sweep.5 = (f32[8,128]{1,0:T(8,128)S(1)}, f32[1544,128]{1,0:T(8,128)S(1)}, f32[1544,128]{1,0:T(8,128)S(1)}, f32[264,128]{1,0:T(8,128)}, f32[264,128]{1,0:T(8,128)}) custom-call(s32[1]{0:T(128)} %constant.33.clone.1.first_ref, f32[16]{0:T(128)S(1)} %get-tuple-element.278, f32[8,128]{1,0:T(8,128)S(1)} %get-tuple-element.99.acc_in, ...), custom_call_target="tpu_custom_call" | custom-call | flops 400000000 | bytes 4000000 | tf_op jit(solution)/shard_map/sweep/pallas_call | solution.py:328
  252.9 3.0 %collective-permute-done.17 = f32[8,128]{1,0:T(8,128)S(1)} collective-permute-done((f32[8,128]{1,0:T(8,128)S(1)}, f32[8,128]{1,0:T(8,128)S(1)}, u32[]{:S(2)}, u32[]{:S(2)}) %collective-permute-start.17) | collective-permute-done | bytes 4128 | tf_op jit(solution)/shard_map/ppermute | solution.py:610
  256.1 1.2 collective-permute-done.18
  257.3 4.6 %collective-permute-start.21 = (f32[8,128]{1,0:T(8,128)S(1)}, f32[8,128]{1,0:T(8,128)S(1)}, u32[]{:S(2)}, u32[]{:S(2)}) collective-permute-start(f32[8,128]{1,0:T(8,128)S(1)} %add.46), channel_id=1, source_target_pairs={{0,6},{1,7},{2,4},{3,5},{4,2},{5,3},{6,0},{7,1},{8,14},{9,15},{10,... | collective-permute-start | bytes 12296 | tf_op jit(solution)/shard_map/ppermute | solution.py:529
  262.4 1.1 collective-permute-done.21
  263.5 5.6 %collective-permute-start.23 = (f32[8,128]{1,0:T(8,128)S(1)}, f32[8,128]{1,0:T(8,128)S(1)}, u32[]{:S(2)}, u32[]{:S(2)}) collective-permute-start(f32[8,128]{1,0:T(8,128)S(1)} %add_add_fusion.2), channel_id=1, source_target_pairs={{0,16},{1,17},{2,18},{3,19},{4,20},{5,21},{6,22},{7,23},{8,24},{9,... | collective-permute-start | bytes 12296 | tf_op jit(solution)/shard_map/ppermute | solution.py:529
  269.1 7.6 %collective-permute-done.23 = f32[8,128]{1,0:T(8,128)S(1)} collective-permute-done((f32[8,128]{1,0:T(8,128)S(1)}, f32[8,128]{1,0:T(8,128)S(1)}, u32[]{:S(2)}, u32[]{:S(2)}) %collective-permute-start.23) | collective-permute-done | bytes 4128 | tf_op jit(solution)/shard_map/ppermute | solution.py:529
  276.7 1.6 collective-permute-start.25
  278.3 1.7 collective-permute-start.26
  280.0 1.5 collective-permute-start.27
  281.5 1.9 collective-permute-done.26
  283.4 1.4 collective-permute-done.27
  285.5 2.0 finish.1
  (76 shorter events, 10.6 us)
Async XLA Ops:
  0.6 22.1 %copy-start = (f32[1,12,256,128]{3,2,1,0:T(8,128)S(1)}, f32[1,12,256,128]{3,2,1,0:T(8,128)}, u32[]{:S(2)}) copy-start(f32[1,12,256,128]{3,2,1,0:T(8,128)} %param.13) | copy-start | bytes 4718596
  0.6 22.0 %collective-permute-start.10 = (f32[12,256,128]{2,1,0:T(8,128)}, f32[12,256,128]{2,1,0:T(8,128)S(1)}, u32[]{:S(2)}, u32[]{:S(2)}) collective-permute-start(f32[12,256,128]{2,1,0:T(8,128)} %bitcast.19), channel_id=1, source_target_pairs={{0,1},{1,0},{2,3},{3,2},{4,5},{5,4},{6,7},{7,6},{8,9},{9,8},{10,11... | collective-permute-start | bytes 4718600 | tf_op jit(solution)/shard_map/ppermute | solution.py:580
  0.7 21.9 %collective-permute-start.9 = (f32[2,12,128,128]{3,2,1,0:T(8,128)}, f32[2,12,128,128]{3,2,1,0:T(8,128)}, u32[]{:S(2)}, u32[]{:S(2)}) collective-permute-start(f32[2,12,128,128]{3,2,1,0:T(8,128)} %bitcast.21), channel_id=1, source_target_pairs={{0,1},{1,0},{2,3},{3,2},{4,5},{5,4},{6,7},{7,6},{8,9},{9,8},{10,11... | collective-permute-start | bytes 4718600 | tf_op jit(solution)/shard_map/ppermute | solution.py:579
  3.3 11.9 %collective-permute-start.7 = (f32[32]{0:T(128)S(1)}, f32[32]{0:T(128)S(1)}, u32[]{:S(2)}, u32[]{:S(2)}) collective-permute-start(f32[32]{0:T(128)S(1)} %concatenate.6), channel_id=1, source_target_pairs={{0,126},{2,0},{4,2},{6,4},{8,6},{10,8},{12,10},{14,12},{16,14},{18... | collective-permute-start | bytes 392 | tf_op jit(solution)/shard_map/ppermute | solution.py:567
  12.1 3.1 %collective-permute-start.6 = (f32[32]{0:T(128)S(1)}, f32[32]{0:T(128)S(1)}, u32[]{:S(2)}, u32[]{:S(2)}) collective-permute-start(f32[32]{0:T(128)S(1)} %concatenate.6), channel_id=1, source_target_pairs={{0,1},{1,0},{2,3},{3,2},{4,5},{5,4},{6,7},{7,6},{8,9},{9,8},{10,11... | collective-permute-start | bytes 392 | tf_op jit(solution)/shard_map/ppermute | solution.py:566
  14.2 8.4 %collective-permute-start.8 = (f32[32]{0:T(128)S(1)}, f32[32]{0:T(128)S(1)}, u32[]{:S(2)}, u32[]{:S(2)}) collective-permute-start(f32[32]{0:T(128)S(1)} %concatenate.6), channel_id=1, source_target_pairs={{2,1},{4,3},{6,5},{8,7},{10,9},{12,11},{14,13},{16,15},{18,17},{20... | collective-permute-start | bytes 392 | tf_op jit(solution)/shard_map/ppermute | solution.py:568
  22.7 1.4 copy-start.1
  28.2 17.0 %copy-start.2 = (f32[6,256,128]{2,1,0:T(8,128)}, f32[6,256,128]{2,1,0:T(8,128)S(1)}, u32[]{:S(2)}) copy-start(f32[6,256,128]{2,1,0:T(8,128)S(1)} %get-tuple-element.225.sketch) | copy-start | bytes 2359300
  28.2 13.4 %copy-start.4 = (f32[6,256,128]{2,1,0:T(8,128)S(1)}, f32[6,256,128]{2,1,0:T(8,128)}, u32[]{:S(2)}) copy-start(f32[6,256,128]{2,1,0:T(8,128)} %slice_bitcast_fusion) | copy-start | bytes 2359300
  41.6 13.6 %collective-permute-start.11 = (f32[1544,128]{1,0:T(8,128)S(1)}, f32[1544,128]{1,0:T(8,128)}, u32[]{:S(2)}, u32[]{:S(2)}) collective-permute-start(f32[1544,128]{1,0:T(8,128)S(1)} %get-tuple-element.95), channel_id=1, source_target_pairs={{0,126},{2,0},{4,2},{6,4},{8,6},{10,8},{12,10},{14,12},{16,14},{18... | collective-permute-start | bytes 2371592 | tf_op jit(solution)/shard_map/ppermute | solution.py:590
  41.6 2.9 %collective-permute-start.14 = (f32[6,256,128]{2,1,0:T(8,128)S(1)}, f32[6,256,128]{2,1,0:T(8,128)S(1)}, u32[]{:S(2)}, u32[]{:S(2)}) collective-permute-start(f32[6,256,128]{2,1,0:T(8,128)S(1)} %copy-done.4), channel_id=1, source_target_pairs={{1,3},{3,5},{5,7},{7,9},{9,11},{11,13},{13,15},{15,17},{17,19},{19... | collective-permute-start | bytes 2359304 | tf_op jit(solution)/shard_map/ppermute | solution.py:582
  42.3 2.9 %collective-permute-start.12 = (f32[264,128]{1,0:T(8,128)S(1)}, f32[264,128]{1,0:T(8,128)S(1)}, u32[]{:S(2)}, u32[]{:S(2)}) collective-permute-start(f32[264,128]{1,0:T(8,128)S(1)} %get-tuple-element.96), channel_id=1, source_target_pairs={{0,1},{1,0},{2,3},{3,2},{4,5},{5,4},{6,7},{7,6},{8,9},{9,8},{10,11... | collective-permute-start | bytes 405512 | tf_op jit(solution)/shard_map/ppermute | solution.py:592
  42.4 6.3 %collective-permute-start.13 = (f32[264,128]{1,0:T(8,128)S(1)}, f32[264,128]{1,0:T(8,128)S(1)}, u32[]{:S(2)}, u32[]{:S(2)}) collective-permute-start(f32[264,128]{1,0:T(8,128)S(1)} %get-tuple-element.97), channel_id=1, source_target_pairs={{0,3},{2,5},{4,7},{6,9},{8,11},{10,13},{12,15},{14,17},{16,19},{18... | collective-permute-start | bytes 405512 | tf_op jit(solution)/shard_map/ppermute | solution.py:591
  55.2 30.9 %copy-start.3 = (f32[6,256,128]{2,1,0:T(8,128)S(1)}, f32[6,256,128]{2,1,0:T(8,128)}, u32[]{:S(2)}) copy-start(f32[6,256,128]{2,1,0:T(8,128)} %get-tuple-element.249.sketch) | copy-start | bytes 2359300 | tf_op jit(solution)/shard_map/while
  68.6 17.5 %collective-permute-start = (f32[1544,128]{1,0:T(8,128)S(1)}, f32[1544,128]{1,0:T(8,128)S(1)}, u32[]{:S(2)}, u32[]{:S(2)}) collective-permute-start(f32[1544,128]{1,0:T(8,128)S(1)} %get-tuple-element.208), channel_id=1, source_target_pairs={{126,0},{0,2},{2,4},{4,6},{6,8},{8,10},{10,12},{12,14},{14,16},{16... | collective-permute-start | bytes 2371592 | tf_op jit(solution)/shard_map/while/body/eval_jaxpr/ppermute | solution.py:590
  68.7 10.0 %collective-permute-start.1 = (f32[264,128]{1,0:T(8,128)S(1)}, f32[264,128]{1,0:T(8,128)S(1)}, u32[]{:S(2)}, u32[]{:S(2)}) collective-permute-start(f32[264,128]{1,0:T(8,128)S(1)} %get-tuple-element.209), channel_id=1, source_target_pairs={{0,1},{1,0},{2,3},{3,2},{4,5},{5,4},{6,7},{7,6},{8,9},{9,8},{10,11... | collective-permute-start | bytes 405512 | tf_op jit(solution)/shard_map/while/body/eval_jaxpr/ppermute | solution.py:592
  77.7 5.1 %collective-permute-start.2 = (f32[264,128]{1,0:T(8,128)S(1)}, f32[264,128]{1,0:T(8,128)S(1)}, u32[]{:S(2)}, u32[]{:S(2)}) collective-permute-start(f32[264,128]{1,0:T(8,128)S(1)} %get-tuple-element.210), channel_id=1, source_target_pairs={{0,3},{2,5},{4,7},{6,9},{8,11},{10,13},{12,15},{14,17},{16,19},{18... | collective-permute-start | bytes 405512 | tf_op jit(solution)/shard_map/while/body/eval_jaxpr/ppermute | solution.py:591
  99.5 20.6 %collective-permute-start.3 = (f32[1544,128]{1,0:T(8,128)S(1)}, f32[1544,128]{1,0:T(8,128)}, u32[]{:S(2)}, u32[]{:S(2)}) collective-permute-start(f32[1544,128]{1,0:T(8,128)S(1)} %get-tuple-element.213), channel_id=1, source_target_pairs={{0,126},{2,0},{4,2},{6,4},{8,6},{10,8},{12,10},{14,12},{16,14},{18... | collective-permute-start | bytes 2371592 | tf_op jit(solution)/shard_map/while/body/eval_jaxpr/ppermute | solution.py:590
  109.2 1.4 collective-permute-start.4
  109.2 4.4 %collective-permute-start.5 = (f32[264,128]{1,0:T(8,128)S(1)}, f32[264,128]{1,0:T(8,128)S(1)}, u32[]{:S(2)}, u32[]{:S(2)}) collective-permute-start(f32[264,128]{1,0:T(8,128)S(1)} %get-tuple-element.215), channel_id=1, source_target_pairs={{0,3},{2,5},{4,7},{6,9},{8,11},{10,13},{12,15},{14,17},{16,19},{18... | collective-permute-start | bytes 405512 | tf_op jit(solution)/shard_map/while/body/eval_jaxpr/ppermute | solution.py:591
  120.1 30.9 %copy-start.3 = (f32[6,256,128]{2,1,0:T(8,128)S(1)}, f32[6,256,128]{2,1,0:T(8,128)}, u32[]{:S(2)}) copy-start(f32[6,256,128]{2,1,0:T(8,128)} %get-tuple-element.249.sketch) | copy-start | bytes 2359300 | tf_op jit(solution)/shard_map/while
  133.4 17.5 %collective-permute-start = (f32[1544,128]{1,0:T(8,128)S(1)}, f32[1544,128]{1,0:T(8,128)S(1)}, u32[]{:S(2)}, u32[]{:S(2)}) collective-permute-start(f32[1544,128]{1,0:T(8,128)S(1)} %get-tuple-element.208), channel_id=1, source_target_pairs={{126,0},{0,2},{2,4},{4,6},{6,8},{8,10},{10,12},{12,14},{14,16},{16... | collective-permute-start | bytes 2371592 | tf_op jit(solution)/shard_map/while/body/eval_jaxpr/ppermute | solution.py:590
  133.5 1.4 collective-permute-start.1
  133.6 10.9 %collective-permute-start.2 = (f32[264,128]{1,0:T(8,128)S(1)}, f32[264,128]{1,0:T(8,128)S(1)}, u32[]{:S(2)}, u32[]{:S(2)}) collective-permute-start(f32[264,128]{1,0:T(8,128)S(1)} %get-tuple-element.210), channel_id=1, source_target_pairs={{0,3},{2,5},{4,7},{6,9},{8,11},{10,13},{12,15},{14,17},{16,19},{18... | collective-permute-start | bytes 405512 | tf_op jit(solution)/shard_map/while/body/eval_jaxpr/ppermute | solution.py:591
  164.3 13.6 %collective-permute-start.3 = (f32[1544,128]{1,0:T(8,128)S(1)}, f32[1544,128]{1,0:T(8,128)}, u32[]{:S(2)}, u32[]{:S(2)}) collective-permute-start(f32[1544,128]{1,0:T(8,128)S(1)} %get-tuple-element.213), channel_id=1, source_target_pairs={{0,126},{2,0},{4,2},{6,4},{8,6},{10,8},{12,10},{14,12},{16,14},{18... | collective-permute-start | bytes 2371592 | tf_op jit(solution)/shard_map/while/body/eval_jaxpr/ppermute | solution.py:590
  165.3 1.4 collective-permute-start.4
  165.6 5.9 %collective-permute-start.5 = (f32[264,128]{1,0:T(8,128)S(1)}, f32[264,128]{1,0:T(8,128)S(1)}, u32[]{:S(2)}, u32[]{:S(2)}) collective-permute-start(f32[264,128]{1,0:T(8,128)S(1)} %get-tuple-element.215), channel_id=1, source_target_pairs={{0,3},{2,5},{4,7},{6,9},{8,11},{10,13},{12,15},{14,17},{16,19},{18... | collective-permute-start | bytes 405512 | tf_op jit(solution)/shard_map/while/body/eval_jaxpr/ppermute | solution.py:591
  177.9 30.9 %copy-start.3 = (f32[6,256,128]{2,1,0:T(8,128)S(1)}, f32[6,256,128]{2,1,0:T(8,128)}, u32[]{:S(2)}) copy-start(f32[6,256,128]{2,1,0:T(8,128)} %get-tuple-element.249.sketch) | copy-start | bytes 2359300 | tf_op jit(solution)/shard_map/while
  191.2 17.5 %collective-permute-start = (f32[1544,128]{1,0:T(8,128)S(1)}, f32[1544,128]{1,0:T(8,128)S(1)}, u32[]{:S(2)}, u32[]{:S(2)}) collective-permute-start(f32[1544,128]{1,0:T(8,128)S(1)} %get-tuple-element.208), channel_id=1, source_target_pairs={{126,0},{0,2},{2,4},{4,6},{6,8},{8,10},{10,12},{12,14},{14,16},{16... | collective-permute-start | bytes 2371592 | tf_op jit(solution)/shard_map/while/body/eval_jaxpr/ppermute | solution.py:590
  191.3 6.0 %collective-permute-start.1 = (f32[264,128]{1,0:T(8,128)S(1)}, f32[264,128]{1,0:T(8,128)S(1)}, u32[]{:S(2)}, u32[]{:S(2)}) collective-permute-start(f32[264,128]{1,0:T(8,128)S(1)} %get-tuple-element.209), channel_id=1, source_target_pairs={{0,1},{1,0},{2,3},{3,2},{4,5},{5,4},{6,7},{7,6},{8,9},{9,8},{10,11... | collective-permute-start | bytes 405512 | tf_op jit(solution)/shard_map/while/body/eval_jaxpr/ppermute | solution.py:592
  196.3 6.2 %collective-permute-start.2 = (f32[264,128]{1,0:T(8,128)S(1)}, f32[264,128]{1,0:T(8,128)S(1)}, u32[]{:S(2)}, u32[]{:S(2)}) collective-permute-start(f32[264,128]{1,0:T(8,128)S(1)} %get-tuple-element.210), channel_id=1, source_target_pairs={{0,3},{2,5},{4,7},{6,9},{8,11},{10,13},{12,15},{14,17},{16,19},{18... | collective-permute-start | bytes 405512 | tf_op jit(solution)/shard_map/while/body/eval_jaxpr/ppermute | solution.py:591
  222.1 16.8 %collective-permute-start.3 = (f32[1544,128]{1,0:T(8,128)S(1)}, f32[1544,128]{1,0:T(8,128)}, u32[]{:S(2)}, u32[]{:S(2)}) collective-permute-start(f32[1544,128]{1,0:T(8,128)S(1)} %get-tuple-element.213), channel_id=1, source_target_pairs={{0,126},{2,0},{4,2},{6,4},{8,6},{10,8},{12,10},{14,12},{16,14},{18... | collective-permute-start | bytes 2371592 | tf_op jit(solution)/shard_map/while/body/eval_jaxpr/ppermute | solution.py:590
  227.9 1.4 collective-permute-start.4
  227.9 5.9 %collective-permute-start.5 = (f32[264,128]{1,0:T(8,128)S(1)}, f32[264,128]{1,0:T(8,128)S(1)}, u32[]{:S(2)}, u32[]{:S(2)}) collective-permute-start(f32[264,128]{1,0:T(8,128)S(1)} %get-tuple-element.215), channel_id=1, source_target_pairs={{0,3},{2,5},{4,7},{6,9},{8,11},{10,13},{12,15},{14,17},{16,19},{18... | collective-permute-start | bytes 405512 | tf_op jit(solution)/shard_map/while/body/eval_jaxpr/ppermute | solution.py:591
  252.9 3.0 %collective-permute-start.17 = (f32[8,128]{1,0:T(8,128)S(1)}, f32[8,128]{1,0:T(8,128)S(1)}, u32[]{:S(2)}, u32[]{:S(2)}) collective-permute-start(f32[8,128]{1,0:T(8,128)S(1)} %slice.23), channel_id=1, source_target_pairs={{0,3},{2,5},{4,7},{6,9},{8,11},{10,13},{12,15},{14,17},{16,19},{18... | collective-permute-start | bytes 12296 | tf_op jit(solution)/shard_map/ppermute | solution.py:610
  256.0 1.2 collective-permute-start.18
  257.2 4.7 %collective-permute-start.19 = (f32[8,128]{1,0:T(8,128)S(1)}, f32[8,128]{1,0:T(8,128)S(1)}, u32[]{:S(2)}, u32[]{:S(2)}) collective-permute-start(f32[8,128]{1,0:T(8,128)S(1)} %add.46), channel_id=1, source_target_pairs={{0,2},{1,3},{2,0},{3,1},{4,6},{5,7},{6,4},{7,5},{8,10},{9,11},{10,... | collective-permute-start | bytes 12296 | tf_op jit(solution)/shard_map/ppermute | solution.py:529
  257.3 5.1 %collective-permute-start.20 = (f32[8,128]{1,0:T(8,128)S(1)}, f32[8,128]{1,0:T(8,128)S(1)}, u32[]{:S(2)}, u32[]{:S(2)}) collective-permute-start(f32[8,128]{1,0:T(8,128)S(1)} %add.46), channel_id=1, source_target_pairs={{0,4},{1,5},{2,6},{3,7},{4,0},{5,1},{6,2},{7,3},{8,12},{9,13},{10,... | collective-permute-start | bytes 12296 | tf_op jit(solution)/shard_map/ppermute | solution.py:529
  257.3 6.2 %collective-permute-start.21 = (f32[8,128]{1,0:T(8,128)S(1)}, f32[8,128]{1,0:T(8,128)S(1)}, u32[]{:S(2)}, u32[]{:S(2)}) collective-permute-start(f32[8,128]{1,0:T(8,128)S(1)} %add.46), channel_id=1, source_target_pairs={{0,6},{1,7},{2,4},{3,5},{4,2},{5,3},{6,0},{7,1},{8,14},{9,15},{10,... | collective-permute-start | bytes 12296 | tf_op jit(solution)/shard_map/ppermute | solution.py:529
  261.9 23.5 %collective-permute-start.16 = (f32[1544,128]{1,0:T(8,128)S(1)}, f32[1544,128]{1,0:T(8,128)S(1)}, u32[]{:S(2)}, u32[]{:S(2)}) collective-permute-start(f32[1544,128]{1,0:T(8,128)S(1)} %get-tuple-element.105), channel_id=1, source_target_pairs={{0,1},{1,0},{2,3},{3,2},{4,5},{5,4},{6,7},{7,6},{8,9},{9,8},{10,11... | collective-permute-start | bytes 2371592 | tf_op jit(solution)/shard_map/ppermute | solution.py:616
  261.9 23.5 %collective-permute-start.15 = (f32[1544,128]{1,0:T(8,128)S(1)}, f32[1544,128]{1,0:T(8,128)S(1)}, u32[]{:S(2)}, u32[]{:S(2)}) collective-permute-start(f32[1544,128]{1,0:T(8,128)S(1)} %get-tuple-element.104), channel_id=1, source_target_pairs={{126,0},{0,2},{2,4},{4,6},{6,8},{8,10},{10,12},{12,14},{14,16},{16... | collective-permute-start | bytes 2371592 | tf_op jit(solution)/shard_map/ppermute | solution.py:615
  263.5 5.6 %collective-permute-start.22 = (f32[8,128]{1,0:T(8,128)S(1)}, f32[8,128]{1,0:T(8,128)S(1)}, u32[]{:S(2)}, u32[]{:S(2)}) collective-permute-start(f32[8,128]{1,0:T(8,128)S(1)} %add_add_fusion.2), channel_id=1, source_target_pairs={{0,8},{1,9},{2,10},{3,11},{4,12},{5,13},{6,14},{7,15},{8,0},{9,1},... | collective-permute-start | bytes 12296 | tf_op jit(solution)/shard_map/ppermute | solution.py:529
  263.5 13.2 %collective-permute-start.23 = (f32[8,128]{1,0:T(8,128)S(1)}, f32[8,128]{1,0:T(8,128)S(1)}, u32[]{:S(2)}, u32[]{:S(2)}) collective-permute-start(f32[8,128]{1,0:T(8,128)S(1)} %add_add_fusion.2), channel_id=1, source_target_pairs={{0,16},{1,17},{2,18},{3,19},{4,20},{5,21},{6,22},{7,23},{8,24},{9,... | collective-permute-start | bytes 12296 | tf_op jit(solution)/shard_map/ppermute | solution.py:529
  269.1 7.6 %collective-permute-start.24 = (f32[8,128]{1,0:T(8,128)S(1)}, f32[8,128]{1,0:T(8,128)S(1)}, u32[]{:S(2)}, u32[]{:S(2)}) collective-permute-start(f32[8,128]{1,0:T(8,128)S(1)} %add_add_fusion.2), channel_id=1, source_target_pairs={{0,24},{1,25},{2,26},{3,27},{4,28},{5,29},{6,30},{7,31},{8,16},{9,... | collective-permute-start | bytes 12296 | tf_op jit(solution)/shard_map/ppermute | solution.py:529
  276.7 4.8 %collective-permute-start.25 = (f32[8,128]{1,0:T(8,128)S(1)}, f32[8,128]{1,0:T(8,128)S(1)}, u32[]{:S(2)}, u32[]{:S(2)}) collective-permute-start(f32[8,128]{1,0:T(8,128)S(1)} %add_add_fusion.1), channel_id=1, source_target_pairs={{0,32},{1,33},{2,34},{3,35},{4,36},{5,37},{6,38},{7,39},{8,40},{9,... | collective-permute-start | bytes 12296 | tf_op jit(solution)/shard_map/ppermute | solution.py:529
  278.3 5.1 %collective-permute-start.26 = (f32[8,128]{1,0:T(8,128)S(1)}, f32[8,128]{1,0:T(8,128)S(1)}, u32[]{:S(2)}, u32[]{:S(2)}) collective-permute-start(f32[8,128]{1,0:T(8,128)S(1)} %add_add_fusion.1), channel_id=1, source_target_pairs={{0,64},{1,65},{2,66},{3,67},{4,68},{5,69},{6,70},{7,71},{8,72},{9,... | collective-permute-start | bytes 12296 | tf_op jit(solution)/shard_map/ppermute | solution.py:529
  280.0 4.8 %collective-permute-start.27 = (f32[8,128]{1,0:T(8,128)S(1)}, f32[8,128]{1,0:T(8,128)S(1)}, u32[]{:S(2)}, u32[]{:S(2)}) collective-permute-start(f32[8,128]{1,0:T(8,128)S(1)} %add_add_fusion.1), channel_id=1, source_target_pairs={{0,96},{1,97},{2,98},{3,99},{4,100},{5,101},{6,102},{7,103},{8,104... | collective-permute-start | bytes 12296 | tf_op jit(solution)/shard_map/ppermute | solution.py:529

commit v3 on v2

--- a/solution.py
+++ b/solution.py
@@ -39,6 +39,14 @@
         pair = jnp.concatenate([a2, a1], ca)
         low = low + dot(pair, jnp.concatenate([b2, b2], cb), dims)
         return low + dot(pair, jnp.concatenate([b1, b1], cb), dims)
+    cn = 1 - cb
+    if b1.shape[cn] <= 128:
+        both = jnp.concatenate([b1, b2], cn)
+        wide = dot(a2, both, dims)
+        wide = wide + dot(a1, both, dims)
+        out = dot(a1, b3, dims)
+        out = out + dot(a3, b1, dims)
+        return out + wide[:, 128:] + wide[:, :128]
     out = dot(a1, b3, dims)
     out = out + dot(a3, b1, dims)
     out = out + dot(a2, b2, dims)

time: 288 us -> 283 us (0.983)
  Pallas kernels: 114 us -> 109 us
    pallas_call x8, Pallas kernels: 107 us -> 102 us  [sweep(): pl.pallas_call(functools.partial(sweep_kernel, parity), out_shape=(shape(...]
where the time goes in v3:
time: 283 us
  Pallas kernels  109 us (39%)
  waiting for transfers between devices  105 us (37%)
  starting transfers between devices  60.6 us (21%)
  local copies, waits for them, and re-layouts  4.86 us (2%)
    pallas_call x8, Pallas kernels, sweep(): pl.pallas_call(functools.partial(sweep_kernel, parity), out_shape=(shape(...  102 us
    ppermute x7, waiting for transfers between devices, spread(): recv = lax.ppermute(send, 'site', moves)  40.5 us
    ppermute x7, waiting for transfers between devices, spread(): cross = lax.ppermute(cross, 'site', over)  34.7 us
    ppermute x7, starting transfers between devices, spread(): recv = lax.ppermute(send, 'site', moves)  16.8 us
    ppermute x10, starting transfers between devices, everywhere(): terms.append(lax.ppermute(value, 'site', moves))  15.2 us
    ppermute x7, starting transfers between devices, spread(): chip = lax.ppermute(chip, 'site', swap)  14.5 us
    ppermute x10, waiting for transfers between devices, everywhere(): terms.append(lax.ppermute(value, 'site', moves))  13.6 us
    ppermute x1, starting transfers between devices, body(): along = lax.ppermute(row, 'site', apart)  8.8 us
  transfers between devices with their start and end apart: 40, of which 28 were waited for; matrix products, arithmetic and copies ran while one was open for 1% of the time, Pallas kernels for 0%

profile of v3, /device:TPU:0, one launch (start us, length us, event | category | flops | bytes accessed | tf_op | source)
XLA Modules:
  0.0 282.7 jit_solution(48303215067950252)
XLA Ops:
  3.3 8.8 %collective-permute-start.7 = (f32[32]{0:T(128)S(1)}, f32[32]{0:T(128)S(1)}, u32[]{:S(2)}, u32[]{:S(2)}) collective-permute-start(f32[32]{0:T(128)S(1)} %concatenate.6), channel_id=1, source_target_pairs={{0,126},{2,0},{4,2},{6,4},{8,6},{10,8},{12,10},{14,12},{16,14},{18... | collective-permute-start | bytes 392 | tf_op jit(solution)/shard_map/ppermute | solution.py:575
  12.2 2.1 slice_bitcast_fusion
  15.2 7.5 %collective-permute-done.8 = f32[32]{0:T(128)S(1)} collective-permute-done((f32[32]{0:T(128)S(1)}, f32[32]{0:T(128)S(1)}, u32[]{:S(2)}, u32[]{:S(2)}) %collective-permute-start.8) | collective-permute-done | bytes 160 | tf_op jit(solution)/shard_map/ppermute | solution.py:576
  22.7 1.4 copy-done.1
  24.1 4.1 %start.1 = (f32[16]{0:T(128)S(1)}, f32[16]{0:T(128)S(1)}, f32[1544,128]{1,0:T(8,128)S(1)}, f32[1544,128]{1,0:T(8,128)S(1)}, f32[264,128]{1,0:T(8,128)S(1)}, /*in...) custom-call(s32[2]{0:T(128)S(1)} %pad_add_fusion.pos, f32[4,32]{1,0:T(4,128)S(1)} %pad_maximum_fusion.meta, ...), custom_call_target="tpu_custom_call" | custom-call | tf_op jit(solution)/shard_map/start/pallas_call | solution.py:445
  28.3 12.7 %sweep.4 = (f32[8,128]{1,0:T(8,128)S(1)}, f32[1544,128]{1,0:T(8,128)}, f32[1544,128]{1,0:T(8,128)S(1)}, f32[264,128]{1,0:T(8,128)S(1)}, f32[264,128]{1,0:T(8,128)S(1)}) custom-call(s32[1]{0:T(128)} %constant.34.clone.1.first_ref, f32[16]{0:T(128)S(1)} %get-tuple-element.224.scal, f32[8,128]{1,0:T(8,128)S(1)} %broadcast_in_dim.8.acc_in, ...), custom_call_target="tpu_custom_call" | custom-call | flops 400000000 | bytes 4000000 | tf_op jit(solution)/shard_map/sweep/pallas_call | solution.py:336
  41.8 2.1 collective-permute-start.13
  44.6 3.4 %collective-permute-done.13 = f32[264,128]{1,0:T(8,128)S(1)} collective-permute-done((f32[264,128]{1,0:T(8,128)S(1)}, f32[264,128]{1,0:T(8,128)S(1)}, u32[]{:S(2)}, u32[]{:S(2)}) %collective-permute-start.13) | collective-permute-done | bytes 135200 | tf_op jit(solution)/shard_map/ppermute | solution.py:599
  48.0 6.5 %collective-permute-done.11 = f32[1544,128]{1,0:T(8,128)} collective-permute-done((f32[1544,128]{1,0:T(8,128)S(1)}, f32[1544,128]{1,0:T(8,128)}, u32[]{:S(2)}, u32[]{:S(2)}) %collective-permute-start.11) | collective-permute-done | bytes 790560 | tf_op jit(solution)/shard_map/ppermute | solution.py:598
  54.6 180.0 %while.18 = (s32[]{:T(128)}, f32[8,128]{1,0:T(8,128)S(1)}, f32[1544,128]{1,0:T(8,128)}, f32[1544,128]{1,0:T(8,128)}, f32[264,128]{1,0:T(8,128)S(1)}, /*index=5*/...) while((s32[]{:T(128)}, f32[8,128]{1,0:T(8,128)S(1)}, ...), condition=%wide.region_1.2_spmd, body=%wide.region_0.1_spmd.sunk | while | flops 800000000 | bytes 19633024 | solution.py:613
  54.6 12.8 %sweep.6 = (f32[8,128]{1,0:T(8,128)S(1)}, f32[1544,128]{1,0:T(8,128)S(1)}, f32[1544,128]{1,0:T(8,128)S(1)}, f32[264,128]{1,0:T(8,128)S(1)}, f32[264,128]{1,0:T(8,128)S(1)}) custom-call(s32[1]{0:T(128)} %get-tuple-element.251.first_ref, f32[16]{0:T(128)S(1)} %get-tuple-element.246.scal, f32[8,128]{1,0:T(8,128)S(1)} %get-tuple-element.229.acc_in, ...), custom_call_target="tpu_custom_call" | custom-call | flops 400000000 | bytes 4000000 | tf_op jit(solution)/shard_map/while/body/eval_jaxpr/sweep/pallas_call | solution.py:336
  67.4 9.0 %collective-permute-start.1 = (f32[264,128]{1,0:T(8,128)S(1)}, f32[264,128]{1,0:T(8,128)S(1)}, u32[]{:S(2)}, u32[]{:S(2)}) collective-permute-start(f32[264,128]{1,0:T(8,128)S(1)} %get-tuple-element.209), channel_id=1, source_target_pairs={{0,1},{1,0},{2,3},{3,2},{4,5},{5,4},{6,7},{7,6},{8,9},{9,8},{10,11... | collective-permute-start | bytes 405512 | tf_op jit(solution)/shard_map/while/body/eval_jaxpr/ppermute | solution.py:600
  77.4 4.1 %collective-permute-done.2.cross = f32[264,128]{1,0:T(8,128)S(1)} collective-permute-done((f32[264,128]{1,0:T(8,128)S(1)}, f32[264,128]{1,0:T(8,128)S(1)}, u32[]{:S(2)}, u32[]{:S(2)}) %collective-permute-start.2) | collective-permute-done | bytes 135200 | tf_op jit(solution)/shard_map/while/body/eval_jaxpr/ppermute | solution.py:599
  81.5 3.3 %collective-permute-done.recv = f32[1544,128]{1,0:T(8,128)S(1)} collective-permute-done((f32[1544,128]{1,0:T(8,128)S(1)}, f32[1544,128]{1,0:T(8,128)S(1)}, u32[]{:S(2)}, u32[]{:S(2)}) %collective-permute-start) | collective-permute-done | bytes 790560 | tf_op jit(solution)/shard_map/while/body/eval_jaxpr/ppermute | solution.py:598
  84.9 12.7 %sweep.7 = (f32[8,128]{1,0:T(8,128)S(1)}, f32[1544,128]{1,0:T(8,128)}, f32[1544,128]{1,0:T(8,128)S(1)}, f32[264,128]{1,0:T(8,128)S(1)}, f32[264,128]{1,0:T(8,128)S(1)}) custom-call(s32[1]{0:T(128)} %get-tuple-element.251.first_ref, f32[16]{0:T(128)S(1)} %get-tuple-element.248.scal, f32[8,128]{1,0:T(8,128)S(1)} %get-tuple-element.206.acc_in, ...), custom_call_target="tpu_custom_call" | custom-call | flops 400000000 | bytes 4000000 | tf_op jit(solution)/shard_map/while/body/eval_jaxpr/sweep/pallas_call | solution.py:336
  97.6 9.8 %collective-permute-start.3 = (f32[1544,128]{1,0:T(8,128)S(1)}, f32[1544,128]{1,0:T(8,128)}, u32[]{:S(2)}, u32[]{:S(2)}) collective-permute-start(f32[1544,128]{1,0:T(8,128)S(1)} %get-tuple-element.213), channel_id=1, source_target_pairs={{0,126},{2,0},{4,2},{6,4},{8,6},{10,8},{12,10},{14,12},{16,14},{18... | collective-permute-start | bytes 2371592 | tf_op jit(solution)/shard_map/while/body/eval_jaxpr/ppermute | solution.py:598
  107.4 1.3 collective-permute-done.4
  108.7 3.1 %collective-permute-done.5 = f32[264,128]{1,0:T(8,128)S(1)} collective-permute-done((f32[264,128]{1,0:T(8,128)S(1)}, f32[264,128]{1,0:T(8,128)S(1)}, u32[]{:S(2)}, u32[]{:S(2)}) %collective-permute-start.5) | collective-permute-done | bytes 135200 | tf_op jit(solution)/shard_map/while/body/eval_jaxpr/ppermute | solution.py:599
  111.8 6.4 %collective-permute-done.3 = f32[1544,128]{1,0:T(8,128)} collective-permute-done((f32[1544,128]{1,0:T(8,128)S(1)}, f32[1544,128]{1,0:T(8,128)}, u32[]{:S(2)}, u32[]{:S(2)}) %collective-permute-start.3) | collective-permute-done | bytes 790560 | tf_op jit(solution)/shard_map/while/body/eval_jaxpr/ppermute | solution.py:598
  118.2 12.7 %sweep.6 = (f32[8,128]{1,0:T(8,128)S(1)}, f32[1544,128]{1,0:T(8,128)S(1)}, f32[1544,128]{1,0:T(8,128)S(1)}, f32[264,128]{1,0:T(8,128)S(1)}, f32[264,128]{1,0:T(8,128)S(1)}) custom-call(s32[1]{0:T(128)} %get-tuple-element.251.first_ref, f32[16]{0:T(128)S(1)} %get-tuple-element.246.scal, f32[8,128]{1,0:T(8,128)S(1)} %get-tuple-element.229.acc_in, ...), custom_call_target="tpu_custom_call" | custom-call | flops 400000000 | bytes 4000000 | tf_op jit(solution)/shard_map/while/body/eval_jaxpr/sweep/pallas_call | solution.py:336
  131.2 1.2 collective-permute-done.1.chip
  132.5 9.6 %collective-permute-done.2.cross = f32[264,128]{1,0:T(8,128)S(1)} collective-permute-done((f32[264,128]{1,0:T(8,128)S(1)}, f32[264,128]{1,0:T(8,128)S(1)}, u32[]{:S(2)}, u32[]{:S(2)}) %collective-permute-start.2) | collective-permute-done | bytes 135200 | tf_op jit(solution)/shard_map/while/body/eval_jaxpr/ppermute | solution.py:599
  142.0 6.5 %collective-permute-done.recv = f32[1544,128]{1,0:T(8,128)S(1)} collective-permute-done((f32[1544,128]{1,0:T(8,128)S(1)}, f32[1544,128]{1,0:T(8,128)S(1)}, u32[]{:S(2)}, u32[]{:S(2)}) %collective-permute-start) | collective-permute-done | bytes 790560 | tf_op jit(solution)/shard_map/while/body/eval_jaxpr/ppermute | solution.py:598
  148.5 12.7 %sweep.7 = (f32[8,128]{1,0:T(8,128)S(1)}, f32[1544,128]{1,0:T(8,128)}, f32[1544,128]{1,0:T(8,128)S(1)}, f32[264,128]{1,0:T(8,128)S(1)}, f32[264,128]{1,0:T(8,128)S(1)}) custom-call(s32[1]{0:T(128)} %get-tuple-element.251.first_ref, f32[16]{0:T(128)S(1)} %get-tuple-element.248.scal, f32[8,128]{1,0:T(8,128)S(1)} %get-tuple-element.206.acc_in, ...), custom_call_target="tpu_custom_call" | custom-call | flops 400000000 | bytes 4000000 | tf_op jit(solution)/shard_map/while/body/eval_jaxpr/sweep/pallas_call | solution.py:336
  163.5 4.8 %collective-permute-done.5 = f32[264,128]{1,0:T(8,128)S(1)} collective-permute-done((f32[264,128]{1,0:T(8,128)S(1)}, f32[264,128]{1,0:T(8,128)S(1)}, u32[]{:S(2)}, u32[]{:S(2)}) %collective-permute-start.5) | collective-permute-done | bytes 135200 | tf_op jit(solution)/shard_map/while/body/eval_jaxpr/ppermute | solution.py:599
  168.4 6.4 %collective-permute-done.3 = f32[1544,128]{1,0:T(8,128)} collective-permute-done((f32[1544,128]{1,0:T(8,128)S(1)}, f32[1544,128]{1,0:T(8,128)}, u32[]{:S(2)}, u32[]{:S(2)}) %collective-permute-start.3) | collective-permute-done | bytes 790560 | tf_op jit(solution)/shard_map/while/body/eval_jaxpr/ppermute | solution.py:598
  174.8 12.7 %sweep.6 = (f32[8,128]{1,0:T(8,128)S(1)}, f32[1544,128]{1,0:T(8,128)S(1)}, f32[1544,128]{1,0:T(8,128)S(1)}, f32[264,128]{1,0:T(8,128)S(1)}, f32[264,128]{1,0:T(8,128)S(1)}) custom-call(s32[1]{0:T(128)} %get-tuple-element.251.first_ref, f32[16]{0:T(128)S(1)} %get-tuple-element.246.scal, f32[8,128]{1,0:T(8,128)S(1)} %get-tuple-element.229.acc_in, ...), custom_call_target="tpu_custom_call" | custom-call | flops 400000000 | bytes 4000000 | tf_op jit(solution)/shard_map/while/body/eval_jaxpr/sweep/pallas_call | solution.py:336
  187.6 5.0 %collective-permute-start.1 = (f32[264,128]{1,0:T(8,128)S(1)}, f32[264,128]{1,0:T(8,128)S(1)}, u32[]{:S(2)}, u32[]{:S(2)}) collective-permute-start(f32[264,128]{1,0:T(8,128)S(1)} %get-tuple-element.209), channel_id=1, source_target_pairs={{0,1},{1,0},{2,3},{3,2},{4,5},{5,4},{6,7},{7,6},{8,9},{9,8},{10,11... | collective-permute-start | bytes 405512 | tf_op jit(solution)/shard_map/while/body/eval_jaxpr/ppermute | solution.py:600
  193.6 5.2 %collective-permute-done.2.cross = f32[264,128]{1,0:T(8,128)S(1)} collective-permute-done((f32[264,128]{1,0:T(8,128)S(1)}, f32[264,128]{1,0:T(8,128)S(1)}, u32[]{:S(2)}, u32[]{:S(2)}) %collective-permute-start.2) | collective-permute-done | bytes 135200 | tf_op jit(solution)/shard_map/while/body/eval_jaxpr/ppermute | solution.py:599
  198.8 6.3 %collective-permute-done.recv = f32[1544,128]{1,0:T(8,128)S(1)} collective-permute-done((f32[1544,128]{1,0:T(8,128)S(1)}, f32[1544,128]{1,0:T(8,128)S(1)}, u32[]{:S(2)}, u32[]{:S(2)}) %collective-permute-start) | collective-permute-done | bytes 790560 | tf_op jit(solution)/shard_map/while/body/eval_jaxpr/ppermute | solution.py:598
  205.1 12.7 %sweep.7 = (f32[8,128]{1,0:T(8,128)S(1)}, f32[1544,128]{1,0:T(8,128)}, f32[1544,128]{1,0:T(8,128)S(1)}, f32[264,128]{1,0:T(8,128)S(1)}, f32[264,128]{1,0:T(8,128)S(1)}) custom-call(s32[1]{0:T(128)} %get-tuple-element.251.first_ref, f32[16]{0:T(128)S(1)} %get-tuple-element.248.scal, f32[8,128]{1,0:T(8,128)S(1)} %get-tuple-element.206.acc_in, ...), custom_call_target="tpu_custom_call" | custom-call | flops 400000000 | bytes 4000000 | tf_op jit(solution)/shard_map/while/body/eval_jaxpr/sweep/pallas_call | solution.py:336
  217.8 5.8 %collective-permute-start.3 = (f32[1544,128]{1,0:T(8,128)S(1)}, f32[1544,128]{1,0:T(8,128)}, u32[]{:S(2)}, u32[]{:S(2)}) collective-permute-start(f32[1544,128]{1,0:T(8,128)S(1)} %get-tuple-element.213), channel_id=1, source_target_pairs={{0,126},{2,0},{4,2},{6,4},{8,6},{10,8},{12,10},{14,12},{16,14},{18... | collective-permute-start | bytes 2371592 | tf_op jit(solution)/shard_map/while/body/eval_jaxpr/ppermute | solution.py:598
  223.6 1.3 collective-permute-done.4
  224.9 4.5 %collective-permute-done.5 = f32[264,128]{1,0:T(8,128)S(1)} collective-permute-done((f32[264,128]{1,0:T(8,128)S(1)}, f32[264,128]{1,0:T(8,128)S(1)}, u32[]{:S(2)}, u32[]{:S(2)}) %collective-permute-start.5) | collective-permute-done | bytes 135200 | tf_op jit(solution)/shard_map/while/body/eval_jaxpr/ppermute | solution.py:599
  229.4 5.1 %collective-permute-done.3 = f32[1544,128]{1,0:T(8,128)} collective-permute-done((f32[1544,128]{1,0:T(8,128)S(1)}, f32[1544,128]{1,0:T(8,128)}, u32[]{:S(2)}, u32[]{:S(2)}) %collective-permute-start.3) | collective-permute-done | bytes 790560 | tf_op jit(solution)/shard_map/while/body/eval_jaxpr/ppermute | solution.py:598
  234.6 13.4 %sweep.5 = (f32[8,128]{1,0:T(8,128)S(1)}, f32[1544,128]{1,0:T(8,128)S(1)}, f32[1544,128]{1,0:T(8,128)S(1)}, f32[264,128]{1,0:T(8,128)}, f32[264,128]{1,0:T(8,128)}) custom-call(s32[1]{0:T(128)} %constant.33.clone.1.first_ref, f32[16]{0:T(128)S(1)} %get-tuple-element.278, f32[8,128]{1,0:T(8,128)S(1)} %get-tuple-element.99.acc_in, ...), custom_call_target="tpu_custom_call" | custom-call | flops 400000000 | bytes 4000000 | tf_op jit(solution)/shard_map/sweep/pallas_call | solution.py:336
  247.9 3.0 %collective-permute-done.17 = f32[8,128]{1,0:T(8,128)S(1)} collective-permute-done((f32[8,128]{1,0:T(8,128)S(1)}, f32[8,128]{1,0:T(8,128)S(1)}, u32[]{:S(2)}, u32[]{:S(2)}) %collective-permute-start.17) | collective-permute-done | bytes 4128 | tf_op jit(solution)/shard_map/ppermute | solution.py:618
  251.1 1.2 collective-permute-done.18
  252.3 4.6 %collective-permute-start.21 = (f32[8,128]{1,0:T(8,128)S(1)}, f32[8,128]{1,0:T(8,128)S(1)}, u32[]{:S(2)}, u32[]{:S(2)}) collective-permute-start(f32[8,128]{1,0:T(8,128)S(1)} %add.46), channel_id=1, source_target_pairs={{0,6},{1,7},{2,4},{3,5},{4,2},{5,3},{6,0},{7,1},{8,14},{9,15},{10,... | collective-permute-start | bytes 12296 | tf_op jit(solution)/shard_map/ppermute | solution.py:537
  257.4 1.1 collective-permute-done.21
  258.6 5.7 %collective-permute-start.23 = (f32[8,128]{1,0:T(8,128)S(1)}, f32[8,128]{1,0:T(8,128)S(1)}, u32[]{:S(2)}, u32[]{:S(2)}) collective-permute-start(f32[8,128]{1,0:T(8,128)S(1)} %add_add_fusion.2), channel_id=1, source_target_pairs={{0,16},{1,17},{2,18},{3,19},{4,20},{5,21},{6,22},{7,23},{8,24},{9,... | collective-permute-start | bytes 12296 | tf_op jit(solution)/shard_map/ppermute | solution.py:537
  264.2 7.6 %collective-permute-done.23 = f32[8,128]{1,0:T(8,128)S(1)} collective-permute-done((f32[8,128]{1,0:T(8,128)S(1)}, f32[8,128]{1,0:T(8,128)S(1)}, u32[]{:S(2)}, u32[]{:S(2)}) %collective-permute-start.23) | collective-permute-done | bytes 4128 | tf_op jit(solution)/shard_map/ppermute | solution.py:537
  271.8 1.6 collective-permute-start.25
  273.4 1.7 collective-permute-start.26
  275.1 1.5 collective-permute-start.27
  276.6 1.9 collective-permute-done.26
  278.5 1.4 collective-permute-done.27
  280.5 2.0 finish.1
  (76 shorter events, 10.6 us)
Async XLA Ops:
  0.6 22.1 %copy-start = (f32[1,12,256,128]{3,2,1,0:T(8,128)S(1)}, f32[1,12,256,128]{3,2,1,0:T(8,128)}, u32[]{:S(2)}) copy-start(f32[1,12,256,128]{3,2,1,0:T(8,128)} %param.13) | copy-start | bytes 4718596
  0.6 22.0 %collective-permute-start.10 = (f32[12,256,128]{2,1,0:T(8,128)}, f32[12,256,128]{2,1,0:T(8,128)S(1)}, u32[]{:S(2)}, u32[]{:S(2)}) collective-permute-start(f32[12,256,128]{2,1,0:T(8,128)} %bitcast.19), channel_id=1, source_target_pairs={{0,1},{1,0},{2,3},{3,2},{4,5},{5,4},{6,7},{7,6},{8,9},{9,8},{10,11... | collective-permute-start | bytes 4718600 | tf_op jit(solution)/shard_map/ppermute | solution.py:588
  0.7 21.9 %collective-permute-start.9 = (f32[2,12,128,128]{3,2,1,0:T(8,128)}, f32[2,12,128,128]{3,2,1,0:T(8,128)}, u32[]{:S(2)}, u32[]{:S(2)}) collective-permute-start(f32[2,12,128,128]{3,2,1,0:T(8,128)} %bitcast.21), channel_id=1, source_target_pairs={{0,1},{1,0},{2,3},{3,2},{4,5},{5,4},{6,7},{7,6},{8,9},{9,8},{10,11... | collective-permute-start | bytes 4718600 | tf_op jit(solution)/shard_map/ppermute | solution.py:587
  3.3 11.9 %collective-permute-start.7 = (f32[32]{0:T(128)S(1)}, f32[32]{0:T(128)S(1)}, u32[]{:S(2)}, u32[]{:S(2)}) collective-permute-start(f32[32]{0:T(128)S(1)} %concatenate.6), channel_id=1, source_target_pairs={{0,126},{2,0},{4,2},{6,4},{8,6},{10,8},{12,10},{14,12},{16,14},{18... | collective-permute-start | bytes 392 | tf_op jit(solution)/shard_map/ppermute | solution.py:575
  12.1 3.1 %collective-permute-start.6 = (f32[32]{0:T(128)S(1)}, f32[32]{0:T(128)S(1)}, u32[]{:S(2)}, u32[]{:S(2)}) collective-permute-start(f32[32]{0:T(128)S(1)} %concatenate.6), channel_id=1, source_target_pairs={{0,1},{1,0},{2,3},{3,2},{4,5},{5,4},{6,7},{7,6},{8,9},{9,8},{10,11... | collective-permute-start | bytes 392 | tf_op jit(solution)/shard_map/ppermute | solution.py:574
  14.2 8.4 %collective-permute-start.8 = (f32[32]{0:T(128)S(1)}, f32[32]{0:T(128)S(1)}, u32[]{:S(2)}, u32[]{:S(2)}) collective-permute-start(f32[32]{0:T(128)S(1)} %concatenate.6), channel_id=1, source_target_pairs={{2,1},{4,3},{6,5},{8,7},{10,9},{12,11},{14,13},{16,15},{18,17},{20... | collective-permute-start | bytes 392 | tf_op jit(solution)/shard_map/ppermute | solution.py:576
  22.7 1.4 copy-start.1
  28.2 16.4 %copy-start.2 = (f32[6,256,128]{2,1,0:T(8,128)}, f32[6,256,128]{2,1,0:T(8,128)S(1)}, u32[]{:S(2)}) copy-start(f32[6,256,128]{2,1,0:T(8,128)S(1)} %get-tuple-element.225.sketch) | copy-start | bytes 2359300
  28.2 12.7 %copy-start.4 = (f32[6,256,128]{2,1,0:T(8,128)S(1)}, f32[6,256,128]{2,1,0:T(8,128)}, u32[]{:S(2)}) copy-start(f32[6,256,128]{2,1,0:T(8,128)} %slice_bitcast_fusion) | copy-start | bytes 2359300
  41.0 13.6 %collective-permute-start.11 = (f32[1544,128]{1,0:T(8,128)S(1)}, f32[1544,128]{1,0:T(8,128)}, u32[]{:S(2)}, u32[]{:S(2)}) collective-permute-start(f32[1544,128]{1,0:T(8,128)S(1)} %get-tuple-element.95), channel_id=1, source_target_pairs={{0,126},{2,0},{4,2},{6,4},{8,6},{10,8},{12,10},{14,12},{16,14},{18... | collective-permute-start | bytes 2371592 | tf_op jit(solution)/shard_map/ppermute | solution.py:598
  41.0 2.9 %collective-permute-start.14 = (f32[6,256,128]{2,1,0:T(8,128)S(1)}, f32[6,256,128]{2,1,0:T(8,128)S(1)}, u32[]{:S(2)}, u32[]{:S(2)}) collective-permute-start(f32[6,256,128]{2,1,0:T(8,128)S(1)} %copy-done.4), channel_id=1, source_target_pairs={{1,3},{3,5},{5,7},{7,9},{9,11},{11,13},{13,15},{15,17},{17,19},{19... | collective-permute-start | bytes 2359304 | tf_op jit(solution)/shard_map/ppermute | solution.py:590
  41.7 2.9 %collective-permute-start.12 = (f32[264,128]{1,0:T(8,128)S(1)}, f32[264,128]{1,0:T(8,128)S(1)}, u32[]{:S(2)}, u32[]{:S(2)}) collective-permute-start(f32[264,128]{1,0:T(8,128)S(1)} %get-tuple-element.96), channel_id=1, source_target_pairs={{0,1},{1,0},{2,3},{3,2},{4,5},{5,4},{6,7},{7,6},{8,9},{9,8},{10,11... | collective-permute-start | bytes 405512 | tf_op jit(solution)/shard_map/ppermute | solution.py:600
  41.8 6.3 %collective-permute-start.13 = (f32[264,128]{1,0:T(8,128)S(1)}, f32[264,128]{1,0:T(8,128)S(1)}, u32[]{:S(2)}, u32[]{:S(2)}) collective-permute-start(f32[264,128]{1,0:T(8,128)S(1)} %get-tuple-element.97), channel_id=1, source_target_pairs={{0,3},{2,5},{4,7},{6,9},{8,11},{10,13},{12,15},{14,17},{16,19},{18... | collective-permute-start | bytes 405512 | tf_op jit(solution)/shard_map/ppermute | solution.py:599
  54.6 30.3 %copy-start.3 = (f32[6,256,128]{2,1,0:T(8,128)S(1)}, f32[6,256,128]{2,1,0:T(8,128)}, u32[]{:S(2)}) copy-start(f32[6,256,128]{2,1,0:T(8,128)} %get-tuple-element.249.sketch) | copy-start | bytes 2359300 | tf_op jit(solution)/shard_map/while
  67.3 17.5 %collective-permute-start = (f32[1544,128]{1,0:T(8,128)S(1)}, f32[1544,128]{1,0:T(8,128)S(1)}, u32[]{:S(2)}, u32[]{:S(2)}) collective-permute-start(f32[1544,128]{1,0:T(8,128)S(1)} %get-tuple-element.208), channel_id=1, source_target_pairs={{126,0},{0,2},{2,4},{4,6},{6,8},{8,10},{10,12},{12,14},{14,16},{16... | collective-permute-start | bytes 2371592 | tf_op jit(solution)/shard_map/while/body/eval_jaxpr/ppermute | solution.py:598
  67.4 10.0 %collective-permute-start.1 = (f32[264,128]{1,0:T(8,128)S(1)}, f32[264,128]{1,0:T(8,128)S(1)}, u32[]{:S(2)}, u32[]{:S(2)}) collective-permute-start(f32[264,128]{1,0:T(8,128)S(1)} %get-tuple-element.209), channel_id=1, source_target_pairs={{0,1},{1,0},{2,3},{3,2},{4,5},{5,4},{6,7},{7,6},{8,9},{9,8},{10,11... | collective-permute-start | bytes 405512 | tf_op jit(solution)/shard_map/while/body/eval_jaxpr/ppermute | solution.py:600
  76.4 5.1 %collective-permute-start.2 = (f32[264,128]{1,0:T(8,128)S(1)}, f32[264,128]{1,0:T(8,128)S(1)}, u32[]{:S(2)}, u32[]{:S(2)}) collective-permute-start(f32[264,128]{1,0:T(8,128)S(1)} %get-tuple-element.210), channel_id=1, source_target_pairs={{0,3},{2,5},{4,7},{6,9},{8,11},{10,13},{12,15},{14,17},{16,19},{18... | collective-permute-start | bytes 405512 | tf_op jit(solution)/shard_map/while/body/eval_jaxpr/ppermute | solution.py:599
  97.6 20.6 %collective-permute-start.3 = (f32[1544,128]{1,0:T(8,128)S(1)}, f32[1544,128]{1,0:T(8,128)}, u32[]{:S(2)}, u32[]{:S(2)}) collective-permute-start(f32[1544,128]{1,0:T(8,128)S(1)} %get-tuple-element.213), channel_id=1, source_target_pairs={{0,126},{2,0},{4,2},{6,4},{8,6},{10,8},{12,10},{14,12},{16,14},{18... | collective-permute-start | bytes 2371592 | tf_op jit(solution)/shard_map/while/body/eval_jaxpr/ppermute | solution.py:598
  107.4 1.4 collective-permute-start.4
  107.4 4.4 %collective-permute-start.5 = (f32[264,128]{1,0:T(8,128)S(1)}, f32[264,128]{1,0:T(8,128)S(1)}, u32[]{:S(2)}, u32[]{:S(2)}) collective-permute-start(f32[264,128]{1,0:T(8,128)S(1)} %get-tuple-element.215), channel_id=1, source_target_pairs={{0,3},{2,5},{4,7},{6,9},{8,11},{10,13},{12,15},{14,17},{16,19},{18... | collective-permute-start | bytes 405512 | tf_op jit(solution)/shard_map/while/body/eval_jaxpr/ppermute | solution.py:599
  118.2 30.3 %copy-start.3 = (f32[6,256,128]{2,1,0:T(8,128)S(1)}, f32[6,256,128]{2,1,0:T(8,128)}, u32[]{:S(2)}) copy-start(f32[6,256,128]{2,1,0:T(8,128)} %get-tuple-element.249.sketch) | copy-start | bytes 2359300 | tf_op jit(solution)/shard_map/while
  130.9 17.5 %collective-permute-start = (f32[1544,128]{1,0:T(8,128)S(1)}, f32[1544,128]{1,0:T(8,128)S(1)}, u32[]{:S(2)}, u32[]{:S(2)}) collective-permute-start(f32[1544,128]{1,0:T(8,128)S(1)} %get-tuple-element.208), channel_id=1, source_target_pairs={{126,0},{0,2},{2,4},{4,6},{6,8},{8,10},{10,12},{12,14},{14,16},{16... | collective-permute-start | bytes 2371592 | tf_op jit(solution)/shard_map/while/body/eval_jaxpr/ppermute | solution.py:598
  131.0 1.4 collective-permute-start.1
  131.1 10.9 %collective-permute-start.2 = (f32[264,128]{1,0:T(8,128)S(1)}, f32[264,128]{1,0:T(8,128)S(1)}, u32[]{:S(2)}, u32[]{:S(2)}) collective-permute-start(f32[264,128]{1,0:T(8,128)S(1)} %get-tuple-element.210), channel_id=1, source_target_pairs={{0,3},{2,5},{4,7},{6,9},{8,11},{10,13},{12,15},{14,17},{16,19},{18... | collective-permute-start | bytes 405512 | tf_op jit(solution)/shard_map/while/body/eval_jaxpr/ppermute | solution.py:599
  161.2 13.6 %collective-permute-start.3 = (f32[1544,128]{1,0:T(8,128)S(1)}, f32[1544,128]{1,0:T(8,128)}, u32[]{:S(2)}, u32[]{:S(2)}) collective-permute-start(f32[1544,128]{1,0:T(8,128)S(1)} %get-tuple-element.213), channel_id=1, source_target_pairs={{0,126},{2,0},{4,2},{6,4},{8,6},{10,8},{12,10},{14,12},{16,14},{18... | collective-permute-start | bytes 2371592 | tf_op jit(solution)/shard_map/while/body/eval_jaxpr/ppermute | solution.py:598
  162.2 1.4 collective-permute-start.4
  162.5 5.9 %collective-permute-start.5 = (f32[264,128]{1,0:T(8,128)S(1)}, f32[264,128]{1,0:T(8,128)S(1)}, u32[]{:S(2)}, u32[]{:S(2)}) collective-permute-start(f32[264,128]{1,0:T(8,128)S(1)} %get-tuple-element.215), channel_id=1, source_target_pairs={{0,3},{2,5},{4,7},{6,9},{8,11},{10,13},{12,15},{14,17},{16,19},{18... | collective-permute-start | bytes 405512 | tf_op jit(solution)/shard_map/while/body/eval_jaxpr/ppermute | solution.py:599
  174.8 30.3 %copy-start.3 = (f32[6,256,128]{2,1,0:T(8,128)S(1)}, f32[6,256,128]{2,1,0:T(8,128)}, u32[]{:S(2)}) copy-start(f32[6,256,128]{2,1,0:T(8,128)} %get-tuple-element.249.sketch) | copy-start | bytes 2359300 | tf_op jit(solution)/shard_map/while
  187.5 17.5 %collective-permute-start = (f32[1544,128]{1,0:T(8,128)S(1)}, f32[1544,128]{1,0:T(8,128)S(1)}, u32[]{:S(2)}, u32[]{:S(2)}) collective-permute-start(f32[1544,128]{1,0:T(8,128)S(1)} %get-tuple-element.208), channel_id=1, source_target_pairs={{126,0},{0,2},{2,4},{4,6},{6,8},{8,10},{10,12},{12,14},{14,16},{16... | collective-permute-start | bytes 2371592 | tf_op jit(solution)/shard_map/while/body/eval_jaxpr/ppermute | solution.py:598
  187.6 6.0 %collective-permute-start.1 = (f32[264,128]{1,0:T(8,128)S(1)}, f32[264,128]{1,0:T(8,128)S(1)}, u32[]{:S(2)}, u32[]{:S(2)}) collective-permute-start(f32[264,128]{1,0:T(8,128)S(1)} %get-tuple-element.209), channel_id=1, source_target_pairs={{0,1},{1,0},{2,3},{3,2},{4,5},{5,4},{6,7},{7,6},{8,9},{9,8},{10,11... | collective-permute-start | bytes 405512 | tf_op jit(solution)/shard_map/while/body/eval_jaxpr/ppermute | solution.py:600
  192.6 6.2 %collective-permute-start.2 = (f32[264,128]{1,0:T(8,128)S(1)}, f32[264,128]{1,0:T(8,128)S(1)}, u32[]{:S(2)}, u32[]{:S(2)}) collective-permute-start(f32[264,128]{1,0:T(8,128)S(1)} %get-tuple-element.210), channel_id=1, source_target_pairs={{0,3},{2,5},{4,7},{6,9},{8,11},{10,13},{12,15},{14,17},{16,19},{18... | collective-permute-start | bytes 405512 | tf_op jit(solution)/shard_map/while/body/eval_jaxpr/ppermute | solution.py:599
  217.8 16.8 %collective-permute-start.3 = (f32[1544,128]{1,0:T(8,128)S(1)}, f32[1544,128]{1,0:T(8,128)}, u32[]{:S(2)}, u32[]{:S(2)}) collective-permute-start(f32[1544,128]{1,0:T(8,128)S(1)} %get-tuple-element.213), channel_id=1, source_target_pairs={{0,126},{2,0},{4,2},{6,4},{8,6},{10,8},{12,10},{14,12},{16,14},{18... | collective-permute-start | bytes 2371592 | tf_op jit(solution)/shard_map/while/body/eval_jaxpr/ppermute | solution.py:598
  223.6 1.4 collective-permute-start.4
  223.6 5.9 %collective-permute-start.5 = (f32[264,128]{1,0:T(8,128)S(1)}, f32[264,128]{1,0:T(8,128)S(1)}, u32[]{:S(2)}, u32[]{:S(2)}) collective-permute-start(f32[264,128]{1,0:T(8,128)S(1)} %get-tuple-element.215), channel_id=1, source_target_pairs={{0,3},{2,5},{4,7},{6,9},{8,11},{10,13},{12,15},{14,17},{16,19},{18... | collective-permute-start | bytes 405512 | tf_op jit(solution)/shard_map/while/body/eval_jaxpr/ppermute | solution.py:599
  247.9 3.0 %collective-permute-start.17 = (f32[8,128]{1,0:T(8,128)S(1)}, f32[8,128]{1,0:T(8,128)S(1)}, u32[]{:S(2)}, u32[]{:S(2)}) collective-permute-start(f32[8,128]{1,0:T(8,128)S(1)} %slice.23), channel_id=1, source_target_pairs={{0,3},{2,5},{4,7},{6,9},{8,11},{10,13},{12,15},{14,17},{16,19},{18... | collective-permute-start | bytes 12296 | tf_op jit(solution)/shard_map/ppermute | solution.py:618
  251.0 1.2 collective-permute-start.18
  252.3 4.7 %collective-permute-start.19 = (f32[8,128]{1,0:T(8,128)S(1)}, f32[8,128]{1,0:T(8,128)S(1)}, u32[]{:S(2)}, u32[]{:S(2)}) collective-permute-start(f32[8,128]{1,0:T(8,128)S(1)} %add.46), channel_id=1, source_target_pairs={{0,2},{1,3},{2,0},{3,1},{4,6},{5,7},{6,4},{7,5},{8,10},{9,11},{10,... | collective-permute-start | bytes 12296 | tf_op jit(solution)/shard_map/ppermute | solution.py:537
  252.3 5.1 %collective-permute-start.20 = (f32[8,128]{1,0:T(8,128)S(1)}, f32[8,128]{1,0:T(8,128)S(1)}, u32[]{:S(2)}, u32[]{:S(2)}) collective-permute-start(f32[8,128]{1,0:T(8,128)S(1)} %add.46), channel_id=1, source_target_pairs={{0,4},{1,5},{2,6},{3,7},{4,0},{5,1},{6,2},{7,3},{8,12},{9,13},{10,... | collective-permute-start | bytes 12296 | tf_op jit(solution)/shard_map/ppermute | solution.py:537
  252.3 6.2 %collective-permute-start.21 = (f32[8,128]{1,0:T(8,128)S(1)}, f32[8,128]{1,0:T(8,128)S(1)}, u32[]{:S(2)}, u32[]{:S(2)}) collective-permute-start(f32[8,128]{1,0:T(8,128)S(1)} %add.46), channel_id=1, source_target_pairs={{0,6},{1,7},{2,4},{3,5},{4,2},{5,3},{6,0},{7,1},{8,14},{9,15},{10,... | collective-permute-start | bytes 12296 | tf_op jit(solution)/shard_map/ppermute | solution.py:537
  257.0 23.6 %collective-permute-start.16 = (f32[1544,128]{1,0:T(8,128)S(1)}, f32[1544,128]{1,0:T(8,128)S(1)}, u32[]{:S(2)}, u32[]{:S(2)}) collective-permute-start(f32[1544,128]{1,0:T(8,128)S(1)} %get-tuple-element.105), channel_id=1, source_target_pairs={{0,1},{1,0},{2,3},{3,2},{4,5},{5,4},{6,7},{7,6},{8,9},{9,8},{10,11... | collective-permute-start | bytes 2371592 | tf_op jit(solution)/shard_map/ppermute | solution.py:624
  257.0 23.6 %collective-permute-start.15 = (f32[1544,128]{1,0:T(8,128)S(1)}, f32[1544,128]{1,0:T(8,128)S(1)}, u32[]{:S(2)}, u32[]{:S(2)}) collective-permute-start(f32[1544,128]{1,0:T(8,128)S(1)} %get-tuple-element.104), channel_id=1, source_target_pairs={{126,0},{0,2},{2,4},{4,6},{6,8},{8,10},{10,12},{12,14},{14,16},{16... | collective-permute-start | bytes 2371592 | tf_op jit(solution)/shard_map/ppermute | solution.py:623
  258.5 5.7 %collective-permute-start.22 = (f32[8,128]{1,0:T(8,128)S(1)}, f32[8,128]{1,0:T(8,128)S(1)}, u32[]{:S(2)}, u32[]{:S(2)}) collective-permute-start(f32[8,128]{1,0:T(8,128)S(1)} %add_add_fusion.2), channel_id=1, source_target_pairs={{0,8},{1,9},{2,10},{3,11},{4,12},{5,13},{6,14},{7,15},{8,0},{9,1},... | collective-permute-start | bytes 12296 | tf_op jit(solution)/shard_map/ppermute | solution.py:537
  258.6 13.2 %collective-permute-start.23 = (f32[8,128]{1,0:T(8,128)S(1)}, f32[8,128]{1,0:T(8,128)S(1)}, u32[]{:S(2)}, u32[]{:S(2)}) collective-permute-start(f32[8,128]{1,0:T(8,128)S(1)} %add_add_fusion.2), channel_id=1, source_target_pairs={{0,16},{1,17},{2,18},{3,19},{4,20},{5,21},{6,22},{7,23},{8,24},{9,... | collective-permute-start | bytes 12296 | tf_op jit(solution)/shard_map/ppermute | solution.py:537
  264.2 7.6 %collective-permute-start.24 = (f32[8,128]{1,0:T(8,128)S(1)}, f32[8,128]{1,0:T(8,128)S(1)}, u32[]{:S(2)}, u32[]{:S(2)}) collective-permute-start(f32[8,128]{1,0:T(8,128)S(1)} %add_add_fusion.2), channel_id=1, source_target_pairs={{0,24},{1,25},{2,26},{3,27},{4,28},{5,29},{6,30},{7,31},{8,16},{9,... | collective-permute-start | bytes 12296 | tf_op jit(solution)/shard_map/ppermute | solution.py:537
  271.8 4.8 %collective-permute-start.25 = (f32[8,128]{1,0:T(8,128)S(1)}, f32[8,128]{1,0:T(8,128)S(1)}, u32[]{:S(2)}, u32[]{:S(2)}) collective-permute-start(f32[8,128]{1,0:T(8,128)S(1)} %add_add_fusion.1), channel_id=1, source_target_pairs={{0,32},{1,33},{2,34},{3,35},{4,36},{5,37},{6,38},{7,39},{8,40},{9,... | collective-permute-start | bytes 12296 | tf_op jit(solution)/shard_map/ppermute | solution.py:537
  273.4 5.1 %collective-permute-start.26 = (f32[8,128]{1,0:T(8,128)S(1)}, f32[8,128]{1,0:T(8,128)S(1)}, u32[]{:S(2)}, u32[]{:S(2)}) collective-permute-start(f32[8,128]{1,0:T(8,128)S(1)} %add_add_fusion.1), channel_id=1, source_target_pairs={{0,64},{1,65},{2,66},{3,67},{4,68},{5,69},{6,70},{7,71},{8,72},{9,... | collective-permute-start | bytes 12296 | tf_op jit(solution)/shard_map/ppermute | solution.py:537
  275.1 4.8 %collective-permute-start.27 = (f32[8,128]{1,0:T(8,128)S(1)}, f32[8,128]{1,0:T(8,128)S(1)}, u32[]{:S(2)}, u32[]{:S(2)}) collective-permute-start(f32[8,128]{1,0:T(8,128)S(1)} %add_add_fusion.1), channel_id=1, source_target_pairs={{0,96},{1,97},{2,98},{3,99},{4,100},{5,101},{6,102},{7,103},{8,104... | collective-permute-start | bytes 12296 | tf_op jit(solution)/shard_map/ppermute | solution.py:537
